TPU v7x, 64 devices: a 2x2x8 block of a 4x4x8 slice. The times are simulated.
64 devices in a mesh: dp: 4 (over x, y), sp: 16 (over z, core).
Axes of the slice: x: 2, y: 2, z: 8, core: 2. Of those that a mesh axis runs over, the one named last changes fastest.
The devices are a block of a 4x4x8 slice.
Arguments:
- x_in: bfloat16 [4, 2048, 1024], P('dp', 'sp'), parts along dimension 0
- grad_y: bfloat16 [4, 2048, 1024], P('dp', 'sp'), parts along dimension 0
- positions: int32 [8192], P(('dp', 'sp')), parts along dimension 0
- w_q: bfloat16 [1024, 2048], replicated
- w_k: bfloat16 [1024, 1024], replicated
- w_v: bfloat16 [1024, 1024], replicated
- w_o: bfloat16 [2048, 1024], replicated
- w_gate: bfloat16 [1024, 3072], replicated
- w_up: bfloat16 [1024, 3072], replicated
- w_down: bfloat16 [3072, 1024], replicated
- norm_gain: float32 [1024], replicated
- q_norm: float32 [16, 128], replicated
- k_norm: float32 [8, 128], replicated
Outputs:
- output 1: bfloat16 [4, 2048, 1024], P('dp', 'sp'), parts along dimension 0
- output 2: bfloat16 [4, 2048, 1024], P('dp', 'sp'), parts along dimension 0
- output 3: bfloat16 [4096, 2048], P('dp'), parts along dimension 0
- output 4: bfloat16 [4096, 1024], P('dp'), parts along dimension 0
- output 5: bfloat16 [4096, 1024], P('dp'), parts along dimension 0
- output 6: bfloat16 [8192, 1024], P('dp'), parts along dimension 0
- output 7: bfloat16 [4096, 3072], P('dp'), parts along dimension 0
- output 8: bfloat16 [4096, 3072], P('dp'), parts along dimension 0
- output 9: bfloat16 [12288, 1024], P('dp'), parts along dimension 0
- output 10: float32 [4096], P('dp'), parts along dimension 0
- output 11: float32 [64, 128], P('dp'), parts along dimension 0
- output 12: float32 [32, 128], P('dp'), parts along dimension 0
There are 4 independent parts. A program takes and returns all parts, laid end to end along the dimension named above; an argument that names none is the same for every part.
All inputs are finite; a program needn't handle non-finite values.
Results may differ from a plain program's by a relative error of at most 0.02.
Values are sent between devices in bfloat16 or wider.
A program may use at most 768 MiB of HBM per device.

v0:
```python
import jax
import jax.numpy as jnp
from jax import lax
from jax.sharding import PartitionSpec as P

NORM_EPS = 1e-5
ROPE_THETA = 75.0e6


def input_norm(x_f32, norm_gain):
    row_mean = jnp.mean(x_f32, axis=-1, keepdims=True)
    centered = x_f32 - row_mean
    row_var = jnp.mean(centered * centered, axis=-1, keepdims=True)
    return (centered * lax.rsqrt(row_var + NORM_EPS) * norm_gain).astype(jnp.bfloat16)


def rope_tables(positions, head_dim):
    inv_freq = ROPE_THETA ** (-(jnp.arange(head_dim // 2, dtype=jnp.float32) * 2.0) / head_dim)
    angles = positions.astype(jnp.float32)[:, None] * inv_freq[None, :]
    return jnp.cos(angles), jnp.sin(angles)


def head_prepare(proj_in, norm_weight, cos_t, sin_t):
    proj_f32 = proj_in.astype(jnp.float32)
    row_mean = jnp.mean(proj_f32, axis=-1, keepdims=True)
    centered = proj_f32 - row_mean
    row_var = jnp.mean(centered * centered, axis=-1, keepdims=True)
    normed = centered * lax.rsqrt(row_var + NORM_EPS) * norm_weight
    pair_view = normed.reshape(normed.shape[:-1] + (normed.shape[-1] // 2, 2))
    even_part = pair_view[..., 0]
    odd_part = pair_view[..., 1]
    cos_rows = cos_t[:, None, :]
    sin_rows = sin_t[:, None, :]
    rotated = jnp.stack([even_part * cos_rows - odd_part * sin_rows, even_part * sin_rows + odd_part * cos_rows], axis=-1)
    return rotated.reshape(normed.shape).astype(jnp.bfloat16)


def swiglu(gate_pre, up_proj):
    return (jax.nn.silu(gate_pre) * up_proj).astype(jnp.bfloat16)


def attend(q_rot, k_rot, v_proj, q_start):
    score_scale = q_rot.shape[-1] ** -0.5
    scores = jnp.einsum('bqkgd,bskd->bkgqs', q_rot, k_rot, preferred_element_type=jnp.float32) * score_scale
    q_index = q_start + jnp.arange(q_rot.shape[1])
    k_index = jnp.arange(k_rot.shape[1])
    causal = q_index[:, None] >= k_index[None, :]
    attn_probs = jax.nn.softmax(jnp.where(causal, scores, -1e30), axis=-1).astype(jnp.bfloat16)
    attended = jnp.einsum('bkgqs,bskd->bqkgd', attn_probs, v_proj, preferred_element_type=jnp.float32)
    return attended.astype(jnp.bfloat16)


def times_transposed(lhs_mat, rhs_mat):
    return lax.dot_general(lhs_mat, rhs_mat, (((1,), (1,)), ((), ())), preferred_element_type=jnp.float32)


def grad_product(act_rows, grad_rows):
    return lax.dot_general(act_rows, grad_rows, (((0,), (0,)), ((), ())), preferred_element_type=jnp.float32)


def solution(mesh):
    group_devices = mesh.shape['sp']
    seq_spec = P('dp', 'sp', None)
    grad_spec = P('dp', None)

    def layer_step(x_in, grad_y, positions, w_q, w_k, w_v, w_o, w_gate, w_up, w_down, norm_gain, q_norm, k_norm):
        batch_rows, local_len, model_dim = x_in.shape
        num_heads, head_dim = q_norm.shape
        num_kv = k_norm.shape[0]
        kv_copies = max(group_devices // num_kv, 1)
        full_len = local_len * group_devices
        tokens = batch_rows * local_len
        x_f32 = x_in.astype(jnp.float32)
        normed, norm_back = jax.vjp(input_norm, x_f32, norm_gain)
        flat_norm = normed.reshape(tokens, model_dim)
        q_proj = jnp.dot(flat_norm, w_q, preferred_element_type=jnp.float32).astype(jnp.bfloat16)
        k_proj = jnp.dot(flat_norm, w_k, preferred_element_type=jnp.float32).astype(jnp.bfloat16)
        v_proj = jnp.dot(flat_norm, w_v, preferred_element_type=jnp.float32).astype(jnp.bfloat16)
        cos_t, sin_t = rope_tables(positions, head_dim)
        q_rot, q_back = jax.vjp(lambda proj_in, weight: head_prepare(proj_in, weight, cos_t, sin_t), q_proj.reshape(batch_rows, local_len, num_heads, head_dim), q_norm)
        k_rot, k_back = jax.vjp(lambda proj_in, weight: head_prepare(proj_in, weight, cos_t, sin_t), k_proj.reshape(batch_rows, local_len, num_kv, head_dim), k_norm)
        v_heads = v_proj.reshape(batch_rows, local_len, num_kv, head_dim)
        q_by_head = lax.all_to_all(q_rot, 'sp', 2, 1, tiled=True)
        k_by_head = lax.all_to_all(jnp.repeat(k_rot, kv_copies, axis=2), 'sp', 2, 1, tiled=True)
        v_by_head = lax.all_to_all(jnp.repeat(v_heads, kv_copies, axis=2), 'sp', 2, 1, tiled=True)
        local_q = q_by_head.shape[2]
        local_kv = k_by_head.shape[2]
        grouped_shape = (batch_rows, full_len, local_kv, local_q // local_kv, head_dim)
        attn_heads, attn_back = jax.vjp(lambda q_arg, k_arg, v_arg: attend(q_arg, k_arg, v_arg, 0), q_by_head.reshape(grouped_shape), k_by_head, v_by_head)
        attn_seq = lax.all_to_all(attn_heads.reshape(batch_rows, full_len, local_q, head_dim), 'sp', 1, 2, tiled=True)
        attn_flat = attn_seq.reshape(tokens, num_heads * head_dim)
        attn_out = jnp.dot(attn_flat, w_o, preferred_element_type=jnp.float32).astype(jnp.bfloat16)
        gate_pre = jnp.dot(flat_norm, w_gate, preferred_element_type=jnp.float32)
        up_proj = jnp.dot(flat_norm, w_up, preferred_element_type=jnp.float32)
        hidden, act_back = jax.vjp(swiglu, gate_pre, up_proj)
        mlp_out = jnp.dot(hidden, w_down, preferred_element_type=jnp.float32).astype(jnp.bfloat16)
        y_out = (x_f32 + attn_out.astype(jnp.float32).reshape(x_in.shape) + mlp_out.astype(jnp.float32).reshape(x_in.shape)).astype(jnp.bfloat16)

        grad_flat = grad_y.reshape(tokens, model_dim)
        d_hidden = times_transposed(grad_flat, w_down).astype(jnp.bfloat16)
        d_gate, d_up = act_back(d_hidden)
        d_gate = d_gate.astype(jnp.bfloat16)
        d_up = d_up.astype(jnp.bfloat16)
        d_attn = times_transposed(grad_flat, w_o).astype(jnp.bfloat16)
        d_attn_heads = lax.all_to_all(d_attn.reshape(batch_rows, local_len, num_heads, head_dim), 'sp', 2, 1, tiled=True)
        dq_heads, dk_heads, dv_heads = attn_back(d_attn_heads.reshape(grouped_shape))
        dq_rot = lax.all_to_all(dq_heads.reshape(batch_rows, full_len, local_q, head_dim), 'sp', 1, 2, tiled=True)
        dk_copies = lax.all_to_all(dk_heads, 'sp', 1, 2, tiled=True)
        dv_copies = lax.all_to_all(dv_heads, 'sp', 1, 2, tiled=True)
        copy_shape = (batch_rows, local_len, num_kv, kv_copies, head_dim)
        dk_rot = jnp.sum(dk_copies.reshape(copy_shape), axis=3, dtype=jnp.float32).astype(jnp.bfloat16)
        dv_seq = jnp.sum(dv_copies.reshape(copy_shape), axis=3, dtype=jnp.float32).astype(jnp.bfloat16)
        dq_proj, grad_q_norm = q_back(dq_rot)
        dk_proj, grad_k_norm = k_back(dk_rot)
        dq_flat = dq_proj.reshape(tokens, num_heads * head_dim)
        dk_flat = dk_proj.reshape(tokens, num_kv * head_dim)
        dv_flat = dv_seq.reshape(tokens, num_kv * head_dim)
        d_norm = (times_transposed(dq_flat, w_q) + times_transposed(dk_flat, w_k) + times_transposed(dv_flat, w_v)
                  + times_transposed(d_gate, w_gate) + times_transposed(d_up, w_up)).astype(jnp.bfloat16)
        dx_norm, grad_gain = norm_back(d_norm.reshape(x_in.shape))
        grad_x = (grad_y.astype(jnp.float32) + dx_norm).astype(jnp.bfloat16)
        partial_mats = (grad_product(flat_norm, dq_flat), grad_product(flat_norm, dk_flat), grad_product(flat_norm, dv_flat),
                        grad_product(attn_flat, grad_flat), grad_product(flat_norm, d_gate), grad_product(flat_norm, d_up),
                        grad_product(hidden, grad_flat))
        summed_mats = [lax.psum(part_grad, 'sp').astype(jnp.bfloat16) for part_grad in partial_mats]
        summed_small = [lax.psum(part_grad, 'sp') for part_grad in (grad_gain, grad_q_norm, grad_k_norm)]
        return tuple([y_out, grad_x] + summed_mats + summed_small)

    in_specs = (seq_spec, seq_spec, P(('dp', 'sp'))) + (P(),) * 10
    out_specs = (seq_spec, seq_spec) + (grad_spec,) * 7 + (P('dp'), grad_spec, grad_spec)
    return jax.shard_map(layer_step, mesh=mesh, in_specs=in_specs, out_specs=out_specs, check_vma=False)
```

profile of v0, /device:TPU:21, one launch (start us, length us, event | category | flops | bytes accessed | tf_op | source)
XLA Modules:
  0.0 1107.7 jit_solution(13293275234375893210)
XLA Ops:
  20.8 10.7 all-to-all-start.1
  63.7 6.3 fusion.69
  70.1 6.4 fusion.89
  80.9 7.0 fusion.91
  87.9 7.2 all-to-all-start.2
  106.7 6.1 fusion.111
  113.7 7.2 all-to-all-start
  126.8 8.3 fusion.9
  142.9 8.2 fusion.14
  151.1 7.7 all-to-all-done.4
  158.8 12.0 %fusion.8 = (f32[2048]{0:T(1024)S(1)}, bf16[2048,2048]{0,1:T(8,128)(2,1)}) fusion(f32[2048]{0:T(1024)S(1)} %multiply_divide_fusion, f32[2048]{0:T(1024)S(1)} %get-tuple-element.105, f32[2048,2048]{1,0:T(8,128)} %get-tuple-element.106, bf16[2048,128]{1,0:T(8,128)(2,1)} %bitcast.4, bf16[128,2048]{0,1:T(8,128)(2,1)S(1)} %bitcast.344), kind=kOutput, calls=%fused_computation.10 | convolution fusion | flops 1111488512 | bytes 26238976 | tf_op jit(solution)/shard_map/transpose(jvp(bkgqs,bskd->bqkgd))/dot_general | solution.py:49
  170.8 12.7 %fusion.24 = bf16[1,2048,1,128]{3,1,2,0:T(8,128)(2,1)S(1)} fusion(bf16[2048,128]{1,0:T(8,128)(2,1)S(1)} %bitcast.347, bf16[2048,2048]{0,1:T(8,128)(2,1)} %get-tuple-element.108, f32[2048]{0:T(1024)S(1)} %neg.41, f32[2048]{0:T(1024)S(1)} %fusion.14, f32[2048]{0:T(1024)S(1)} %get-tuple-element.105, f32[2048,2048]{1,0:T(8,128)} %get-tuple-element.106), kind=kOutput, calls=%fused_computation.33 | convolution fusion | flops 1115947008 | bytes 26238976 | tf_op jit(solution)/shard_map/transpose(jvp(bqkgd,bskd->bkgqs))/dot_general | solution.py:44
  183.6 11.8 %fusion.23 = bf16[1,2048,1,128]{3,1,2,0:T(8,128)(2,1)} fusion(bf16[2048,128]{1,0:T(8,128)(2,1)} %bitcast.11, bf16[2048,2048]{0,1:T(8,128)(2,1)} %get-tuple-element.108, f32[2048]{0:T(1024)S(1)} %neg.41, f32[2048]{0:T(1024)S(1)} %fusion.14, f32[2048]{0:T(1024)S(1)} %get-tuple-element.105, f32[2048,2048]{1,0:T(8,128)S(1)} %bitcast.293), kind=kOutput, calls=%fused_computation.32 | convolution fusion | flops 1115947008 | bytes 26238976 | tf_op jit(solution)/shard_map/transpose(jvp(bqkgd,bskd->bkgqs))/dot_general | solution.py:44
  195.4 8.3 copy.308
  204.3 12.3 %reduce.28 = bf16[2048,128]{1,0:T(8,128)(2,1)} reduce(bf16[2048,1,1,128]{3,2,1,0:T(2,128)(2,1)S(1)} %bitcast.314, bf16[]{:T(256)} %broadcast.503), dimensions={1,2}, to_apply=%bitcast.288.reduce_sub_computation | reduce | bytes 1048578
  223.3 9.9 fusion.25
  235.5 12.3 %reduce.27 = bf16[2048,128]{1,0:T(8,128)(2,1)} reduce(bf16[2048,1,1,128]{3,2,1,0:T(2,128)(2,1)S(1)} %bitcast.318, bf16[]{:T(256)} %broadcast.503), dimensions={1,2}, to_apply=%bitcast.243.reduce_sub_computation | reduce | bytes 1048578
  249.8 7.6 all-to-all-start.7
  257.4 8.7 fusion.28
  268.1 13.4 %reduce.26 = bf16[2048,128]{1,0:T(8,128)(2,1)} reduce(bf16[2048,1,1,128]{3,2,1,0:T(2,128)(2,1)} %bitcast.319, bf16[]{:T(256)} %broadcast.503), dimensions={1,2}, to_apply=%bitcast.241.reduce_sub_computation | reduce | bytes 1048578
  286.1 13.6 %reduce.29 = bf16[2048,128]{1,0:T(8,128)(2,1)} reduce(bf16[2048,1,1,128]{3,2,1,0:T(2,128)(2,1)} %bitcast.316, bf16[]{:T(256)} %broadcast.503), dimensions={1,2}, to_apply=%bitcast.289.reduce_sub_computation | reduce | bytes 1048578
  315.1 7.2 all-to-all-start.5
  338.6 7.8 all-to-all-start.3
  418.4 687.7 %all-reduce.6 = (bf16[1024,2048]{1,0:T(8,128)(2,1)}, bf16[1024,1024]{1,0:T(8,128)(2,1)}, bf16[1024,1024]{1,0:T(8,128)(2,1)}, bf16[2048,1024]{1,0:T(8,128)(2,1)},...) all-reduce(f32[1024,2048]{1,0:T(8,128)} %fusion.97, ...), channel_id=1, replica_groups=mesh['dp'=4,'sp'=16] {'sp'}, use_global_device_ids=true, to_apply=%region_17.18 | all-reduce | flops 15732736 | bytes 94404608 | tf_op jit(solution)/shard_map/psum | solution.py:125
  (286 shorter events, 205.2 us)
Async XLA Ops:
  0.6 94.5 %copy-start = (bf16[1024,1024]{1,0:T(8,128)(2,1)S(1)}, bf16[1024,1024]{1,0:T(8,128)(2,1)}, u32[]{:S(2)}) copy-start(bf16[1024,1024]{1,0:T(8,128)(2,1)} %param.18) | copy-start | bytes 6291460
  2.6 92.5 %copy-start.50 = (f32[128]{0:T(128)}, f32[128]{0:T(128)S(1)}, u32[]{:S(2)}) copy-start(f32[128]{0:T(128)S(1)} %broadcast_multiply_fusion.2) | copy-start | bytes 1540
  3.8 36.3 %copy-start.57 = (f32[128]{0:T(128)}, f32[128]{0:T(128)S(1)}, u32[]{:S(2)}) copy-start(f32[128]{0:T(128)S(1)} %fusion.77) | copy-start | bytes 1540
  13.5 43.1 %copy-start.35 = (f32[128,64]{0,1:T(8,128)}, f32[128,64]{0,1:T(8,128)S(1)}, u32[]{:S(2)}) copy-start(f32[128,64]{0,1:T(8,128)S(1)} %get-tuple-element.103) | copy-start | bytes 98308
  13.5 43.1 %copy-start.37 = (f32[128,64]{0,1:T(8,128)}, f32[128,64]{0,1:T(8,128)S(1)}, u32[]{:S(2)}) copy-start(f32[128,64]{0,1:T(8,128)S(1)} %get-tuple-element.104) | copy-start | bytes 98308
  20.8 67.1 %all-to-all-start.1 = ((bf16[1,128,16,128]{3,1,0,2:T(8,128)(2,1)}), bf16[1,128,16,128]{3,1,0,2:T(8,128)(2,1)}, u32[]{:S(2)}, u32[]{:S(2)}) async-start(bf16[1,128,16,128]{3,1,0,2:T(8,128)(2,1)} %bitcast.331), calls=%async_computation.1 | async-start | bytes 1048576 | tf_op jit(solution)/shard_map/all_to_all | solution.py:84
  42.3 54.8 %copy-start.44 = (f32[128,16]{0,1:T(8,128)}, f32[128,16]{0,1:T(8,128)S(1)}, u32[]{:S(2)}) copy-start(f32[128,16]{0,1:T(8,128)S(1)} %broadcast_multiply_fusion) | copy-start | bytes 24580
  87.9 24.9 %all-to-all-start.2 = ((bf16[1,128,16,128]{1,3,0,2:T(8,128)(2,1)}), bf16[1,128,16,128]{1,3,0,2:T(8,128)(2,1)}, u32[]{:S(2)}, u32[]{:S(2)}) async-start(bf16[1,128,16,128]{1,3,0,2:T(8,128)(2,1)} %bitcast.327), calls=%async_computation.2 | async-start | bytes 1048576 | tf_op jit(solution)/shard_map/all_to_all | solution.py:83
  113.7 23.5 %all-to-all-start = ((bf16[1,128,16,128]{3,1,0,2:T(8,128)(2,1)}), bf16[1,128,16,128]{3,1,0,2:T(8,128)(2,1)}, u32[]{:S(2)}, u32[]{:S(2)}) async-start(bf16[1,128,16,128]{3,1,0,2:T(8,128)(2,1)} %bitcast.332), calls=%async_computation | async-start | bytes 1048576 | tf_op jit(solution)/shard_map/all_to_all | solution.py:85
  137.2 21.6 %all-to-all-start.4 = ((bf16[1,128,16,128]{3,1,0,2:T(8,128)(2,1)}), bf16[1,128,16,128]{3,1,0,2:T(8,128)(2,1)S(1)}, u32[]{:S(2)}, u32[]{:S(2)}) async-start(bf16[1,128,16,128]{3,1,0,2:T(8,128)(2,1)} %copy.231), calls=%async_computation.4 | async-start | bytes 1048576 | tf_op jit(solution)/shard_map/all_to_all | solution.py:105
  218.5 31.3 %all-to-all-start.6 = ((bf16[16,2,8192]{2,1,0:T(2,128)(2,1)}), bf16[16,2,8192]{2,1,0:T(2,128)(2,1)}, u32[]{:S(2)}, u32[]{:S(2)}) async-start(bf16[16,2,8192]{2,1,0:T(2,128)(2,1)} %reshape.808), calls=%async_computation.6 | async-start | bytes 1048576 | tf_op jit(solution)/shard_map/all_to_all | solution.py:108
  249.8 65.3 %all-to-all-start.7 = ((bf16[16,2,8192]{2,1,0:T(2,128)(2,1)}), bf16[16,2,8192]{2,1,0:T(2,128)(2,1)}, u32[]{:S(2)}, u32[]{:S(2)}) async-start(bf16[16,2,8192]{2,1,0:T(2,128)(2,1)} %reshape.812), calls=%async_computation.7 | async-start | bytes 1048576 | tf_op jit(solution)/shard_map/all_to_all | solution.py:109
  266.1 45.9 %copy-start.36 = (f32[128,64]{0,1:T(8,128)S(1)}, f32[128,64]{0,1:T(8,128)}, u32[]{:S(2)}) copy-start(f32[128,64]{0,1:T(8,128)} %copy-done.35) | copy-start | bytes 98308
  266.1 45.9 %copy-start.38 = (f32[128,64]{0,1:T(8,128)S(1)}, f32[128,64]{0,1:T(8,128)}, u32[]{:S(2)}) copy-start(f32[128,64]{0,1:T(8,128)} %copy-done.37) | copy-start | bytes 98308
  266.1 48.1 %copy-start.18 = (f32[1,128,8,128]{1,2,3,0:T(8,128)S(1)}, f32[1,128,8,128]{1,2,3,0:T(8,128)}, u32[]{:S(2)}) copy-start(f32[1,128,8,128]{1,2,3,0:T(8,128)} %copy.216) | copy-start | bytes 1572868
  266.1 48.1 %copy-start.42 = (f32[8,128]{0,1:T(8,128)S(1)}, f32[8,128]{0,1:T(8,128)}, u32[]{:S(2)}) copy-start(f32[8,128]{0,1:T(8,128)} %copy-done.41) | copy-start | bytes 12292
  266.1 48.1 %copy-start.54 = (f32[128,8]{0,1:T(8,128)S(1)}, f32[128,8]{0,1:T(8,128)}, u32[]{:S(2)}) copy-start(f32[128,8]{0,1:T(8,128)} %copy-done.52) | copy-start | bytes 12292
  268.1 64.0 %copy-start.17 = (f32[128,1024]{0,1:T(8,128)S(1)}, f32[128,1024]{0,1:T(8,128)}, u32[]{:S(2)}) copy-start(f32[128,1024]{0,1:T(8,128)} %copy-done.16) | copy-start | bytes 1572868
  281.5 54.0 %copy-start.2 = (bf16[1,128,1024]{2,1,0:T(8,128)(2,1)S(1)}, bf16[1,128,1024]{2,1,0:T(8,128)(2,1)}, u32[]{:S(2)}) copy-start(bf16[1,128,1024]{2,1,0:T(8,128)(2,1)} %param.13) | copy-start | bytes 786436
  281.5 54.0 %copy-start.29 = (f32[1024]{0:T(1024)S(1)}, f32[1024]{0:T(1024)}, u32[]{:S(2)}) copy-start(f32[1024]{0:T(1024)} %param.23) | copy-start | bytes 12292
  281.5 54.0 %copy-start.51 = (f32[128]{0:T(128)S(1)}, f32[128]{0:T(128)}, u32[]{:S(2)}) copy-start(f32[128]{0:T(128)} %copy-done.50) | copy-start | bytes 1540
  281.5 54.0 %copy-start.60 = (f32[128]{0:T(128)S(1)}, f32[128]{0:T(128)}, u32[]{:S(2)}) copy-start(f32[128]{0:T(128)} %copy-done.57) | copy-start | bytes 1540
  315.1 23.5 %all-to-all-start.5 = ((bf16[16,2,8192]{2,1,0:T(2,128)(2,1)}), bf16[16,2,8192]{2,1,0:T(2,128)(2,1)}, u32[]{:S(2)}, u32[]{:S(2)}) async-start(bf16[16,2,8192]{2,1,0:T(2,128)(2,1)} %reshape.814), calls=%async_computation.5 | async-start | bytes 1048576 | tf_op jit(solution)/shard_map/all_to_all | solution.py:107
  338.6 43.8 %all-to-all-start.3 = ((bf16[16,2,8192]{2,1,0:T(2,128)(2,1)}), bf16[16,2,8192]{2,1,0:T(2,128)(2,1)}, u32[]{:S(2)}, u32[]{:S(2)}) async-start(bf16[16,2,8192]{2,1,0:T(2,128)(2,1)} %reshape.810), calls=%async_computation.3 | async-start | bytes 1048576 | tf_op jit(solution)/shard_map/all_to_all | solution.py:90
  (59 other events, 783.3 us)
where the time goes:
time: 1120 us; the launch traced here: 1110 us
  blocking collectives  688 us (61%)
  matrix products  144 us (13%)
  other arithmetic  104 us (9%)
  local copies, waits for them, and re-layouts  102 us (9%)
  starting transfers between devices  58.2 us (5%)
    psum x1, blocking collectives, layer_step(): lax.psum(part_grad, 'sp').astype(jnp.bfloat16)  688 us
    unnamed x6, other arithmetic  51.6 us
    dot_general x7, matrix products, grad_product(): lax.dot_general(act_rows, grad_rows, (((0,), (0,)), ((), ())), preferred_...  36.8 us
    unnamed x169, local copies, waits for them, and re-layouts  33.5 us
    dot_general x3, matrix products, attend(): jnp.einsum('bqkgd,bskd->bkgqs', q_rot, k_rot, preferred_element_type=jnp....  32.9 us
    dot_general x3, matrix products, attend(): jnp.einsum('bkgqs,bskd->bqkgd', attn_probs, v_proj, preferred_element_typ...  30.5 us
    dot_general x7, matrix products, times_transposed(): lax.dot_general(lhs_mat, rhs_mat, (((1,), (1,)), ((), ())), preferred_ele...  26 us
  transfers between devices with their start and end apart: 8, of which 3 were waited for; matrix products, arithmetic and copies ran while one was open for 21% of the time, Pallas kernels for 0%

commit v1 on v0

v1 whole, which is shorter than its diff:
```python
import functools

import jax
import jax.numpy as jnp
from jax import lax
from jax.experimental import pallas as pl
from jax.experimental.pallas import tpu as pltpu
from jax.sharding import PartitionSpec as P

NORM_EPS = 1e-5
ROPE_THETA = 75.0e6
VMEM_LIMIT = 60 * 1024 * 1024
F32 = jnp.float32
BF16 = jnp.bfloat16


def input_norm(x_f32, norm_gain):
    row_mean = jnp.mean(x_f32, axis=-1, keepdims=True)
    centered = x_f32 - row_mean
    row_var = jnp.mean(centered * centered, axis=-1, keepdims=True)
    return (centered * lax.rsqrt(row_var + NORM_EPS) * norm_gain).astype(BF16)


def swiglu(gate_pre, up_proj):
    return (jax.nn.silu(gate_pre) * up_proj).astype(BF16)


def times_transposed(lhs_mat, rhs_mat):
    return lax.dot_general(lhs_mat, rhs_mat, (((1,), (1,)), ((), ())), preferred_element_type=F32)


def transposed_times(lhs_mat, rhs_mat):
    return lax.dot_general(lhs_mat, rhs_mat, (((0,), (0,)), ((), ())), preferred_element_type=F32)


def rope_lanes(positions, head_dim):
    pair_index = jnp.arange(head_dim, dtype=jnp.int32) // 2
    inv_freq = ROPE_THETA ** (-(pair_index.astype(F32) * 2.0) / head_dim)
    angles = positions.astype(F32)[:, None] * inv_freq[None, :]
    sign = jnp.where(jnp.arange(head_dim) % 2 == 0, -1.0, 1.0).astype(F32)
    return jnp.cos(angles), jnp.sin(angles) * sign[None, :]


def swap_pairs(rows):
    lane = lax.broadcasted_iota(jnp.int32, rows.shape, 1)
    width = rows.shape[1]
    return jnp.where(lane % 2 == 0, pltpu.roll(rows, width - 1, 1), pltpu.roll(rows, 1, 1))


def head_stats(proj_f32):
    row_mean = jnp.mean(proj_f32, axis=-1, keepdims=True)
    centered = proj_f32 - row_mean
    inv_std = lax.rsqrt(jnp.mean(centered * centered, axis=-1, keepdims=True) + NORM_EPS)
    return centered * inv_std, inv_std


def head_forward(proj_f32, weight, cos_t, sin_t):
    unit, _ = head_stats(proj_f32)
    normed = unit * weight
    return (normed * cos_t + swap_pairs(normed) * sin_t).astype(BF16)


def head_backward(d_rot, proj_f32, weight, cos_t, sin_t):
    unit, inv_std = head_stats(proj_f32)
    d_normed = d_rot * cos_t + swap_pairs(d_rot * sin_t)
    d_weight = jnp.sum(d_normed * unit, axis=0, keepdims=True)
    d_unit = d_normed * weight
    mean_d = jnp.mean(d_unit, axis=-1, keepdims=True)
    mean_du = jnp.mean(d_unit * unit, axis=-1, keepdims=True)
    return inv_std * (d_unit - mean_d - unit * mean_du), d_weight


def attention_kernel(block, idx_ref, n_ref, dy_ref, wq_ref, wk_ref, wv_ref, wo_ref, qn_ref, kn_ref, cos_ref, sin_ref,
                     o_ref, dq_ref, send_ref, keep_ref, kproj_ref, dwq_ref, dwo_ref, gq_ref,
                     q_s, k_s, v_s, do_s, qp_s, e_s, dk_s, dv_s, gq_s):
    seq_len, head_dim = o_ref.shape
    steps = seq_len // block
    scale = head_dim ** -0.5

    def project(i, carry):
        rows = pl.ds(pl.multiple_of(i * block, block), block)
        n_rows = n_ref[rows, :]
        q_proj = jnp.dot(n_rows, wq_ref[...], preferred_element_type=F32).astype(BF16)
        k_proj = jnp.dot(n_rows, wk_ref[...], preferred_element_type=F32).astype(BF16)
        qp_s[rows, :] = q_proj
        kproj_ref[rows, :] = k_proj
        v_s[rows, :] = jnp.dot(n_rows, wv_ref[...], preferred_element_type=F32).astype(BF16)
        do_s[rows, :] = times_transposed(dy_ref[rows, :], wo_ref[...]).astype(BF16)
        cos_t, sin_t = cos_ref[rows, :], sin_ref[rows, :]
        q_s[rows, :] = head_forward(q_proj.astype(F32), qn_ref[0], cos_t, sin_t)
        k_s[rows, :] = head_forward(k_proj.astype(F32), kn_ref[0], cos_t, sin_t)
        dk_s[rows, :] = jnp.zeros((block, head_dim), F32)
        dv_s[rows, :] = jnp.zeros((block, head_dim), F32)
        return carry

    lax.fori_loop(0, steps, project, 0)
    gq_s[...] = jnp.zeros_like(gq_s)
    causal = lax.broadcasted_iota(jnp.int32, (block, block), 0) >= lax.broadcasted_iota(jnp.int32, (block, block), 1)

    def lanes_max(tile):
        parts = [tile[:, c:c + 128] for c in range(0, block, 128)]
        return functools.reduce(jnp.maximum, parts)

    def lanes_sum(tile):
        parts = [tile[:, c:c + 128] for c in range(0, block, 128)]
        return functools.reduce(jnp.add, parts)

    def query_block(i, carry):
        rows = pl.ds(pl.multiple_of(i * block, block), block)
        q_rows, do_rows = q_s[rows, :], do_s[rows, :]

        def keys_of(j):
            return pl.ds(pl.multiple_of(j * block, block), block)

        def score(j, top):
            tile = times_transposed(q_rows, k_s[keys_of(j), :])
            e_s[:, keys_of(j)] = tile
            return jnp.maximum(top, lanes_max(tile))

        top = lax.fori_loop(0, i, score, jnp.full((block, 128), -1e30, F32))
        diag = jnp.where(causal, times_transposed(q_rows, k_s[rows, :]), -1e30)
        e_s[:, rows] = diag
        top = jnp.max(jnp.maximum(top, lanes_max(diag)), axis=-1, keepdims=True)

        def exponent(j, total):
            tile = jnp.exp((e_s[:, keys_of(j)] - top) * scale)
            e_s[:, keys_of(j)] = tile
            return total + lanes_sum(tile)

        total = lax.fori_loop(0, i + 1, exponent, jnp.zeros((block, 128), F32))
        inv_total = 1.0 / jnp.sum(total, axis=-1, keepdims=True)

        def attend(j, acc):
            probs = e_s[:, keys_of(j)] * inv_total
            e_s[:, keys_of(j)] = probs
            probs = probs.astype(BF16)
            dv_s[keys_of(j), :] += transposed_times(probs, do_rows)
            return acc + jnp.dot(probs, v_s[keys_of(j), :], preferred_element_type=F32)

        out = lax.fori_loop(0, i + 1, attend, jnp.zeros((block, head_dim), F32))
        o_ref[rows, :] = out.astype(BF16)
        delta = jnp.sum(out * do_rows.astype(F32), axis=-1, keepdims=True)

        def back(j, acc):
            d_probs = times_transposed(do_rows, v_s[keys_of(j), :]).astype(BF16).astype(F32)
            d_score = (e_s[:, keys_of(j)] * (d_probs - delta) * scale).astype(BF16)
            dk_s[keys_of(j), :] += transposed_times(d_score, q_rows)
            return acc + jnp.dot(d_score, k_s[keys_of(j), :], preferred_element_type=F32)

        dq = lax.fori_loop(0, i + 1, back, jnp.zeros((block, head_dim), F32)).astype(BF16).astype(F32)
        dq_proj, d_weight = head_backward(dq, qp_s[rows, :].astype(F32), qn_ref[0], cos_ref[rows, :], sin_ref[rows, :])
        dq_ref[rows, :] = dq_proj.astype(BF16)
        gq_s[...] += d_weight
        return carry

    lax.fori_loop(0, steps, query_block, 0)
    gq_ref[...] = gq_s[...]
    first = idx_ref[2] == 0
    dk_all, dv_all = dk_s[...].astype(BF16), dv_s[...].astype(BF16)

    @pl.when(first)
    def _():
        keep_ref[...] = dk_all
        send_ref[...] = dv_all

    @pl.when(jnp.logical_not(first))
    def _():
        keep_ref[...] = dv_all
        send_ref[...] = dk_all

    dwq_ref[...] = transposed_times(n_ref[...], dq_ref[...]).astype(BF16)
    dwo_ref[...] = transposed_times(o_ref[...], dy_ref[...]).astype(BF16)


def key_value_kernel(idx_ref, keep_ref, got_ref, kproj_ref, n_ref, kn_ref, cos_ref, sin_ref, dkv_ref, dwkv_ref, gk_ref):
    total = (keep_ref[...].astype(F32) + got_ref[...].astype(F32)).astype(BF16)
    first = idx_ref[2] == 0

    @pl.when(first)
    def _():
        dk_proj, d_weight = head_backward(total.astype(F32), kproj_ref[...].astype(F32), kn_ref[0], cos_ref[...], sin_ref[...])
        dkv_ref[...] = dk_proj.astype(BF16)
        gk_ref[...] = d_weight

    @pl.when(jnp.logical_not(first))
    def _():
        dkv_ref[...] = total
        gk_ref[...] = jnp.zeros_like(gk_ref)

    dwkv_ref[...] = transposed_times(n_ref[...], dkv_ref[...]).astype(BF16)


def mlp_kernel(chunk, idx_ref, n_ref, dy_ref, wg_ref, wu_ref, wd_ref,
               fg_ref, fu_ref, fd_ref, hg_ref, hu_ref, hd_ref, nt_s, hid_s, dg_s, du_s):
    seq_len = n_ref.shape[0]

    @pl.when(pl.program_id(0) == 0)
    def _():
        def turn(i, carry):
            rows = pl.ds(pl.multiple_of(i * chunk, chunk), chunk)
            nt_s[:, rows] = n_ref[rows, :].T
            return carry
        lax.fori_loop(0, seq_len // chunk, turn, 0)

    def forward(i, carry):
        rows = pl.ds(pl.multiple_of(i * chunk, chunk), chunk)
        n_rows, dy_rows = n_ref[rows, :], dy_ref[rows, :]
        gate = jnp.dot(n_rows, wg_ref[...], preferred_element_type=F32)
        up = jnp.dot(n_rows, wu_ref[...], preferred_element_type=F32)
        d_hidden = times_transposed(dy_rows, wd_ref[...]).astype(BF16).astype(F32)
        sig = jax.nn.sigmoid(gate)
        silu = gate * sig
        hid_s[rows, :] = (silu * up).astype(BF16)
        du_s[rows, :] = (d_hidden * silu).astype(BF16)
        dg_s[rows, :] = (d_hidden * up * (sig * (1.0 + gate * (1.0 - sig)))).astype(BF16)
        return carry

    lax.fori_loop(0, seq_len // chunk, forward, 0)

    rows_out = nt_s.shape[0]
    piece = rows_out // 4

    def weights(i, carry):
        rows = pl.ds(pl.multiple_of(i * piece, piece), piece)
        nt_rows = nt_s[rows, :]
        d_gate = jnp.dot(nt_rows, dg_s[...], preferred_element_type=F32).astype(BF16)
        d_up = jnp.dot(nt_rows, du_s[...], preferred_element_type=F32).astype(BF16)
        fg_ref[rows, :] = d_gate
        hg_ref[rows, :] = d_gate
        fu_ref[rows, :] = d_up
        hu_ref[rows, :] = d_up
        return carry

    lax.fori_loop(0, 4, weights, 0)
    d_down = transposed_times(hid_s[...], dy_ref[...]).astype(BF16)
    fd_ref[...] = d_down
    hd_ref[...] = d_down


def fill_kernel(idx_ref, hg_ref, hu_ref, hd_ref, ag_ref, au_ref, ad_ref, fg_ref, fu_ref, fd_ref):
    fg_ref[...] = hg_ref[...]
    fu_ref[...] = hu_ref[...]
    fd_ref[...] = hd_ref[...]


def whole(shape):
    return pl.BlockSpec(shape, lambda *_: (0,) * len(shape))


def solution(mesh):
    group_devices = mesh.shape['sp']
    seq_spec = P('dp', 'sp', None)
    grad_spec = P('dp', None)
    pair_swap = [(i, i ^ 1) for i in range(group_devices)]

    def layer_step(x_in, grad_y, positions, w_q, w_k, w_v, w_o, w_gate, w_up, w_down, norm_gain, q_norm, k_norm):
        batch_rows, local_len, model_dim = x_in.shape
        num_heads, head_dim = q_norm.shape
        num_kv = k_norm.shape[0]
        share = num_heads // num_kv
        ffn_dim = w_gate.shape[1]
        seq_len = local_len * group_devices
        me = lax.axis_index('sp')
        core = me % 2
        idx = jnp.stack([me, me // share, core]).astype(jnp.int32)

        all_pos = lax.all_gather(positions, 'sp', axis=0, tiled=True)
        x_f32 = x_in.reshape(local_len, model_dim).astype(F32)
        flat_norm, norm_back = jax.vjp(input_norm, x_f32, norm_gain)
        grad_flat = grad_y.reshape(local_len, model_dim)
        n_all = lax.all_gather(flat_norm, 'sp', axis=0, tiled=True)
        dy_all = lax.all_gather(grad_flat, 'sp', axis=0, tiled=True)
        cos_t, sin_t = rope_lanes(all_pos, head_dim)

        gate_pre = jnp.dot(flat_norm, w_gate, preferred_element_type=F32)
        up_proj = jnp.dot(flat_norm, w_up, preferred_element_type=F32)
        hidden, act_back = jax.vjp(swiglu, gate_pre, up_proj)
        mlp_out = jnp.dot(hidden, w_down, preferred_element_type=F32).astype(BF16)
        d_hidden = times_transposed(grad_flat, w_down).astype(BF16)
        d_gate, d_up = act_back(d_hidden)
        d_norm_mlp = times_transposed(d_gate.astype(BF16), w_gate) + times_transposed(d_up.astype(BF16), w_up)

        vec = jax.ShapeDtypeStruct((1, head_dim), F32)
        rows_bf = jax.ShapeDtypeStruct((seq_len, head_dim), BF16)
        block = 512
        qn3 = q_norm.reshape(num_heads, 1, head_dim)
        kn3 = k_norm.reshape(num_kv, 1, head_dim)
        o_h, dq_h, send, keep, k_proj, dwq_h, dwo_h, gq = pl.pallas_call(
            functools.partial(attention_kernel, block),
            out_shape=[rows_bf, rows_bf, rows_bf, rows_bf, rows_bf,
                       jax.ShapeDtypeStruct((model_dim, head_dim), BF16), jax.ShapeDtypeStruct((head_dim, model_dim), BF16), vec],
            grid_spec=pltpu.PrefetchScalarGridSpec(
                num_scalar_prefetch=1, grid=(1,),
                in_specs=[whole((seq_len, model_dim)), whole((seq_len, model_dim)),
                          pl.BlockSpec((model_dim, head_dim), lambda g, s: (0, s[0])),
                          pl.BlockSpec((model_dim, head_dim), lambda g, s: (0, s[1])),
                          pl.BlockSpec((model_dim, head_dim), lambda g, s: (0, s[1])),
                          pl.BlockSpec((head_dim, model_dim), lambda g, s: (s[0], 0)),
                          pl.BlockSpec((1, 1, head_dim), lambda g, s: (s[0], 0, 0)),
                          pl.BlockSpec((1, 1, head_dim), lambda g, s: (s[1], 0, 0)),
                          whole((seq_len, head_dim)), whole((seq_len, head_dim))],
                out_specs=[whole((seq_len, head_dim))] * 5 + [whole((model_dim, head_dim)), whole((head_dim, model_dim)), whole((1, head_dim))],
                scratch_shapes=[pltpu.VMEM((seq_len, head_dim), BF16)] * 5
                + [pltpu.VMEM((block, seq_len), F32), pltpu.VMEM((seq_len, head_dim), F32), pltpu.VMEM((seq_len, head_dim), F32),
                   pltpu.VMEM((1, head_dim), F32)]),
            compiler_params=pltpu.CompilerParams(vmem_limit_bytes=VMEM_LIMIT),
            cost_estimate=pl.CostEstimate(flops=20_000_000_000, bytes_accessed=20_000_000, transcendentals=0),
            name="attention",
        )(idx, n_all, dy_all, w_q, w_k, w_v, w_o, qn3, kn3, cos_t, sin_t)

        got = lax.ppermute(send, 'sp', pair_swap)
        dkv_h, dwkv_h, gk = pl.pallas_call(
            key_value_kernel,
            out_shape=[rows_bf, jax.ShapeDtypeStruct((model_dim, head_dim), BF16), vec],
            grid_spec=pltpu.PrefetchScalarGridSpec(
                num_scalar_prefetch=1, grid=(1,),
                in_specs=[whole((seq_len, head_dim))] * 3 + [whole((seq_len, model_dim)),
                          pl.BlockSpec((1, 1, head_dim), lambda g, s: (s[1], 0, 0)),
                          whole((seq_len, head_dim)), whole((seq_len, head_dim))],
                out_specs=[whole((seq_len, head_dim)), whole((model_dim, head_dim)), whole((1, head_dim))]),
            compiler_params=pltpu.CompilerParams(vmem_limit_bytes=VMEM_LIMIT),
            cost_estimate=pl.CostEstimate(flops=5_000_000_000, bytes_accessed=8_000_000, transcendentals=0),
            name="key_value",
        )(idx, keep, got, k_proj, n_all, kn3, cos_t, sin_t)

        dwo_all = lax.all_gather(dwo_h, 'sp', axis=0, tiled=True)
        dwq_all = lax.all_gather(dwq_h, 'sp', axis=0)
        dwkv_all = lax.all_gather(dwkv_h, 'sp', axis=0)

        tile = 256
        half = ffn_dim // 2
        tiles = half // tile
        full_in = jax.ShapeDtypeStruct((model_dim, ffn_dim), BF16)
        full_out = jax.ShapeDtypeStruct((ffn_dim, model_dim), BF16)
        half_in = jax.ShapeDtypeStruct((model_dim, half), BF16)
        half_out = jax.ShapeDtypeStruct((half, model_dim), BF16)
        col_here = pl.BlockSpec((model_dim, tile), lambda i, s: (0, s[2] * tiles + i))
        row_here = pl.BlockSpec((tile, model_dim), lambda i, s: (s[2] * tiles + i, 0))
        col_half = pl.BlockSpec((model_dim, tile), lambda i, s: (0, i))
        row_half = pl.BlockSpec((tile, model_dim), lambda i, s: (i, 0))
        part_g, part_u, part_d, half_g, half_u, half_d = pl.pallas_call(
            functools.partial(mlp_kernel, 256),
            out_shape=[full_in, full_in, full_out, half_in, half_in, half_out],
            grid_spec=pltpu.PrefetchScalarGridSpec(
                num_scalar_prefetch=1, grid=(tiles,),
                in_specs=[whole((seq_len, model_dim)), whole((seq_len, model_dim)), col_here, col_here, row_here],
                out_specs=[col_here, col_here, row_here, col_half, col_half, row_half],
                scratch_shapes=[pltpu.VMEM((model_dim, seq_len), BF16)] + [pltpu.VMEM((seq_len, tile), BF16)] * 3),
            compiler_params=pltpu.CompilerParams(vmem_limit_bytes=VMEM_LIMIT),
            cost_estimate=pl.CostEstimate(flops=12 * seq_len * model_dim * half, bytes_accessed=40_000_000, transcendentals=0),
            name="mlp",
        )(idx, n_all, dy_all, w_gate, w_up, w_down)
        got_g = lax.ppermute(half_g, 'sp', pair_swap)
        got_u = lax.ppermute(half_u, 'sp', pair_swap)
        got_d = lax.ppermute(half_d, 'sp', pair_swap)
        col_there = pl.BlockSpec((model_dim, tile), lambda i, s: (0, (1 - s[2]) * tiles + i))
        row_there = pl.BlockSpec((tile, model_dim), lambda i, s: ((1 - s[2]) * tiles + i, 0))
        hbm = pl.BlockSpec(memory_space=pl.ANY)
        dw_gate, dw_up, dw_down = pl.pallas_call(
            fill_kernel,
            out_shape=[full_in, full_in, full_out],
            grid_spec=pltpu.PrefetchScalarGridSpec(
                num_scalar_prefetch=1, grid=(tiles,),
                in_specs=[col_half, col_half, row_half, hbm, hbm, hbm],
                out_specs=[col_there, col_there, row_there]),
            input_output_aliases={4: 0, 5: 1, 6: 2},
            cost_estimate=pl.CostEstimate(flops=1_000_000_000, bytes_accessed=20_000_000, transcendentals=0),
            name="fill",
        )(idx, got_g, got_u, got_d, part_g, part_u, part_d)

        attn_flat = lax.all_to_all(o_h, 'sp', 0, 1, tiled=True)
        attn_out = jnp.dot(attn_flat, w_o, preferred_element_type=F32).astype(BF16)
        y_out = (x_f32 + attn_out.astype(F32) + mlp_out.astype(F32)).astype(BF16)

        d_rows = lax.all_to_all(jnp.concatenate([dq_h, dkv_h], axis=1), 'sp', 0, 1, tiled=True)
        d_rows = d_rows.reshape(local_len, num_kv, share, 2, head_dim)
        dq_flat = d_rows[:, :, :, 0].reshape(local_len, num_heads * head_dim)
        dk_flat = d_rows[:, :, 0, 1].reshape(local_len, num_kv * head_dim)
        dv_flat = d_rows[:, :, 1, 1].reshape(local_len, num_kv * head_dim)
        d_norm = (times_transposed(dq_flat, w_q) + times_transposed(dk_flat, w_k) + times_transposed(dv_flat, w_v) + d_norm_mlp).astype(BF16)
        dx_norm, grad_gain = norm_back(d_norm)
        grad_x = (grad_flat.astype(F32) + dx_norm).astype(BF16)

        small = jnp.concatenate([grad_gain.reshape(-1, head_dim), gq, gk], axis=0)
        small_all = lax.all_gather(small, 'sp', axis=0)
        gain_rows = model_dim // head_dim
        grad_gain = jnp.sum(small_all[:, :gain_rows], axis=0).reshape(model_dim)
        grad_q_norm = small_all[:, gain_rows]
        grad_k_norm = small_all[::share, gain_rows + 1]

        dw_q = dwq_all.transpose(1, 0, 2).reshape(model_dim, num_heads * head_dim)
        dwkv = dwkv_all.reshape(num_kv, share, model_dim, head_dim)
        dw_k = dwkv[:, 0].transpose(1, 0, 2).reshape(model_dim, num_kv * head_dim)
        dw_v = dwkv[:, 1].transpose(1, 0, 2).reshape(model_dim, num_kv * head_dim)
        return (y_out.reshape(x_in.shape), grad_x.reshape(x_in.shape), dw_q, dw_k, dw_v, dwo_all, dw_gate, dw_up, dw_down,
                grad_gain, grad_q_norm, grad_k_norm)

    in_specs = (seq_spec, seq_spec, P(('dp', 'sp'))) + (P(),) * 10
    out_specs = (seq_spec, seq_spec) + (grad_spec,) * 7 + (P('dp'), grad_spec, grad_spec)
    return jax.shard_map(layer_step, mesh=mesh, in_specs=in_specs, out_specs=out_specs, check_vma=False)
```

time: 1120 us -> 306 us (0.27); the launches traced: 1110 us -> 305 us
  blocking collectives: 688 us -> 40.4 us
  Pallas kernels: 0 us -> 114 us
  matrix products: 144 us -> 32.2 us
  other arithmetic: 104 us -> 12.4 us
  local copies, waits for them, and re-layouts: 102 us -> 20.9 us
  waiting for transfers between devices: 9.93 us -> 60.9 us
  starting transfers between devices: 58.2 us -> 10.2 us
  between operations: 1.9 us -> 14.2 us
    psum x1 -> x0, blocking collectives: 688 us -> none  [layer_step(): lax.psum(part_grad, 'sp').astype(jnp.bfloat16)]
    pallas_call x0 -> x4, Pallas kernels: none -> 114 us  [the longest x1 61 us: layer_step(): pl.pallas_call(functools.partial(mlp_kernel, 256), out_shape=[full_in, fu...]
    dot_general x20 -> x4, matrix products: 118 us -> 16.3 us  [the longest x1 4.7 us: layer_step(): mlp_out = jnp.dot(hidden, w_down, preferred_element_type=F32).astype(BF16)]
    all_gather x0 -> x5, waiting for transfers between devices: none -> 52.5 us  [the longest x1 38.4 us: layer_step(): dy_all = lax.all_gather(grad_flat, 'sp', axis=0, tiled=True)]
    unnamed x6 -> x3, other arithmetic: 51.6 us -> 0.01 us
    all_to_all x8 -> x2, starting transfers between devices: 58.2 us -> 8.46 us  [the longest x1 4.35 us: layer_step(): attn_flat = lax.all_to_all(o_h, 'sp', 0, 1, tiled=True)]
    all_gather x0 -> x2, blocking collectives: none -> 40.4 us  [the longest x1 22.8 us: layer_step(): all_pos = lax.all_gather(positions, 'sp', axis=0, tiled=True)]
    unnamed x169 -> x48, local copies, waits for them, and re-layouts: 33.5 us -> 8.03 us
  transfers between devices with their start and end apart: 8 -> 11, of which waited for: 3 -> 3; matrix products, arithmetic and copies ran while one was open for 21% -> 16% of each run, Pallas kernels for 0% -> 25%
where the time goes in v1:
time: 306 us; the launch traced here: 305 us
  Pallas kernels  114 us (37%)
  waiting for transfers between devices  60.9 us (20%)
  blocking collectives  40.4 us (13%)
  matrix products  32.2 us (11%)
  local copies, waits for them, and re-layouts  20.9 us (7%)
  between operations  14.2 us (5%)
  other arithmetic  12.4 us (4%)
  starting transfers between devices  10.2 us (3%)
    pallas_call x1, Pallas kernels, layer_step(): pl.pallas_call(functools.partial(mlp_kernel, 256), out_shape=[full_in, fu...  61 us
    all_gather x1, waiting for transfers between devices, layer_step(): dy_all = lax.all_gather(grad_flat, 'sp', axis=0, tiled=True)  38.4 us
    pallas_call x1, Pallas kernels, layer_step(): pl.pallas_call(functools.partial(attention_kernel, block), out_shape=[row...  37.4 us
    all_gather x1, blocking collectives, layer_step(): all_pos = lax.all_gather(positions, 'sp', axis=0, tiled=True)  22.8 us
    all_gather x1, blocking collectives, layer_step(): small_all = lax.all_gather(small, 'sp', axis=0)  17.6 us
    dot_general x6, matrix products, times_transposed(): lax.dot_general(lhs_mat, rhs_mat, (((1,), (1,)), ((), ())), preferred_ele...  15.9 us
    all_gather x1, waiting for transfers between devices, layer_step(): n_all = lax.all_gather(flat_norm, 'sp', axis=0, tiled=True)  14.1 us
    pallas_call x1, Pallas kernels, layer_step(): pl.pallas_call(fill_kernel, out_shape=[full_in, full_in, full_out], grid_...  9.24 us
  transfers between devices with their start and end apart: 11, of which 3 were waited for; matrix products, arithmetic and copies ran while one was open for 16% of the time, Pallas kernels for 25%

profile of v1, /device:TPU:21, one launch (start us, length us, event | category | flops | bytes accessed | tf_op | source)
XLA Modules:
  0.0 305.1 jit_solution(10930969437957968331)
XLA Ops:
  12.4 22.8 %all-gather.4 = s32[16,1,128]{2,1,0:T(1,128)S(1)} all-gather(s32[1,1,128]{2,1,0:T(1,128)} %bitcast.127), channel_id=1, replica_groups=mesh['dp'=4,'sp'=16] {'sp'}, dimensions={0}, use_global_device_ids=true | all-gather | bytes 8704 | tf_op jit(solution)/shard_map/all_gather | solution.py:267
  35.8 5.5 %fusion.15 = (f32[2048,128]{1,0:T(8,128)}, f32[2048,128]{1,0:T(8,128)}) fusion(f32[128]{0:T(128)S(1)} %get-tuple-element.62, f32[128]{0:T(128)S(1)} %get-tuple-element.63, f32[2048]{0:T(1024)S(1)} %bitcast.122), kind=kLoop, calls=%fused_computation.31 | loop fusion | flops 524288 | bytes 2106368 | tf_op jit(solution)/shard_map/mul | solution.py:41
  41.3 14.1 %all-gather.12.cloned.1.call-done.n_ref = bf16[2048,1024]{1,0:T(8,128)(2,1)} async-done(((bf16[128,1024]{1,0:T(8,128)(2,1)}), bf16[2048,1024]{1,0:T(8,128)(2,1)}) %all-gather.12.cloned.1.call-update) | async-done | bytes 4194320 | tf_op jit(solution)/shard_map/all_gather | solution.py:271
  55.4 38.4 %all-gather.16.cloned.1.call-done = bf16[1,2048,1024]{2,1,0:T(8,128)(2,1)} async-done(((bf16[1,128,1024]{2,1,0:T(8,128)(2,1)}), bf16[1,2048,1024]{2,1,0:T(8,128)(2,1)}) %all-gather.16.cloned.1.call-update) | async-done | bytes 4194320 | tf_op jit(solution)/shard_map/all_gather | solution.py:272
  93.8 37.4 %attention.1 = (bf16[2048,128]{1,0:T(8,128)(2,1)}, bf16[2048,128]{1,0:T(8,128)(2,1)}, bf16[2048,128]{1,0:T(8,128)(2,1)}, bf16[2048,128]{1,0:T(8,128)(2,1)}, bf16...) custom-call(s32[3]{0:T(128)} %pad_add_fusion.idx_ref, ...), custom_call_target="tpu_custom_call" | custom-call | flops 20000000000 | bytes 20000000 | tf_op jit(solution)/shard_map/attention/pallas_call | solution.py:288
  131.9 3.9 %fusion.45 = f32[128,3072]{1,0:T(8,128)S(1)} fusion(bf16[128,1024]{1,0:T(8,128)(2,1)S(1)} %copy-done.1, bf16[1024,3072]{1,0:T(8,128)(2,1)} %wg_ref.1), kind=kOutput, calls=%fused_computation.76 | convolution fusion | flops 805306368 | bytes 8126464 | tf_op jit(solution)/shard_map/dot_general | solution.py:275
  135.9 4.6 %fusion.46 = f32[128,3072]{1,0:T(8,128)S(1)} fusion(bf16[128,1024]{1,0:T(8,128)(2,1)S(1)} %copy-done.1, bf16[1024,3072]{1,0:T(8,128)(2,1)} %wu_ref.1), kind=kOutput, calls=%fused_computation.77 | convolution fusion | flops 805306368 | bytes 8126464 | tf_op jit(solution)/shard_map/dot_general | solution.py:276
  140.6 2.2 fusion
  143.4 2.4 fusion.16
  146.8 4.3 %all-to-all-start = ((bf16[16,128,128]{1,2,0:T(8,128)(2,1)}), bf16[16,128,128]{1,2,0:T(8,128)(2,1)S(1)}, u32[]{:S(2)}, u32[]{:S(2)}) async-start(bf16[16,128,128]{1,2,0:T(8,128)(2,1)} %copy.40), calls=%async_computation | async-start | bytes 1048576 | tf_op jit(solution)/shard_map/all_to_all | solution.py:371
  152.0 6.3 %key_value.1 = (bf16[2048,128]{1,0:T(8,128)(2,1)}, bf16[1024,128]{1,0:T(8,128)(2,1)}, f32[1,128]{1,0:T(1,128)}) custom-call(s32[3]{0:T(128)} %pad_add_fusion.idx_ref, bf16[2048,128]{1,0:T(8,128)(2,1)} %get-tuple-element.34.keep_ref, bf16[2048,128]{1,0:T(8,128)(2,1)} %copy-done.18, bf16[2048,128]{1,0:T(8,128)(2,1)} %get-tuple-element.36.kproj_ref, ...), custom_call_target="tpu_custom_call" | custom-call | flops 5000000000 | bytes 8000000 | tf_op jit(solution)/shard_map/key_value/pallas_call | solution.py:312
  158.4 6.0 %convolution_add_fusion.1 = f32[128,1024]{1,0:T(8,128)S(1)} fusion(f32[128,1024]{1,0:T(8,128)S(1)} %fusion.16, bf16[1024,3072]{1,0:T(8,128)(2,1)} %wu_ref.1, f32[128,3072]{1,0:T(8,128)} %copy-done.10, f32[128,3072]{1,0:T(8,128)} %copy-done.6), kind=kOutput, calls=%fused_computation.20 | convolution fusion | flops 807796736 | bytes 10485760 | tf_op jit(solution)/shard_map/dot_general | solution.py:29
  165.9 7.0 %all-to-all-done = bf16[16,128,128]{1,2,0:T(8,128)(2,1)S(1)} async-done(((bf16[16,128,128]{1,2,0:T(8,128)(2,1)}), bf16[16,128,128]{1,2,0:T(8,128)(2,1)S(1)}, u32[]{:S(2)}, u32[]{:S(2)}) %all-to-all-start) | async-done | bytes 524320 | tf_op jit(solution)/shard_map/all_to_all | solution.py:371
  172.8 4.1 %all-to-all-start.1 = ((bf16[16,128,256]{1,2,0:T(8,128)(2,1)}), bf16[16,128,256]{1,2,0:T(8,128)(2,1)S(1)}, u32[]{:S(2)}, u32[]{:S(2)}) async-start(bf16[16,128,256]{1,2,0:T(8,128)(2,1)} %copy.41), calls=%async_computation.1 | async-start | bytes 2097152 | tf_op jit(solution)/shard_map/all_to_all | solution.py:375
  177.0 61.0 %mlp.1 = (bf16[1024,3072]{1,0:T(8,128)(2,1)}, bf16[1024,3072]{1,0:T(8,128)(2,1)}, bf16[3072,1024]{1,0:T(8,128)(2,1)}, bf16[1024,1536]{1,0:T(8,128)(2,1)}, bf16[1...) custom-call(s32[3]{0:T(128)} %pad_add_fusion.idx_ref, bf16[2048,1024]{1,0:T(8,128)(2,1)} %all-gather.12.cloned.1.call-done.n_ref, ...), custom_call_target="tpu_custom_call" | custom-call | flops 38654705664 | bytes 40000000 | tf_op jit(solution)/shard_map/mlp/pallas_call | solution.py:341
  238.8 3.1 %fusion.13 = f32[128,1024]{1,0:T(8,128)S(1)} fusion(bf16[128,2048]{0,1:T(8,128)(2,1)S(1)} %bitcast.118, bf16[2048,1024]{1,0:T(8,128)(2,1)} %wo_ref.1, bf16[1,128,1024]{2,1,0:T(8,128)(2,1)S(1)} %copy-done), kind=kOutput, calls=%fused_computation.29 | convolution fusion | flops 537395200 | bytes 5505024 | tf_op jit(solution)/shard_map/dot_general | solution.py:372
  241.9 4.7 %fusion.14 = bf16[1,128,1024]{2,1,0:T(8,128)(2,1)} fusion(f32[128,1024]{1,0:T(8,128)S(1)} %fusion.13, bf16[3072,1024]{1,0:T(8,128)(2,1)} %wd_ref.1, f32[128,3072]{1,0:T(8,128)S(1)} %copy-done.9, f32[128,3072]{1,0:T(8,128)S(1)} %copy-done.7), kind=kOutput, calls=%fused_computation.30 | convolution fusion | flops 808189952 | bytes 10223616 | tf_op jit(solution)/shard_map/dot_general | solution.py:278
  249.1 2.8 fusion.48
  254.0 17.6 %all-gather.5 = f32[16,10,128]{2,1,0:T(8,128)S(1)} all-gather(f32[1,10,128]{2,1,0:T(8,128)S(1)} %maximum_bitcast_fusion), channel_id=5, replica_groups=mesh['dp'=4,'sp'=16] {'sp'}, dimensions={0}, use_global_device_ids=true | all-gather | bytes 87040 | tf_op jit(solution)/shard_map/all_gather | solution.py:385
  274.4 9.2 %fill.1 = (bf16[1024,3072]{1,0:T(8,128)(2,1)}, bf16[1024,3072]{1,0:T(8,128)(2,1)}, bf16[3072,1024]{1,0:T(8,128)(2,1)}) custom-call(s32[3]{0:T(128)} %pad_add_fusion.idx_ref, bf16[1024,1536]{1,0:T(8,128)(2,1)} %collective-permute-done.1.hg_ref, ...), custom_call_target="tpu_custom_call", output_to_operand_aliasing={{0}: (4, {}), {1}: (5, {}), {2}: (6, {})} | custom-call | flops 1000000000 | bytes 20000000 | tf_op jit(solution)/shard_map/fill/pallas_call | solution.py:359
  283.7 5.4 %copy.51 = bf16[16,128,8,128]{3,2,0,1:T(8,128)(2,1)} copy(bf16[16,128,8,128]{3,2,1,0:T(8,128)(2,1)} %bitcast.109) | data formatting | bytes 8388608 | tf_op jit(solution)/shard_map/reshape | solution.py:391
  289.1 2.5 slice_bitcast_fusion
  291.6 1.9 copy.52
  296.5 2.0 copy.58
  (94 shorter events, 21.5 us)
Async XLA Ops:
  7.2 48.2 %all-gather.12.cloned.1.call-start = ((), (), s32[]{:S(2)}) async-start(), calls=%async_computation.2 | async-start | bytes 4456448 | tf_op jit(solution)/shard_map/all_gather | solution.py:271
  11.5 82.3 %all-gather.16.cloned.1.call-start = ((), (), s32[]{:S(2)}) async-start(), calls=%async_computation.4 | async-start | bytes 4456448 | tf_op jit(solution)/shard_map/all_gather | solution.py:272
  12.3 271.4 %all-gather.18.cloned.1.call-start = ((), (), s32[]{:S(2)}) async-start(), calls=%async_computation.5 | async-start | bytes 4456448 | tf_op jit(solution)/shard_map/all_gather | solution.py:327
  93.8 38.1 %copy-start.1 = (bf16[128,1024]{1,0:T(8,128)(2,1)S(1)}, bf16[128,1024]{1,0:T(8,128)(2,1)}, u32[]{:S(2)}) copy-start(bf16[128,1024]{1,0:T(8,128)(2,1)} %fusion.26) | copy-start | bytes 786436
  131.2 157.9 %all-gather.14.cloned.1.call-start = ((), (), s32[]{:S(2)}) async-start(), calls=%async_computation.3 | async-start | bytes 4456448 | tf_op jit(solution)/shard_map/all_gather | solution.py:326
  131.9 8.6 %slice-start.2 = ((s8[6291456]{0:T(1024)(128)(4,1)}), s8[4194304]{0:T(1024)(128)(4,1)S(1)}, s32[]{:S(2)}) async-start(s8[6291456]{0:T(1024)(128)(4,1)} %bitcast.107), calls=%async_computation.9 | async-start | bytes 8388608
  131.9 11.5 %slice-start = ((s8[6291456]{0:T(1024)(128)(4,1)}), s8[4194304]{0:T(1024)(128)(4,1)S(1)}, s32[]{:S(2)}) async-start(s8[6291456]{0:T(1024)(128)(4,1)} %bitcast.105), calls=%async_computation.7 | async-start | bytes 8388608
  135.8 7.6 %copy-start.6 = (f32[128,3072]{1,0:T(8,128)}, f32[128,3072]{1,0:T(8,128)S(1)}, u32[]{:S(2)}) copy-start(f32[128,3072]{1,0:T(8,128)S(1)} %fusion.45) | copy-start | bytes 4718596
  135.8 4.7 %slice-start.3 = ((s8[6291456]{0:T(1024)(128)(4,1)}), s8[2097152]{0:T(1024)(128)(4,1)S(1)}, s32[]{:S(2)}) async-start(s8[6291456]{0:T(1024)(128)(4,1)} %bitcast.107), calls=%async_computation.10 | async-start | bytes 4194304
  135.9 4.7 %copy-start.4 = (bf16[1,128,1024]{2,1,0:T(8,128)(2,1)S(1)}, bf16[1,128,1024]{2,1,0:T(8,128)(2,1)}, u32[]{:S(2)}) copy-start(bf16[1,128,1024]{2,1,0:T(8,128)(2,1)} %param.14) | copy-start | bytes 786436
  135.9 7.5 %slice-start.1 = ((s8[6291456]{0:T(1024)(128)(4,1)}), s8[2097152]{0:T(1024)(128)(4,1)S(1)}, s32[]{:S(2)}) async-start(s8[6291456]{0:T(1024)(128)(4,1)} %bitcast.105), calls=%async_computation.8 | async-start | bytes 4194304
  142.8 8.4 %collective-permute-start = (bf16[2048,128]{1,0:T(8,128)(2,1)S(1)}, bf16[2048,128]{1,0:T(8,128)(2,1)S(1)}, u32[]{:S(2)}, u32[]{:S(2)}) collective-permute-start(bf16[2048,128]{1,0:T(8,128)(2,1)S(1)} %copy-done.17), channel_id=1, source_target_pairs={{0,1},{1,0},{2,3},{3,2},{4,5},{5,4},{6,7},{7,6},{8,9},{9,8},{10,11... | collective-permute-start | bytes 1572872 | tf_op jit(solution)/shard_map/ppermute | solution.py:311
  146.8 26.0 %all-to-all-start = ((bf16[16,128,128]{1,2,0:T(8,128)(2,1)}), bf16[16,128,128]{1,2,0:T(8,128)(2,1)S(1)}, u32[]{:S(2)}, u32[]{:S(2)}) async-start(bf16[16,128,128]{1,2,0:T(8,128)(2,1)} %copy.40), calls=%async_computation | async-start | bytes 1048576 | tf_op jit(solution)/shard_map/all_to_all | solution.py:371
  151.2 137.9 %all-gather.20.cloned.1.call-start = ((), (), s32[]{:S(2)}) async-start(), calls=%async_computation.6 | async-start | bytes 4456448 | tf_op jit(solution)/shard_map/all_gather | solution.py:328
  158.4 6.1 %copy-start.12 = (bf16[2048,128]{1,0:T(8,128)(2,1)S(1)}, bf16[2048,128]{1,0:T(8,128)(2,1)}, u32[]{:S(2)}) copy-start(bf16[2048,128]{1,0:T(8,128)(2,1)} %get-tuple-element.33) | copy-start | bytes 1572868
  158.4 6.1 %copy-start.13 = (bf16[2048,128]{1,0:T(8,128)(2,1)S(1)}, bf16[2048,128]{1,0:T(8,128)(2,1)}, u32[]{:S(2)}) copy-start(bf16[2048,128]{1,0:T(8,128)(2,1)} %get-tuple-element.37) | copy-start | bytes 1572868
  172.8 73.8 %all-to-all-start.1 = ((bf16[16,128,256]{1,2,0:T(8,128)(2,1)}), bf16[16,128,256]{1,2,0:T(8,128)(2,1)S(1)}, u32[]{:S(2)}, u32[]{:S(2)}) async-start(bf16[16,128,256]{1,2,0:T(8,128)(2,1)} %copy.41), calls=%async_computation.1 | async-start | bytes 2097152 | tf_op jit(solution)/shard_map/all_to_all | solution.py:375
  177.0 61.8 %copy-start = (bf16[1,128,1024]{2,1,0:T(8,128)(2,1)S(1)}, bf16[1,128,1024]{2,1,0:T(8,128)(2,1)}, u32[]{:S(2)}) copy-start(bf16[1,128,1024]{2,1,0:T(8,128)(2,1)} %param.13) | copy-start | bytes 786436
  237.9 36.5 %collective-permute-start.1 = (bf16[1024,1536]{1,0:T(8,128)(2,1)}, bf16[1024,1536]{1,0:T(8,128)(2,1)}, u32[]{:S(2)}, u32[]{:S(2)}) collective-permute-start(bf16[1024,1536]{1,0:T(8,128)(2,1)} %get-tuple-element.41), channel_id=1, source_target_pairs={{0,1},{1,0},{2,3},{3,2},{4,5},{5,4},{6,7},{7,6},{8,9},{9,8},{10,11... | collective-permute-start | bytes 9437192 | tf_op jit(solution)/shard_map/ppermute | solution.py:353
  238.3 36.2 %collective-permute-start.2 = (bf16[1024,1536]{1,0:T(8,128)(2,1)}, bf16[1024,1536]{1,0:T(8,128)(2,1)}, u32[]{:S(2)}, u32[]{:S(2)}) collective-permute-start(bf16[1024,1536]{1,0:T(8,128)(2,1)} %get-tuple-element.42), channel_id=1, source_target_pairs={{0,1},{1,0},{2,3},{3,2},{4,5},{5,4},{6,7},{7,6},{8,9},{9,8},{10,11... | collective-permute-start | bytes 9437192 | tf_op jit(solution)/shard_map/ppermute | solution.py:354
  238.5 36.0 %collective-permute-start.3 = (bf16[1536,1024]{1,0:T(8,128)(2,1)}, bf16[1536,1024]{1,0:T(8,128)(2,1)}, u32[]{:S(2)}, u32[]{:S(2)}) collective-permute-start(bf16[1536,1024]{1,0:T(8,128)(2,1)} %get-tuple-element.43), channel_id=1, source_target_pairs={{0,1},{1,0},{2,3},{3,2},{4,5},{5,4},{6,7},{7,6},{8,9},{9,8},{10,11... | collective-permute-start | bytes 9437192 | tf_op jit(solution)/shard_map/ppermute | solution.py:355
  238.8 3.1 %copy-start.7 = (f32[128,3072]{1,0:T(8,128)S(1)}, f32[128,3072]{1,0:T(8,128)}, u32[]{:S(2)}) copy-start(f32[128,3072]{1,0:T(8,128)} %copy-done.6) | copy-start | bytes 4718596
  238.8 3.1 %copy-start.9 = (f32[128,3072]{1,0:T(8,128)S(1)}, f32[128,3072]{1,0:T(8,128)}, u32[]{:S(2)}) copy-start(f32[128,3072]{1,0:T(8,128)} %copy-done.8) | copy-start | bytes 4718596
  248.2 3.7 %copy-start.2 = (bf16[1024,2048]{1,0:T(8,128)(2,1)S(1)}, bf16[1024,2048]{1,0:T(8,128)(2,1)}, u32[]{:S(2)}) copy-start(bf16[1024,2048]{1,0:T(8,128)(2,1)} %wq_ref.1) | copy-start | bytes 12582916
  (10 other events, 23.4 us)
Sparse Core Ops, SparseCore 0:
  11.6 43.7 all-gather.11
  57.0 36.7 all-gather.15
  131.4 46.0 all-gather.17
  178.9 49.0 all-gather.13
  229.5 37.4 all-gather.19

commit v2 on v1

v2 whole, which is shorter than its diff:
```python
import functools

import jax
import jax.numpy as jnp
from jax import lax
from jax.experimental import pallas as pl
from jax.experimental.pallas import tpu as pltpu
from jax.sharding import PartitionSpec as P

NORM_EPS = 1e-5
ROPE_THETA = 75.0e6
VMEM_LIMIT = 60 * 1024 * 1024
F32 = jnp.float32
BF16 = jnp.bfloat16
MESH = pl.DeviceIdType.MESH


def input_norm(x_f32, norm_gain):
    row_mean = jnp.mean(x_f32, axis=-1, keepdims=True)
    centered = x_f32 - row_mean
    row_var = jnp.mean(centered * centered, axis=-1, keepdims=True)
    return (centered * lax.rsqrt(row_var + NORM_EPS) * norm_gain).astype(BF16)


def swiglu(gate_pre, up_proj):
    return (jax.nn.silu(gate_pre) * up_proj).astype(BF16)


def times_transposed(lhs_mat, rhs_mat):
    return lax.dot_general(lhs_mat, rhs_mat, (((1,), (1,)), ((), ())), preferred_element_type=F32)


def transposed_times(lhs_mat, rhs_mat):
    return lax.dot_general(lhs_mat, rhs_mat, (((0,), (0,)), ((), ())), preferred_element_type=F32)


def rope_lanes(positions, head_dim):
    pair_index = jnp.arange(head_dim, dtype=jnp.int32) // 2
    inv_freq = ROPE_THETA ** (-(pair_index.astype(F32) * 2.0) / head_dim)
    angles = positions.astype(F32)[:, None] * inv_freq[None, :]
    sign = jnp.where(jnp.arange(head_dim) % 2 == 0, -1.0, 1.0).astype(F32)
    return jnp.cos(angles), jnp.sin(angles) * sign[None, :]


def swap_pairs(rows):
    lane = lax.broadcasted_iota(jnp.int32, rows.shape, 1)
    width = rows.shape[1]
    return jnp.where(lane % 2 == 0, pltpu.roll(rows, width - 1, 1), pltpu.roll(rows, 1, 1))


def head_stats(proj_f32):
    row_mean = jnp.mean(proj_f32, axis=-1, keepdims=True)
    centered = proj_f32 - row_mean
    inv_std = lax.rsqrt(jnp.mean(centered * centered, axis=-1, keepdims=True) + NORM_EPS)
    return centered * inv_std, inv_std


def head_forward(proj_f32, weight, cos_t, sin_t):
    unit, _ = head_stats(proj_f32)
    normed = unit * weight
    return (normed * cos_t + swap_pairs(normed) * sin_t).astype(BF16)


def head_backward(d_rot, proj_f32, weight, cos_t, sin_t):
    unit, inv_std = head_stats(proj_f32)
    d_normed = d_rot * cos_t + swap_pairs(d_rot * sin_t)
    d_weight = jnp.sum(d_normed * unit, axis=0, keepdims=True)
    d_unit = d_normed * weight
    mean_d = jnp.mean(d_unit, axis=-1, keepdims=True)
    mean_du = jnp.mean(d_unit * unit, axis=-1, keepdims=True)
    return inv_std * (d_unit - mean_d - unit * mean_du), d_weight


def forward_kernel(block, idx_ref, n_s, wq_ref, wk_ref, wv_ref, qn_ref, kn_ref, cos_ref, sin_ref,
                   o_ref, o32_ref, lse_ref, q_ref, k_ref, v_ref, qproj_ref, kproj_ref, e_s):
    seq_len, head_dim = o_ref.shape
    steps = seq_len // block
    scale = head_dim ** -0.5

    def project(i, carry):
        rows = pl.ds(pl.multiple_of(i * block, block), block)
        n_rows = n_s[rows, :]
        weights = jnp.concatenate([wq_ref[...], wk_ref[...], wv_ref[...]], axis=1)
        proj = jnp.dot(n_rows, weights, preferred_element_type=F32).astype(BF16)
        q_proj, k_proj = proj[:, :head_dim], proj[:, head_dim:2 * head_dim]
        qproj_ref[rows, :] = q_proj
        kproj_ref[rows, :] = k_proj
        v_ref[rows, :] = proj[:, 2 * head_dim:]
        cos_t, sin_t = cos_ref[rows, :], sin_ref[rows, :]
        q_ref[rows, :] = head_forward(q_proj.astype(F32), qn_ref[0], cos_t, sin_t)
        k_ref[rows, :] = head_forward(k_proj.astype(F32), kn_ref[0], cos_t, sin_t)
        return carry

    lax.fori_loop(0, steps, project, 0)
    causal = lax.broadcasted_iota(jnp.int32, (block, block), 0) >= lax.broadcasted_iota(jnp.int32, (block, block), 1)

    def lanes(op, tile):
        return functools.reduce(op, [tile[:, c:c + 128] for c in range(0, block, 128)])

    def keys_of(j):
        return pl.ds(pl.multiple_of(j * block, block), block)

    def query_block(i, carry):
        rows = keys_of(i)
        q_rows = q_ref[rows, :]

        def score(j, top):
            tile = times_transposed(q_rows, k_ref[keys_of(j), :])
            e_s[:, keys_of(j)] = tile
            return jnp.maximum(top, lanes(jnp.maximum, tile))

        top = lax.fori_loop(0, i, score, jnp.full((block, 128), -1e30, F32))
        diag = jnp.where(causal, times_transposed(q_rows, k_ref[rows, :]), -1e30)
        e_s[:, rows] = diag
        top = jnp.max(jnp.maximum(top, lanes(jnp.maximum, diag)), axis=-1, keepdims=True)

        def exponent(j, total):
            tile = jnp.exp((e_s[:, keys_of(j)] - top) * scale)
            e_s[:, keys_of(j)] = tile
            return total + lanes(jnp.add, tile)

        total = lax.fori_loop(0, i + 1, exponent, jnp.zeros((block, 128), F32))
        total = jnp.sum(total, axis=-1, keepdims=True)
        inv_total = 1.0 / total

        def attend(j, acc):
            probs = (e_s[:, keys_of(j)] * inv_total).astype(BF16)
            return acc + jnp.dot(probs, v_ref[keys_of(j), :], preferred_element_type=F32)

        out = lax.fori_loop(0, i + 1, attend, jnp.zeros((block, head_dim), F32))
        o_ref[rows, :] = out.astype(BF16)
        o32_ref[rows, :] = out
        lse_ref[rows, :] = jnp.broadcast_to(top * scale + jnp.log(total), (block, 128))
        return carry

    lax.fori_loop(0, steps, query_block, 0)


def output_grad_kernel(idx_ref, dy_s, wo_ref, o_ref, do_ref, dwo_ref):
    dwo_ref[...] = transposed_times(o_ref[...], dy_s[...]).astype(BF16)
    do_ref[...] = times_transposed(dy_s[...], wo_ref[...]).astype(BF16)


def backward_kernel(block, idx_ref, do_ref, o32_ref, lse_ref, q_ref, k_ref, v_ref, qproj_ref, qn_ref, cos_ref, sin_ref,
                    dq_ref, send_ref, keep_ref, gq_ref, dk_s, dv_s):
    seq_len, head_dim = do_ref.shape
    steps = seq_len // block
    scale = head_dim ** -0.5
    causal = lax.broadcasted_iota(jnp.int32, (block, block), 0) >= lax.broadcasted_iota(jnp.int32, (block, block), 1)
    dk_s[...] = jnp.zeros_like(dk_s)
    dv_s[...] = jnp.zeros_like(dv_s)
    gq_ref[...] = jnp.zeros_like(gq_ref)

    def query_block(i, carry):
        rows = pl.ds(pl.multiple_of(i * block, block), block)
        q_rows, do_rows = q_ref[rows, :], do_ref[rows, :]
        delta = jnp.sum(o32_ref[rows, :] * do_rows.astype(F32), axis=-1, keepdims=True)
        lse = lse_ref[rows, :][:, :1]

        def tile_back(keys, masked):
            k_rows, v_rows = k_ref[keys, :], v_ref[keys, :]
            probs = jnp.exp(times_transposed(q_rows, k_rows) * scale - lse)
            if masked:
                probs = jnp.where(causal, probs, 0.0)
            d_probs = times_transposed(do_rows, v_rows).astype(BF16).astype(F32)
            d_score = (probs * (d_probs - delta) * scale).astype(BF16)
            dv_s[keys, :] += transposed_times(probs.astype(BF16), do_rows)
            dk_s[keys, :] += transposed_times(d_score, q_rows)
            return jnp.dot(d_score, k_rows, preferred_element_type=F32)

        def back(j, acc):
            return acc + tile_back(pl.ds(pl.multiple_of(j * block, block), block), False)

        dq = lax.fori_loop(0, i, back, tile_back(rows, True)).astype(BF16).astype(F32)
        dq_proj, d_weight = head_backward(dq, qproj_ref[rows, :].astype(F32), qn_ref[0], cos_ref[rows, :], sin_ref[rows, :])
        dq_ref[rows, :] = dq_proj.astype(BF16)
        gq_ref[...] += d_weight
        return carry

    lax.fori_loop(0, steps, query_block, 0)
    first = idx_ref[2] == 0

    @pl.when(first)
    def _():
        keep_ref[...] = dk_s[...].astype(BF16)
        send_ref[...] = dv_s[...].astype(BF16)

    @pl.when(jnp.logical_not(first))
    def _():
        keep_ref[...] = dv_s[...].astype(BF16)
        send_ref[...] = dk_s[...].astype(BF16)


def projection_grad_kernel(idx_ref, n_s, dq_ref, keep_ref, got_ref, kproj_ref, kn_ref, cos_ref, sin_ref,
                           rows_ref, dw_ref, gk_ref):
    head_dim = dq_ref.shape[1]
    total = (keep_ref[...].astype(F32) + got_ref[...].astype(F32)).astype(BF16)
    rows_ref[:, :head_dim] = dq_ref[...]
    first = idx_ref[2] == 0

    @pl.when(first)
    def _():
        dk_proj, d_weight = head_backward(total.astype(F32), kproj_ref[...].astype(F32), kn_ref[0], cos_ref[...], sin_ref[...])
        rows_ref[:, head_dim:] = dk_proj.astype(BF16)
        gk_ref[...] = d_weight

    @pl.when(jnp.logical_not(first))
    def _():
        rows_ref[:, head_dim:] = total
        gk_ref[...] = jnp.zeros_like(gk_ref)

    dw_ref[...] = transposed_times(n_s[...], rows_ref[...]).astype(BF16)


class Ring:
    def __init__(self, devices):
        self.chips = devices // 2
        self.me = lax.axis_index('sp')
        self.z, self.core = self.me // 2, self.me % 2
        self.turn = 1 - 2 * self.core
        self.partner = self.me + self.turn
        self.after = self.device(self.z + self.turn, self.core)
        self.before = self.device(self.z - self.turn, self.core)

    def device(self, z, core):
        return 2 * lax.rem(z + 2 * self.chips, self.chips) + core

    def own_slot(self, step):
        return self.device(self.z - self.turn * step, self.core)

    def other_slot(self, step):
        return self.device(self.z + self.turn * step, 1 - self.core)

    def barrier(self):
        sem = pltpu.get_barrier_semaphore()
        for device in (self.after, self.before, self.partner):
            pl.semaphore_signal(sem, inc=1, device_id={'sp': device}, device_id_type=MESH)
        pl.semaphore_wait(sem, 3)

    def forward(self, buf, sems, lane, step):
        slot = buf.at[self.own_slot(step)]
        return pltpu.make_async_remote_copy(slot, slot, sems[0].at[lane, step], sems[1].at[lane, step + 1],
                                            device_id={'sp': self.after}, device_id_type=MESH)

    def share(self, buf, sems, lane, step):
        slot = buf.at[self.own_slot(step)]
        return pltpu.make_async_remote_copy(slot, slot, sems[2].at[lane, step], sems[3].at[lane, step],
                                            device_id={'sp': self.partner}, device_id_type=MESH)

    def arrived(self, buf, sems, lane, step):
        slot = buf.at[self.own_slot(step)]
        return pltpu.make_async_remote_copy(slot, slot, sems[0].at[lane, step], sems[1].at[lane, step],
                                            device_id={'sp': self.before}, device_id_type=MESH)

    def shared(self, buf, sems, lane, step):
        slot = buf.at[self.other_slot(step)]
        return pltpu.make_async_remote_copy(slot, slot, sems[2].at[lane, step], sems[3].at[lane, step],
                                            device_id={'sp': self.partner}, device_id_type=MESH)

    def take(self, buf, sems, lane, step):
        @pl.when(step > 0)
        def _():
            self.arrived(buf, sems, lane, step).wait_recv()

        @pl.when(step < self.chips - 1)
        def _():
            self.forward(buf, sems, lane, step).start()
        self.share(buf, sems, lane, step).start()
        self.shared(buf, sems, lane, step).wait_recv()

    def finish(self, buf, sems, lane):
        def body(step, carry):
            @pl.when(step < self.chips - 1)
            def _():
                self.forward(buf, sems, lane, step).wait_send()
            self.share(buf, sems, lane, step).wait_send()
            return carry
        lax.fori_loop(0, self.chips, body, 0)


def gather_kernel(devices, n_ref, dy_ref, pos_ref, wg_ref, wu_ref, wd_ref,
                  n_out, dy_out, pos_out, hid_out, dg_out, du_out, mlp_out, dn_out,
                  n_s, dy_s, pos_s, wg_s, wu_s, wd_s, hid_s, dg_s, du_s, gate_s, up_s, part_s, got_s,
                  load_sem, weight_sem, ring_send, ring_recv, pair_send, pair_recv, out_sem, act_sem, swap_send, swap_recv):
    ring = Ring(devices)
    sems = (ring_send, ring_recv, pair_send, pair_recv)
    half = wg_s.shape[1]
    lanes = ((pos_s, pos_ref, pos_out), (n_s, n_ref, n_out), (dy_s, dy_ref, dy_out))
    loads = [pltpu.make_async_copy(src, buf.at[ring.me], load_sem.at[i]) for i, (buf, src, _) in enumerate(lanes)]
    columns = pl.ds(pl.multiple_of(ring.core * half, half), half)
    weights = [pltpu.make_async_copy(wg_ref.at[:, columns], wg_s, weight_sem.at[0]),
               pltpu.make_async_copy(wu_ref.at[:, columns], wu_s, weight_sem.at[1]),
               pltpu.make_async_copy(wd_ref.at[columns, :], wd_s, weight_sem.at[2])]
    for copy in loads + weights:
        copy.start()
    ring.barrier()
    for copy in loads:
        copy.wait()

    tile = 512
    acts = ((hid_s, hid_out), (dg_s, dg_out), (du_s, du_out))

    def put(lane, slot):
        buf, _, out = lanes[lane]
        return pltpu.make_async_copy(buf.at[slot], out.at[slot], out_sem.at[lane, slot])

    def put_act(i, slot):
        return pltpu.make_async_copy(acts[i][0].at[slot], acts[i][1].at[slot], act_sem.at[i, slot])

    def step_body(step, carry):
        mine, other = ring.own_slot(step), ring.other_slot(step)
        ring.take(n_s, sems, 1, step)
        ring.take(pos_s, sems, 0, step)

        @pl.when(step == 0)
        def _():
            weights[0].wait()
            weights[1].wait()

        def gate_up(j, inner):
            cols = pl.ds(pl.multiple_of(j * tile, tile), tile)
            n_rows = jnp.concatenate([n_s[mine], n_s[other]], axis=0)
            gate_s[:, cols] = jnp.dot(n_rows, wg_s[:, cols], preferred_element_type=F32)
            up_s[:, cols] = jnp.dot(n_rows, wu_s[:, cols], preferred_element_type=F32)
            return inner
        lax.fori_loop(0, half // tile, gate_up, 0)
        ring.take(dy_s, sems, 2, step)
        for lane in range(3):
            put(lane, mine).start()
            put(lane, other).start()

        @pl.when(step == 0)
        def _():
            weights[2].wait()

        def hidden(j, inner):
            cols = pl.ds(pl.multiple_of(j * tile, tile), tile)
            dy_rows = jnp.concatenate([dy_s[mine], dy_s[other]], axis=0)
            d_hidden = times_transposed(dy_rows, wd_s[cols, :]).astype(BF16).astype(F32)
            gate, up = gate_s[:, cols], up_s[:, cols]
            sig = jax.nn.sigmoid(gate)
            silu = gate * sig
            hid = (silu * up).astype(BF16)
            d_up = (d_hidden * silu).astype(BF16)
            d_gate = (d_hidden * up * (sig * (1.0 + gate * (1.0 - sig)))).astype(BF16)
            rows = hid.shape[0] // 2
            for buf, value in ((hid_s, hid), (dg_s, d_gate), (du_s, d_up)):
                buf[mine, :, cols] = value[:rows]
                buf[other, :, cols] = value[rows:]
            return inner
        lax.fori_loop(0, half // tile, hidden, 0)

        @pl.when(step > 0)
        def _():
            for i in range(3):
                put_act(i, ring.own_slot(step - 1)).start()
                put_act(i, ring.other_slot(step - 1)).start()
        return carry

    lax.fori_loop(0, ring.chips, step_body, 0)
    last = ring.chips - 1
    for i in range(3):
        put_act(i, ring.own_slot(last)).start()
        put_act(i, ring.other_slot(last)).start()

    def partial(slot):
        return (jnp.dot(hid_s[slot], wd_s[...], preferred_element_type=F32),
                times_transposed(dg_s[slot], wg_s[...]) + times_transposed(du_s[slot], wu_s[...]))

    part_s[0], part_s[1] = partial(ring.partner)
    mine_m, mine_n = partial(ring.me)
    dn_out[...] = mine_n
    swap = pltpu.make_async_remote_copy(part_s, got_s, swap_send, swap_recv, device_id={'sp': ring.partner}, device_id_type=MESH)
    swap.start()
    for lane in range(3):
        ring.finish(lanes[lane][0], sems, lane)

    def drain(slot, carry):
        for lane in range(3):
            put(lane, slot).wait()
            put_act(lane, slot).wait()
        return carry
    lax.fori_loop(0, devices, drain, 0)
    swap.wait()
    mlp_out[...] = (mine_m + got_s[0]).astype(BF16)
    dn_out[...] += got_s[1]


def weight_kernel(devices, dwo_ref, dwqkv_ref, n_ref, dy_ref, hid_ref, dg_ref, du_ref,
                  q_out, k_out, v_out, o_out, g_out, u_out, d_out,
                  wo_s, wqkv_s, n_s, dy_s, nt_s, hid_s, dg_s, du_s, st_g, st_u, st_d,
                  load_sem, tile_sem, ring_send, ring_recv, pair_send, pair_recv, out_sem, kv_sem,
                  put_sem, swap_send, swap_recv):
    ring = Ring(devices)
    sems = (ring_send, ring_recv, pair_send, pair_recv)
    head_dim, model_dim = dwo_ref.shape
    half = hid_ref.shape[1]
    tile = st_g.shape[2]
    tiles = half // tile
    loads = [pltpu.make_async_copy(dwo_ref, wo_s.at[ring.me], load_sem.at[0]),
             pltpu.make_async_copy(dwqkv_ref, wqkv_s.at[ring.me], load_sem.at[1]),
             pltpu.make_async_copy(n_ref, n_s, load_sem.at[2]),
             pltpu.make_async_copy(dy_ref, dy_s, load_sem.at[3])]
    tile_bufs = ((hid_ref, hid_s), (dg_ref, dg_s), (du_ref, du_s))

    def fetch(i, t):
        cols = pl.ds(pl.multiple_of(t * tile, tile), tile)
        return pltpu.make_async_copy(tile_bufs[i][0].at[:, cols], tile_bufs[i][1].at[t % 2], tile_sem.at[i, t % 2])

    for copy in loads:
        copy.start()
    for i in range(3):
        fetch(i, 0).start()
    ring.barrier()
    loads[0].wait()
    loads[1].wait()

    def put_o(slot):
        rows = pl.ds(pl.multiple_of(slot * head_dim, head_dim), head_dim)
        return pltpu.make_async_copy(wo_s.at[slot], o_out.at[rows, :], out_sem.at[0, slot])

    def put_q(slot):
        cols = pl.ds(pl.multiple_of(slot * head_dim, head_dim), head_dim)
        return pltpu.make_async_copy(wqkv_s.at[slot, :, pl.ds(0, head_dim)], q_out.at[:, cols], out_sem.at[1, slot])

    def put_kv(slot, out):
        cols = pl.ds(pl.multiple_of(slot // 2 * head_dim, head_dim), head_dim)
        return pltpu.make_async_copy(wqkv_s.at[slot, :, pl.ds(head_dim, head_dim)], out.at[:, cols], kv_sem.at[slot])

    def store(t, i, core):
        st, out = ((st_g, g_out), (st_u, u_out), (st_d, d_out))[i]
        span = pl.ds(pl.multiple_of(core * half + t * tile, tile), tile)
        return st.at[t], (out.at[span, :] if i == 2 else out.at[:, span])

    def put_tile(t, i):
        src, dst = store(t, i, ring.core)
        return pltpu.make_async_copy(src, dst, put_sem.at[i, t])

    def send_tile(t, i, core):
        src, dst = store(t, i, core)
        return pltpu.make_async_remote_copy(src, dst, swap_send.at[i, t], swap_recv.at[i, t],
                                            device_id={'sp': ring.partner}, device_id_type=MESH)

    def step_body(step, carry):
        ring.take(wo_s, sems, 0, step)

        @pl.when(step == 0)
        def _():
            loads[2].wait()

            def turn(i, inner):
                rows = pl.ds(pl.multiple_of(i * 256, 256), 256)
                nt_s[:, rows] = n_s[rows, :].T
                return inner
            lax.fori_loop(0, n_s.shape[0] // 256, turn, 0)
            loads[3].wait()

        piece = model_dim // 4

        @pl.when(step < tiles)
        def _():
            for i in range(3):
                fetch(i, step).wait()

            @pl.when(step + 1 < tiles)
            def _():
                for i in range(3):
                    fetch(i, step + 1).start()

            def in_weights(i, inner):
                rows = pl.ds(pl.multiple_of(i * piece, piece), piece)
                st_g[step, rows, :] = jnp.dot(nt_s[rows, :], dg_s[step % 2], preferred_element_type=F32).astype(BF16)
                st_u[step, rows, :] = jnp.dot(nt_s[rows, :], du_s[step % 2], preferred_element_type=F32).astype(BF16)
                return inner
            lax.fori_loop(0, 4, in_weights, 0)

        ring.take(wqkv_s, sems, 1, step)
        for slot in (ring.own_slot(step), ring.other_slot(step)):
            put_o(slot).start()
            put_q(slot).start()

            @pl.when(slot % 2 == 0)
            def _():
                put_kv(slot, k_out).start()

            @pl.when(slot % 2 == 1)
            def _():
                put_kv(slot, v_out).start()

        @pl.when(step < tiles)
        def _():
            st_d[step] = transposed_times(hid_s[step % 2], dy_s[...]).astype(BF16)

        @pl.when(jnp.logical_and(step > 0, step <= tiles))
        def _():
            for i in range(3):
                put_tile(step - 1, i).start()
                send_tile(step - 1, i, ring.core).start()
        return carry

    lax.fori_loop(0, ring.chips, step_body, 0)
    ring.finish(wo_s, sems, 0)
    ring.finish(wqkv_s, sems, 1)

    def drain(slot, carry):
        put_o(slot).wait()
        put_q(slot).wait()
        put_kv(slot, k_out).wait()
        return carry
    lax.fori_loop(0, devices, drain, 0)

    def drain_tiles(t, carry):
        for i in range(3):
            put_tile(t, i).wait()
            send_tile(t, i, ring.core).wait_send()
            send_tile(t, i, 1 - ring.core).wait_recv()
        return carry
    lax.fori_loop(0, tiles, drain_tiles, 0)


def whole(shape):
    return pl.BlockSpec(shape, lambda *_: (0,) * len(shape))


def solution(mesh):
    group_devices = mesh.shape['sp']
    seq_spec = P('dp', 'sp', None)
    grad_spec = P('dp', None)
    pair_swap = [(i, i ^ 1) for i in range(group_devices)]
    def spread(piece):
        copies = jnp.broadcast_to(piece[None], (group_devices,) + piece.shape)
        return lax.all_to_all(copies, 'sp', 0, 0, tiled=True)

    def layer_step(x_in, grad_y, positions, w_q, w_k, w_v, w_o, w_gate, w_up, w_down, norm_gain, q_norm, k_norm):
        batch_rows, local_len, model_dim = x_in.shape
        num_heads, head_dim = q_norm.shape
        num_kv = k_norm.shape[0]
        share = num_heads // num_kv
        ffn_dim = w_gate.shape[1]
        seq_len = local_len * group_devices
        me = lax.axis_index('sp')
        idx = jnp.stack([me, me // share, me % 2]).astype(jnp.int32)
        params = pltpu.CompilerParams(vmem_limit_bytes=VMEM_LIMIT)
        hbm = pl.BlockSpec(memory_space=pl.ANY)

        def call(kernel, name, flops, bytes_accessed, grid, in_specs, out_specs, out_shape, scratch, aliases=None):
            return pl.pallas_call(
                kernel, out_shape=out_shape, name=name, compiler_params=params, input_output_aliases=aliases or {},
                cost_estimate=pl.CostEstimate(flops=flops, bytes_accessed=bytes_accessed, transcendentals=0),
                grid_spec=pltpu.PrefetchScalarGridSpec(num_scalar_prefetch=1, grid=grid, in_specs=in_specs, out_specs=out_specs,
                                                       scratch_shapes=scratch))

        x_f32 = x_in.reshape(local_len, model_dim).astype(F32)
        flat_norm, norm_back = jax.vjp(input_norm, x_f32, norm_gain)
        grad_flat = grad_y.reshape(local_len, model_dim)
        half = ffn_dim // 2
        dma = pltpu.SemaphoreType.DMA
        chips = group_devices // 2
        ring_sems = lambda lanes: [dma((lanes, chips))] * 4
        struct = jax.ShapeDtypeStruct
        vmem = pltpu.VMEM
        in_vmem = pl.BlockSpec(memory_space=pltpu.VMEM)
        acts = (group_devices, local_len, half)
        blocks = (group_devices, local_len, model_dim)
        pos_rows = jnp.broadcast_to(positions.reshape(1, local_len), (8, local_len))
        n_all, dy_all, pos_all, hid, d_gate, d_up, mlp_out, d_norm_mlp = pl.pallas_call(
            functools.partial(gather_kernel, group_devices), name="gather_tokens",
            out_shape=[struct(blocks, BF16), struct(blocks, BF16), struct((group_devices, 8, local_len), jnp.int32)]
            + [struct(acts, BF16)] * 3 + [struct((local_len, model_dim), BF16), struct((local_len, model_dim), F32)],
            in_specs=[hbm] * 6, out_specs=[hbm] * 6 + [in_vmem] * 2,
            scratch_shapes=[vmem(blocks, BF16), vmem(blocks, BF16), vmem((group_devices, 8, local_len), jnp.int32),
                            vmem((model_dim, half), BF16), vmem((model_dim, half), BF16), vmem((half, model_dim), BF16)]
            + [vmem(acts, BF16)] * 3 + [vmem((2 * local_len, half), F32)] * 2 + [vmem((2, local_len, model_dim), F32)] * 2
            + [dma((3,)), dma((3,))] + ring_sems(3) + [dma((3, group_devices)), dma((3, group_devices)), dma(()), dma(())],
            compiler_params=pltpu.CompilerParams(collective_id=0, has_side_effects=True, vmem_limit_bytes=VMEM_LIMIT),
            cost_estimate=pl.CostEstimate(flops=40_000_000_000, bytes_accessed=40_000_000, transcendentals=0),
        )(flat_norm, grad_flat, pos_rows, w_gate, w_up, w_down)
        n_all, dy_all = n_all.reshape(seq_len, model_dim), dy_all.reshape(seq_len, model_dim)
        hid, d_gate, d_up = (act.reshape(seq_len, half) for act in (hid, d_gate, d_up))
        cos_t, sin_t = rope_lanes(pos_all[:, 0].reshape(seq_len), head_dim)

        vec = jax.ShapeDtypeStruct((1, head_dim), F32)
        rows_bf = jax.ShapeDtypeStruct((seq_len, head_dim), BF16)
        rows_f32 = jax.ShapeDtypeStruct((seq_len, head_dim), F32)
        rows = whole((seq_len, head_dim))
        head_cols = pl.BlockSpec((model_dim, head_dim), lambda g, s: (0, s[0]))
        kv_cols = pl.BlockSpec((model_dim, head_dim), lambda g, s: (0, s[1]))
        head_rows = pl.BlockSpec((head_dim, model_dim), lambda g, s: (s[0], 0))
        head_vec = pl.BlockSpec((1, 1, head_dim), lambda g, s: (s[0], 0, 0))
        kv_vec = pl.BlockSpec((1, 1, head_dim), lambda g, s: (s[1], 0, 0))
        tokens = whole((seq_len, model_dim))
        block = 512
        qn3 = q_norm.reshape(num_heads, 1, head_dim)
        kn3 = k_norm.reshape(num_kv, 1, head_dim)

        o_h, o32, lse, q_rot, k_rot, v_h, q_proj, k_proj = call(
            functools.partial(forward_kernel, block), "attention_fwd", 10_000_000_000, 12_000_000, (1,),
            [tokens, head_cols, kv_cols, kv_cols, head_vec, kv_vec, rows, rows], [rows] * 8,
            [rows_bf, rows_f32, rows_f32] + [rows_bf] * 5, [pltpu.VMEM((block, seq_len), F32)],
        )(idx, n_all, w_q, w_k, w_v, qn3, kn3, cos_t, sin_t)

        d_o, dwo_h = call(
            output_grad_kernel, "output_grad", 3_000_000_000, 6_000_000, (1,), [tokens, head_rows, rows], [rows, whole((head_dim, model_dim))],
            [rows_bf, jax.ShapeDtypeStruct((head_dim, model_dim), BF16)], [],
        )(idx, dy_all, w_o, o_h)

        dq_h, send, keep, gq = call(
            functools.partial(backward_kernel, block), "attention_bwd", 14_000_000_000, 8_000_000, (1,),
            [rows] * 7 + [head_vec, rows, rows], [rows] * 3 + [whole((1, head_dim))], [rows_bf] * 3 + [vec],
            [pltpu.VMEM((seq_len, head_dim), F32)] * 2,
        )(idx, d_o, o32, lse, q_rot, k_rot, v_h, q_proj, qn3, cos_t, sin_t)

        got = lax.ppermute(send, 'sp', pair_swap)
        d_rows, dwqkv_h, gk = call(
            projection_grad_kernel, "projection_grad", 4_000_000_000, 8_000_000, (1,),
            [tokens] + [rows] * 4 + [kv_vec, rows, rows],
            [whole((seq_len, 2 * head_dim)), whole((model_dim, 2 * head_dim)), whole((1, head_dim))],
            [jax.ShapeDtypeStruct((seq_len, 2 * head_dim), BF16), jax.ShapeDtypeStruct((model_dim, 2 * head_dim), BF16), vec],
            [],
        )(idx, n_all, dq_h, keep, got, k_proj, kn3, cos_t, sin_t)

        tile = 256
        tiles = half // tile
        tile_in = (tiles, model_dim, tile)
        dw_q, dw_k, dw_v, dw_o, dw_gate, dw_up, dw_down = pl.pallas_call(
            functools.partial(weight_kernel, group_devices), name="gather_weights",
            out_shape=[struct(w.shape, BF16) for w in (w_q, w_k, w_v, w_o, w_gate, w_up, w_down)],
            in_specs=[hbm] * 7, out_specs=[hbm] * 7,
            scratch_shapes=[vmem((group_devices, head_dim, model_dim), BF16), vmem((group_devices, model_dim, 2 * head_dim), BF16),
                            vmem((seq_len, model_dim), BF16), vmem((seq_len, model_dim), BF16), vmem((model_dim, seq_len), BF16)]
            + [vmem((2, seq_len, tile), BF16)] * 3 + [vmem(tile_in, BF16), vmem(tile_in, BF16), vmem((tiles, tile, model_dim), BF16)]
            + [dma((4,)), dma((3, 2))] + ring_sems(2) + [dma((2, group_devices)), dma((group_devices,))] + [dma((3, tiles))] * 3,
            compiler_params=pltpu.CompilerParams(collective_id=1, has_side_effects=True, vmem_limit_bytes=VMEM_LIMIT),
            cost_estimate=pl.CostEstimate(flops=60_000_000_000, bytes_accessed=60_000_000, transcendentals=0),
        )(dwo_h, dwqkv_h, n_all, dy_all, hid, d_gate, d_up)

        attn_flat = lax.all_to_all(o_h, 'sp', 0, 1, tiled=True)
        attn_out = jnp.dot(attn_flat, w_o, preferred_element_type=F32).astype(BF16)
        y_out = (x_f32 + attn_out.astype(F32) + mlp_out.astype(F32)).astype(BF16)

        d_rows = lax.all_to_all(d_rows, 'sp', 0, 1, tiled=True)
        d_rows = d_rows.reshape(local_len, num_kv, share, 2, head_dim)
        dq_flat = d_rows[:, :, :, 0].reshape(local_len, num_heads * head_dim)
        dk_flat = d_rows[:, :, 0, 1].reshape(local_len, num_kv * head_dim)
        dv_flat = d_rows[:, :, 1, 1].reshape(local_len, num_kv * head_dim)
        d_norm = (times_transposed(dq_flat, w_q) + times_transposed(dk_flat, w_k) + times_transposed(dv_flat, w_v) + d_norm_mlp).astype(BF16)
        dx_norm, grad_gain = norm_back(d_norm)
        grad_x = (grad_flat.astype(F32) + dx_norm).astype(BF16)

        gain_rows = model_dim // head_dim
        small = jnp.concatenate([grad_gain.reshape(gain_rows, head_dim), gq, gk], axis=0)
        small_all = spread(small)
        grad_gain = jnp.sum(small_all[:, :gain_rows], axis=0).reshape(model_dim)
        grad_q_norm = small_all[:, gain_rows]
        grad_k_norm = small_all[::share, gain_rows + 1]

        return (y_out.reshape(x_in.shape), grad_x.reshape(x_in.shape), dw_q, dw_k, dw_v, dw_o, dw_gate, dw_up, dw_down,
                grad_gain, grad_q_norm, grad_k_norm)

    in_specs = (seq_spec, seq_spec, P(('dp', 'sp'))) + (P(),) * 10
    out_specs = (seq_spec, seq_spec) + (grad_spec,) * 7 + (P('dp'), grad_spec, grad_spec)
    return jax.shard_map(layer_step, mesh=mesh, in_specs=in_specs, out_specs=out_specs, check_vma=False)
```

time: 306 us -> 307 us (level)
  Pallas kernels: 114 us -> 224 us
  waiting for transfers between devices: 60.9 us -> 9.24 us
  blocking collectives: 40.4 us -> 0 us
  matrix products: 32.2 us -> 9.22 us
  between operations: 14.2 us -> 0.9 us
  local copies, waits for them, and re-layouts: 20.9 us -> 31 us
  starting transfers between devices: 10.2 us -> 18.3 us
    pallas_call x4 -> x6, Pallas kernels: 114 us -> 224 us  [the longest x1 94 us: layer_step(): pl.pallas_call(functools.partial(weight_kernel, group_devices), name='gat...]
    all_gather x5 -> x0, waiting for transfers between devices: 52.5 us -> none  [the longest x1 38.4 us: layer_step(): dy_all = lax.all_gather(grad_flat, 'sp', axis=0, tiled=True)]
    all_gather x2 -> x0, blocking collectives: 40.4 us -> none  [the longest x1 22.8 us: layer_step(): all_pos = lax.all_gather(positions, 'sp', axis=0, tiled=True)]
    unnamed x48 -> x47, local copies, waits for them, and re-layouts: 8.03 us -> 23.6 us
    dot_general x3 -> x0, matrix products: 13.2 us -> none  [the longest x1 4.7 us: layer_step(): mlp_out = jnp.dot(hidden, w_down, preferred_element_type=F32).astype(BF16)]
    dot_general x6 -> x3, matrix products: 15.9 us -> 5.41 us  [times_transposed(): lax.dot_general(lhs_mat, rhs_mat, (((1,), (1,)), ((), ())), preferred_ele...]
    reshape x3 -> x0, local copies, waits for them, and re-layouts: 9.24 us -> none  [the longest x1 5.4 us: layer_step(): dw_q = dwq_all.transpose(1, 0, 2).reshape(model_dim, num_heads * head_dim)]
    all_to_all x1 -> x2, starting transfers between devices: 4.11 us -> 12.9 us  [the longest x1 8.94 us: layer_step(): d_rows = lax.all_to_all(d_rows, 'sp', 0, 1, tiled=True)]
  transfers between devices with their start and end apart: 11 -> 4, of which waited for: 3 -> 2; matrix products, arithmetic and copies ran while one was open for 16% -> 2% of each run, Pallas kernels for 25% -> 40%
where the time goes in v2:
time: 307 us; the launch traced here: 306 us
  Pallas kernels  224 us (73%)
  local copies, waits for them, and re-layouts  31 us (10%)
  starting transfers between devices  18.3 us (6%)
  other arithmetic  13.1 us (4%)
  waiting for transfers between devices  9.24 us (3%)
  matrix products  9.22 us (3%)
    pallas_call x1, Pallas kernels, layer_step(): pl.pallas_call(functools.partial(weight_kernel, group_devices), name='gat...  94 us
    pallas_call x1, Pallas kernels, layer_step(): pl.pallas_call(functools.partial(gather_kernel, group_devices), name='gat...  78.6 us
    unnamed x47, local copies, waits for them, and re-layouts  23.6 us
    pallas_call x1, Pallas kernels, layer_step(): call(functools.partial(forward_kernel, block), 'attention_fwd', 100000000...  22.5 us
    pallas_call x1, Pallas kernels, layer_step(): call(functools.partial(backward_kernel, block), 'attention_bwd', 14000000...  17.1 us
    all_to_all x1, starting transfers between devices, layer_step(): d_rows = lax.all_to_all(d_rows, 'sp', 0, 1, tiled=True)  8.94 us
    all_to_all x1, waiting for transfers between devices, spread(): return lax.all_to_all(copies, 'sp', 0, 0, tiled=True)  7.65 us
    pallas_call x1, Pallas kernels, layer_step(): call(projection_grad_kernel, 'projection_grad', 4000000000, 8000000, (1,)...  6.58 us
  transfers between devices with their start and end apart: 4, of which 2 were waited for; matrix products, arithmetic and copies ran while one was open for 2% of the time, Pallas kernels for 40%

profile of v2, /device:TPU:21, one launch (start us, length us, event | category | flops | bytes accessed | tf_op | source)
XLA Modules:
  0.0 306.3 jit_solution(16967626596504604672)
XLA Ops:
  2.9 1.9 fusion.17.n_ref
  6.1 78.6 %gather_tokens.1 = (bf16[16,128,1024]{2,1,0:T(8,128)(2,1)}, bf16[16,128,1024]{2,1,0:T(8,128)(2,1)}, s32[16,8,128]{2,1,0:T(8,128)}, bf16[16,128,1536]{2,1,0:T(8,1...) custom-call(bf16[128,1024]{1,0:T(8,128)(2,1)} %fusion.17.n_ref, ...), custom_call_target="tpu_custom_call" | custom-call | flops 40000000000 | bytes 40000000 | tf_op jit(solution)/shard_map/gather_tokens/pallas_call | solution.py:566
  86.1 5.5 %fusion.9 = (f32[2048,128]{1,0:T(8,128)}, f32[2048,128]{1,0:T(8,128)}) fusion(f32[128]{0:T(128)S(1)} %get-tuple-element.84, f32[128]{0:T(128)S(1)} %get-tuple-element.85, f32[2048]{0:T(1024)S(1)} %bitcast.87), kind=kLoop, calls=%fused_computation.13 | loop fusion | flops 524288 | bytes 2106368 | tf_op jit(solution)/shard_map/mul | solution.py:42
  91.6 22.5 %attention_fwd.1 = (bf16[2048,128]{1,0:T(8,128)(2,1)}, f32[2048,128]{1,0:T(8,128)}, f32[2048,128]{1,0:T(8,128)}, bf16[2048,128]{1,0:T(8,128)(2,1)}, bf16[2048,12...) custom-call(s32[3]{0:T(128)} %pad_add_fusion.idx_ref, ...), custom_call_target="tpu_custom_call" | custom-call | flops 10000000000 | bytes 12000000 | tf_op jit(solution)/shard_map/attention_fwd/pallas_call | solution.py:596
  114.1 2.0 copy.28
  116.2 5.1 %all-to-all-start = ((bf16[16,128,128]{1,2,0:T(8,128)(2,1)}), bf16[16,128,128]{1,2,0:T(8,128)(2,1)S(1)}, u32[]{:S(2)}, u32[]{:S(2)}) async-start(bf16[16,128,128]{1,2,0:T(8,128)(2,1)} %copy.28), calls=%async_computation | async-start | bytes 1048576 | tf_op jit(solution)/shard_map/all_to_all | solution.py:637
  121.2 5.7 %output_grad.1 = (bf16[2048,128]{1,0:T(8,128)(2,1)}, bf16[128,1024]{1,0:T(8,128)(2,1)}) custom-call(s32[3]{0:T(128)} %pad_add_fusion.idx_ref, bf16[2048,1024]{1,0:T(8,128)(2,1)} %bitcast.102, bf16[2048,1024]{1,0:T(8,128)(2,1)} %wo_ref.1, bf16[2048,128]{1,0:T(8,128)(2,1)} %get-tuple-element.46.o_ref), custom_call_target="tpu_custom_call" | custom-call | flops 3000000000 | bytes 6000000 | tf_op jit(solution)/shard_map/output_grad/pallas_call | solution.py:602
  126.9 17.1 %attention_bwd.1 = (bf16[2048,128]{1,0:T(8,128)(2,1)}, bf16[2048,128]{1,0:T(8,128)(2,1)}, bf16[2048,128]{1,0:T(8,128)(2,1)}, f32[1,128]{1,0:T(1,128)}) custom-call(s32[3]{0:T(128)} %pad_add_fusion.idx_ref, bf16[2048,128]{1,0:T(8,128)(2,1)} %get-tuple-element.49.do_ref, f32[2048,128]{1,0:T(8,128)} %get-tuple-element.50.o32_ref, ...), custom_call_target="tpu_custom_call" | custom-call | flops 14000000000 | bytes 8000000 | tf_op jit(solution)/shard_map/attention_bwd/pallas_call | solution.py:607
  144.4 1.6 collective-permute-done.got_ref
  146.7 6.6 %projection_grad.1 = (bf16[2048,256]{1,0:T(8,128)(2,1)}, bf16[1024,256]{1,0:T(8,128)(2,1)}, f32[1,128]{1,0:T(1,128)}) custom-call(s32[3]{0:T(128)} %pad_add_fusion.idx_ref, bf16[2048,1024]{1,0:T(8,128)(2,1)} %bitcast.100, bf16[2048,128]{1,0:T(8,128)(2,1)} %get-tuple-element.56.dq_ref, bf16[2048,128]{1,0:T(8,128)(2,1)} %get-tuple-element.57.keep_ref, ...), custom_call_target="tpu_custom_call" | custom-call | flops 4000000000 | bytes 8000000 | tf_op jit(solution)/shard_map/projection_grad/pallas_call | solution.py:614
  153.3 2.3 copy.29
  156.4 8.9 %all-to-all-start.1 = ((bf16[16,128,256]{1,2,0:T(8,128)(2,1)}), bf16[16,128,256]{1,2,0:T(8,128)(2,1)S(1)}, u32[]{:S(2)}, u32[]{:S(2)}) async-start(bf16[16,128,256]{1,2,0:T(8,128)(2,1)} %copy.29), calls=%async_computation.1 | async-start | bytes 2097152 | tf_op jit(solution)/shard_map/all_to_all | solution.py:641
  165.3 94.0 %gather_weights.1 = (bf16[1024,2048]{1,0:T(8,128)(2,1)}, bf16[1024,1024]{1,0:T(8,128)(2,1)}, bf16[1024,1024]{1,0:T(8,128)(2,1)}, bf16[2048,1024]{1,0:T(8,128)(2,...) custom-call(bf16[128,1024]{1,0:T(8,128)(2,1)} %get-tuple-element.62.dwo_ref, ...), custom_call_target="tpu_custom_call" | custom-call | flops 60000002048 | bytes 60000000 | tf_op jit(solution)/shard_map/gather_weights/pallas_call | solution.py:625
  259.4 3.8 %fusion.8 = bf16[1,128,1024]{2,1,0:T(8,128)(2,1)} fusion(bf16[128,2048]{0,1:T(8,128)(2,1)S(1)} %bitcast.81, bf16[2048,1024]{1,0:T(8,128)(2,1)} %wo_ref.1, bf16[1,128,1024]{2,1,0:T(8,128)(2,1)S(1)} %copy-done, bf16[128,1024]{1,0:T(8,128)(2,1)} %get-tuple-element.47), kind=kOutput, calls=%fused_computation.12 | convolution fusion | flops 537788416 | bytes 5505024 | tf_op jit(solution)/shard_map/dot_general | solution.py:638
  264.2 2.9 fusion.30
  267.1 1.7 fusion.20
  269.9 4.0 %all-to-all-start.2 = ((f32[16,10,128]{2,1,0:T(8,128)}), f32[16,10,128]{2,1,0:T(8,128)S(1)}, u32[]{:S(2)}, u32[]{:S(2)}) async-start(f32[16,10,128]{2,1,0:T(8,128)} %broadcast_in_dim.36), calls=%async_computation.2 | async-start | bytes 262144 | tf_op jit(solution)/shard_map/all_to_all | solution.py:532
  274.9 7.6 %all-to-all-done.2 = f32[16,10,128]{2,1,0:T(8,128)S(1)} async-done(((f32[16,10,128]{2,1,0:T(8,128)}), f32[16,10,128]{2,1,0:T(8,128)S(1)}, u32[]{:S(2)}, u32[]{:S(2)}) %all-to-all-start.2) | async-done | bytes 81952 | tf_op jit(solution)/shard_map/all_to_all | solution.py:532
  284.3 5.1 %copy.37 = bf16[1024,2048]{1,0:T(8,128)(2,1)} copy(bf16[1024,2048]{1,0:T(8,128)(2,1)} %get-tuple-element.100) | data formatting | bytes 8388608
  293.2 2.1 copy.40
  295.4 3.2 %copy.41 = bf16[1024,3072]{1,0:T(8,128)(2,1)} copy(bf16[1024,3072]{1,0:T(8,128)(2,1)S(1)} %bitcast.77) | data formatting | bytes 12582912
  298.6 1.3 slice-done.3
  300.0 2.9 copy.42
  303.6 2.7 copy.43
  (67 shorter events, 16.2 us)
Async XLA Ops:
  116.2 39.4 %all-to-all-start = ((bf16[16,128,128]{1,2,0:T(8,128)(2,1)}), bf16[16,128,128]{1,2,0:T(8,128)(2,1)S(1)}, u32[]{:S(2)}, u32[]{:S(2)}) async-start(bf16[16,128,128]{1,2,0:T(8,128)(2,1)} %copy.28), calls=%async_computation | async-start | bytes 1048576 | tf_op jit(solution)/shard_map/all_to_all | solution.py:637
  144.0 1.9 collective-permute-start
  146.0 0.8 copy-start.13
  155.6 0.8 copy-start.6
  156.4 106.8 %all-to-all-start.1 = ((bf16[16,128,256]{1,2,0:T(8,128)(2,1)}), bf16[16,128,256]{1,2,0:T(8,128)(2,1)S(1)}, u32[]{:S(2)}, u32[]{:S(2)}) async-start(bf16[16,128,256]{1,2,0:T(8,128)(2,1)} %copy.29), calls=%async_computation.1 | async-start | bytes 2097152 | tf_op jit(solution)/shard_map/all_to_all | solution.py:641
  165.3 94.0 %copy-start = (bf16[1,128,1024]{2,1,0:T(8,128)(2,1)S(1)}, bf16[1,128,1024]{2,1,0:T(8,128)(2,1)}, u32[]{:S(2)}) copy-start(bf16[1,128,1024]{2,1,0:T(8,128)(2,1)} %param.13) | copy-start | bytes 786436
  165.3 94.1 %copy-start.7 = (bf16[16,128,128]{1,2,0:T(8,128)(2,1)S(1)}, bf16[16,128,128]{1,2,0:T(8,128)(2,1)}, u32[]{:S(2)}) copy-start(bf16[16,128,128]{1,2,0:T(8,128)(2,1)} %copy-done.6) | copy-start | bytes 1572868
  259.4 4.0 %copy-start.3 = (bf16[1024,1024]{1,0:T(8,128)(2,1)S(1)}, bf16[1024,1024]{1,0:T(8,128)(2,1)}, u32[]{:S(2)}) copy-start(bf16[1024,1024]{1,0:T(8,128)(2,1)} %wv_ref.1) | copy-start | bytes 6291460
  263.2 3.9 %copy-start.10 = (f32[1024]{0:T(1024)S(1)}, f32[1024]{0:T(1024)}, u32[]{:S(2)}) copy-start(f32[1024]{0:T(1024)} %param.23) | copy-start | bytes 12292
  263.2 3.9 %copy-start.1 = (bf16[1024,2048]{1,0:T(8,128)(2,1)S(1)}, bf16[1024,2048]{1,0:T(8,128)(2,1)}, u32[]{:S(2)}) copy-start(bf16[1024,2048]{1,0:T(8,128)(2,1)} %wq_ref.1) | copy-start | bytes 12582916
  263.2 3.9 %copy-start.8 = (f32[128,1024]{1,0:T(8,128)S(1)}, f32[128,1024]{1,0:T(8,128)}, u32[]{:S(2)}) copy-start(f32[128,1024]{1,0:T(8,128)} %get-tuple-element.61) | copy-start | bytes 1572868
  267.1 2.1 copy-start.11
  267.1 2.1 copy-start.12
  267.1 6.8 %copy-start.9 = (bf16[1,128,1024]{2,1,0:T(8,128)(2,1)S(1)}, bf16[1,128,1024]{2,1,0:T(8,128)(2,1)}, u32[]{:S(2)}) copy-start(bf16[1,128,1024]{2,1,0:T(8,128)(2,1)} %param.14) | copy-start | bytes 786436
  269.9 12.6 %all-to-all-start.2 = ((f32[16,10,128]{2,1,0:T(8,128)}), f32[16,10,128]{2,1,0:T(8,128)S(1)}, u32[]{:S(2)}, u32[]{:S(2)}) async-start(f32[16,10,128]{2,1,0:T(8,128)} %broadcast_in_dim.36), calls=%async_computation.2 | async-start | bytes 262144 | tf_op jit(solution)/shard_map/all_to_all | solution.py:532
  284.3 5.1 %copy-start.5 = (bf16[1024,1024]{1,0:T(8,128)(2,1)S(1)}, bf16[1024,1024]{1,0:T(8,128)(2,1)}, u32[]{:S(2)}) copy-start(bf16[1024,1024]{1,0:T(8,128)(2,1)} %get-tuple-element.101) | copy-start | bytes 6291460
  284.3 6.4 %copy-start.4 = (bf16[1024,1024]{1,0:T(8,128)(2,1)S(1)}, bf16[1024,1024]{1,0:T(8,128)(2,1)}, u32[]{:S(2)}) copy-start(bf16[1024,1024]{1,0:T(8,128)(2,1)} %get-tuple-element.102) | copy-start | bytes 6291460
  284.3 11.1 %slice-start.4 = ((s8[6291456]{0:T(1024)(128)(4,1)}), s8[4194304]{0:T(1024)(128)(4,1)S(1)}, s32[]{:S(2)}) async-start(s8[6291456]{0:T(1024)(128)(4,1)} %bitcast.76), calls=%async_computation.7 | async-start | bytes 8388608
  289.4 3.9 %copy-start.2 = (bf16[2048,1024]{1,0:T(8,128)(2,1)S(1)}, bf16[2048,1024]{1,0:T(8,128)(2,1)}, u32[]{:S(2)}) copy-start(bf16[2048,1024]{1,0:T(8,128)(2,1)} %get-tuple-element.103) | copy-start | bytes 12582916
  290.7 4.7 %slice-start.5 = ((s8[6291456]{0:T(1024)(128)(4,1)}), s8[2097152]{0:T(1024)(128)(4,1)S(1)}, s32[]{:S(2)}) async-start(s8[6291456]{0:T(1024)(128)(4,1)} %bitcast.76), calls=%async_computation.8 | async-start | bytes 4194304
  293.2 5.4 %slice-start.2 = ((s8[6291456]{0:T(1024)(128)(4,1)}), s8[4194304]{0:T(1024)(128)(4,1)S(1)}, s32[]{:S(2)}) async-start(s8[6291456]{0:T(1024)(128)(4,1)} %bitcast.74), calls=%async_computation.5 | async-start | bytes 8388608
  295.4 4.6 %slice-start.3 = ((s8[6291456]{0:T(1024)(128)(4,1)}), s8[2097152]{0:T(1024)(128)(4,1)S(1)}, s32[]{:S(2)}) async-start(s8[6291456]{0:T(1024)(128)(4,1)} %bitcast.74), calls=%async_computation.6 | async-start | bytes 4194304
  295.4 7.5 %slice-start = ((s8[6291456]{0:T(1024)(128)(4,1)}), s8[4194304]{0:T(1024)(128)(4,1)S(1)}, s32[]{:S(2)}) async-start(s8[6291456]{0:T(1024)(128)(4,1)} %bitcast.72), calls=%async_computation.3 | async-start | bytes 8388608
  300.0 3.6 %slice-start.1 = ((s8[6291456]{0:T(1024)(128)(4,1)}), s8[2097152]{0:T(1024)(128)(4,1)S(1)}, s32[]{:S(2)}) async-start(s8[6291456]{0:T(1024)(128)(4,1)} %bitcast.72), calls=%async_computation.4 | async-start | bytes 4194304

commit v3 on v2

--- a/solution.py
+++ b/solution.py
@@ -266,7 +266,6 @@
         def _():
             self.forward(buf, sems, lane, step).start()
         self.share(buf, sems, lane, step).start()
-        self.shared(buf, sems, lane, step).wait_recv()
 
     def finish(self, buf, sems, lane):
         def body(step, carry):
@@ -280,7 +279,7 @@
 
 def gather_kernel(devices, n_ref, dy_ref, pos_ref, wg_ref, wu_ref, wd_ref,
                   n_out, dy_out, pos_out, hid_out, dg_out, du_out, mlp_out, dn_out,
-                  n_s, dy_s, pos_s, wg_s, wu_s, wd_s, hid_s, dg_s, du_s, gate_s, up_s, part_s, got_s,
+                  n_s, dy_s, pos_s, wg_s, wu_s, wd_s, hid_s, dg_s, du_s, gate_s, up_s, part_s, got_s, mine_s,
                   load_sem, weight_sem, ring_send, ring_recv, pair_send, pair_recv, out_sem, act_sem, swap_send, swap_recv):
     ring = Ring(devices)
     sems = (ring_send, ring_recv, pair_send, pair_recv)
@@ -307,33 +306,21 @@
     def put_act(i, slot):
         return pltpu.make_async_copy(acts[i][0].at[slot], acts[i][1].at[slot], act_sem.at[i, slot])
 
-    def step_body(step, carry):
+    def gate_up(step):
         mine, other = ring.own_slot(step), ring.other_slot(step)
-        ring.take(n_s, sems, 1, step)
-        ring.take(pos_s, sems, 0, step)
-
-        @pl.when(step == 0)
-        def _():
-            weights[0].wait()
-            weights[1].wait()
-
-        def gate_up(j, inner):
+
+        def body(j, inner):
             cols = pl.ds(pl.multiple_of(j * tile, tile), tile)
             n_rows = jnp.concatenate([n_s[mine], n_s[other]], axis=0)
             gate_s[:, cols] = jnp.dot(n_rows, wg_s[:, cols], preferred_element_type=F32)
             up_s[:, cols] = jnp.dot(n_rows, wu_s[:, cols], preferred_element_type=F32)
             return inner
-        lax.fori_loop(0, half // tile, gate_up, 0)
-        ring.take(dy_s, sems, 2, step)
-        for lane in range(3):
-            put(lane, mine).start()
-            put(lane, other).start()
-
-        @pl.when(step == 0)
-        def _():
-            weights[2].wait()
-
-        def hidden(j, inner):
+        lax.fori_loop(0, half // tile, body, 0)
+
+    def hidden(step):
+        mine, other = ring.own_slot(step), ring.other_slot(step)
+
+        def body(j, inner):
             cols = pl.ds(pl.multiple_of(j * tile, tile), tile)
             dy_rows = jnp.concatenate([dy_s[mine], dy_s[other]], axis=0)
             d_hidden = times_transposed(dy_rows, wd_s[cols, :]).astype(BF16).astype(F32)
@@ -348,30 +335,72 @@
                 buf[mine, :, cols] = value[:rows]
                 buf[other, :, cols] = value[rows:]
             return inner
-        lax.fori_loop(0, half // tile, hidden, 0)
+        lax.fori_loop(0, half // tile, body, 0)
+
+    def put_acts(step):
+        for i in range(3):
+            put_act(i, ring.own_slot(step)).start()
+            put_act(i, ring.other_slot(step)).start()
+
+    swap = pltpu.make_async_remote_copy(part_s, got_s, swap_send, swap_recv, device_id={'sp': ring.partner}, device_id_type=MESH)
+
+    def own_tokens(step):
+        for k, (slot, keep) in enumerate(((ring.partner, part_s), (ring.me, mine_s))):
+            @pl.when(step == 3 * k + 2)
+            def _():
+                keep[0] = jnp.dot(hid_s[slot], wd_s[...], preferred_element_type=F32)
+
+            @pl.when(step == 3 * k + 3)
+            def _():
+                keep[1] = times_transposed(dg_s[slot], wg_s[...])
+
+            @pl.when(step == 3 * k + 4)
+            def _():
+                keep[1] += times_transposed(du_s[slot], wu_s[...])
+
+        @pl.when(step == 5)
+        def _():
+            swap.start()
+
+    def step_body(step, carry):
+        ring.take(n_s, sems, 1, step)
+        ring.take(pos_s, sems, 0, step)
+
+        @pl.when(step == 1)
+        def _():
+            weights[0].wait()
+            weights[1].wait()
 
         @pl.when(step > 0)
         def _():
-            for i in range(3):
-                put_act(i, ring.own_slot(step - 1)).start()
-                put_act(i, ring.other_slot(step - 1)).start()
+            gate_up(step - 1)
+        ring.take(dy_s, sems, 2, step)
+
+        @pl.when(step == 1)
+        def _():
+            weights[2].wait()
+
+        @pl.when(step > 0)
+        def _():
+            hidden(step - 1)
+
+        @pl.when(step > 1)
+        def _():
+            put_acts(step - 2)
+        own_tokens(step)
+        for lane in range(3):
+            ring.shared(lanes[lane][0], sems, lane, step).wait_recv()
+            put(lane, ring.own_slot(step)).start()
+            put(lane, ring.other_slot(step)).start()
         return carry
 
     lax.fori_loop(0, ring.chips, step_body, 0)
     last = ring.chips - 1
-    for i in range(3):
-        put_act(i, ring.own_slot(last)).start()
-        put_act(i, ring.other_slot(last)).start()
-
-    def partial(slot):
-        return (jnp.dot(hid_s[slot], wd_s[...], preferred_element_type=F32),
-                times_transposed(dg_s[slot], wg_s[...]) + times_transposed(du_s[slot], wu_s[...]))
-
-    part_s[0], part_s[1] = partial(ring.partner)
-    mine_m, mine_n = partial(ring.me)
-    dn_out[...] = mine_n
-    swap = pltpu.make_async_remote_copy(part_s, got_s, swap_send, swap_recv, device_id={'sp': ring.partner}, device_id_type=MESH)
-    swap.start()
+    gate_up(last)
+    put_acts(last - 1)
+    hidden(last)
+    own_tokens(last + 1)
+    put_acts(last)
     for lane in range(3):
         ring.finish(lanes[lane][0], sems, lane)
 
@@ -382,8 +411,8 @@
         return carry
     lax.fori_loop(0, devices, drain, 0)
     swap.wait()
-    mlp_out[...] = (mine_m + got_s[0]).astype(BF16)
-    dn_out[...] += got_s[1]
+    mlp_out[...] = (mine_s[0] + got_s[0]).astype(BF16)
+    dn_out[...] = mine_s[1] + got_s[1]
 
 
 def weight_kernel(devices, dwo_ref, dwqkv_ref, n_ref, dy_ref, hid_ref, dg_ref, du_ref,
@@ -475,6 +504,13 @@
             lax.fori_loop(0, 4, in_weights, 0)
 
         ring.take(wqkv_s, sems, 1, step)
+
+        @pl.when(step < tiles)
+        def _():
+            st_d[step] = transposed_times(hid_s[step % 2], dy_s[...]).astype(BF16)
+
+        ring.shared(wo_s, sems, 0, step).wait_recv()
+        ring.shared(wqkv_s, sems, 1, step).wait_recv()
         for slot in (ring.own_slot(step), ring.other_slot(step)):
             put_o(slot).start()
             put_q(slot).start()
@@ -486,10 +522,6 @@
             @pl.when(slot % 2 == 1)
             def _():
                 put_kv(slot, v_out).start()
-
-        @pl.when(step < tiles)
-        def _():
-            st_d[step] = transposed_times(hid_s[step % 2], dy_s[...]).astype(BF16)
 
         @pl.when(jnp.logical_and(step > 0, step <= tiles))
         def _():
@@ -570,7 +602,7 @@
             in_specs=[hbm] * 6, out_specs=[hbm] * 6 + [in_vmem] * 2,
             scratch_shapes=[vmem(blocks, BF16), vmem(blocks, BF16), vmem((group_devices, 8, local_len), jnp.int32),
                             vmem((model_dim, half), BF16), vmem((model_dim, half), BF16), vmem((half, model_dim), BF16)]
-            + [vmem(acts, BF16)] * 3 + [vmem((2 * local_len, half), F32)] * 2 + [vmem((2, local_len, model_dim), F32)] * 2
+            + [vmem(acts, BF16)] * 3 + [vmem((2 * local_len, half), F32)] * 2 + [vmem((2, local_len, model_dim), F32)] * 3
             + [dma((3,)), dma((3,))] + ring_sems(3) + [dma((3, group_devices)), dma((3, group_devices)), dma(()), dma(())],
             compiler_params=pltpu.CompilerParams(collective_id=0, has_side_effects=True, vmem_limit_bytes=VMEM_LIMIT),
             cost_estimate=pl.CostEstimate(flops=40_000_000_000, bytes_accessed=40_000_000, transcendentals=0),

time: 307 us -> 288 us (0.938)
  Pallas kernels: 224 us -> 205 us
    pallas_call x1, Pallas kernels: 78.6 us -> 62.1 us  [layer_step(): pl.pallas_call(functools.partial(gather_kernel, group_devices), name='gat...]
  transfers between devices with their start and end apart: 4 -> 4, of which waited for: 2 -> 2; matrix products, arithmetic and copies ran while one was open for 2% -> 2% of each run, Pallas kernels for 40% -> 42%
where the time goes in v3:
time: 288 us; the launch traced here: 287 us
  Pallas kernels  205 us (71%)
  local copies, waits for them, and re-layouts  31 us (11%)
  starting transfers between devices  19 us (7%)
  other arithmetic  13.1 us (5%)
  matrix products  9.23 us (3%)
  waiting for transfers between devices  9.22 us (3%)
    pallas_call x1, Pallas kernels, layer_step(): pl.pallas_call(functools.partial(weight_kernel, group_devices), name='gat...  90.9 us
    pallas_call x1, Pallas kernels, layer_step(): pl.pallas_call(functools.partial(gather_kernel, group_devices), name='gat...  62.1 us
    unnamed x47, local copies, waits for them, and re-layouts  23.6 us
    pallas_call x1, Pallas kernels, layer_step(): call(functools.partial(forward_kernel, block), 'attention_fwd', 100000000...  22.5 us
    pallas_call x1, Pallas kernels, layer_step(): call(functools.partial(backward_kernel, block), 'attention_bwd', 14000000...  17.1 us
    all_to_all x1, starting transfers between devices, layer_step(): d_rows = lax.all_to_all(d_rows, 'sp', 0, 1, tiled=True)  8.94 us
    all_to_all x1, waiting for transfers between devices, spread(): return lax.all_to_all(copies, 'sp', 0, 0, tiled=True)  7.65 us
    pallas_call x1, Pallas kernels, layer_step(): call(projection_grad_kernel, 'projection_grad', 4000000000, 8000000, (1,)...  6.58 us
  transfers between devices with their start and end apart: 4, of which 2 were waited for; matrix products, arithmetic and copies ran while one was open for 2% of the time, Pallas kernels for 42%

profile of v3, /device:TPU:21, one launch (start us, length us, event | category | flops | bytes accessed | tf_op | source)
XLA Modules:
  0.0 287.4 jit_solution(5767356132854740148)
XLA Ops:
  2.9 1.9 fusion.17.n_ref
  6.1 62.1 %gather_tokens.1 = (bf16[16,128,1024]{2,1,0:T(8,128)(2,1)}, bf16[16,128,1024]{2,1,0:T(8,128)(2,1)}, s32[16,8,128]{2,1,0:T(8,128)}, bf16[16,128,1536]{2,1,0:T(8,1...) custom-call(bf16[128,1024]{1,0:T(8,128)(2,1)} %fusion.17.n_ref, ...), custom_call_target="tpu_custom_call" | custom-call | flops 40000000000 | bytes 40000000 | tf_op jit(solution)/shard_map/gather_tokens/pallas_call | solution.py:598
  69.6 5.5 %fusion.9 = (f32[2048,128]{1,0:T(8,128)}, f32[2048,128]{1,0:T(8,128)}) fusion(f32[128]{0:T(128)S(1)} %get-tuple-element.84, f32[128]{0:T(128)S(1)} %get-tuple-element.85, f32[2048]{0:T(1024)S(1)} %bitcast.87), kind=kLoop, calls=%fused_computation.13 | loop fusion | flops 524288 | bytes 2106368 | tf_op jit(solution)/shard_map/mul | solution.py:42
  75.1 22.5 %attention_fwd.1 = (bf16[2048,128]{1,0:T(8,128)(2,1)}, f32[2048,128]{1,0:T(8,128)}, f32[2048,128]{1,0:T(8,128)}, bf16[2048,128]{1,0:T(8,128)(2,1)}, bf16[2048,12...) custom-call(s32[3]{0:T(128)} %pad_add_fusion.idx_ref, ...), custom_call_target="tpu_custom_call" | custom-call | flops 10000000000 | bytes 12000000 | tf_op jit(solution)/shard_map/attention_fwd/pallas_call | solution.py:628
  97.6 2.0 copy.28
  99.6 5.8 %all-to-all-start = ((bf16[16,128,128]{1,2,0:T(8,128)(2,1)}), bf16[16,128,128]{1,2,0:T(8,128)(2,1)S(1)}, u32[]{:S(2)}, u32[]{:S(2)}) async-start(bf16[16,128,128]{1,2,0:T(8,128)(2,1)} %copy.28), calls=%async_computation | async-start | bytes 1048576 | tf_op jit(solution)/shard_map/all_to_all | solution.py:669
  105.4 5.7 %output_grad.1 = (bf16[2048,128]{1,0:T(8,128)(2,1)}, bf16[128,1024]{1,0:T(8,128)(2,1)}) custom-call(s32[3]{0:T(128)} %pad_add_fusion.idx_ref, bf16[2048,1024]{1,0:T(8,128)(2,1)} %bitcast.102, bf16[2048,1024]{1,0:T(8,128)(2,1)} %wo_ref.1, bf16[2048,128]{1,0:T(8,128)(2,1)} %get-tuple-element.46.o_ref), custom_call_target="tpu_custom_call" | custom-call | flops 3000000000 | bytes 6000000 | tf_op jit(solution)/shard_map/output_grad/pallas_call | solution.py:634
  111.1 17.1 %attention_bwd.1 = (bf16[2048,128]{1,0:T(8,128)(2,1)}, bf16[2048,128]{1,0:T(8,128)(2,1)}, bf16[2048,128]{1,0:T(8,128)(2,1)}, f32[1,128]{1,0:T(1,128)}) custom-call(s32[3]{0:T(128)} %pad_add_fusion.idx_ref, bf16[2048,128]{1,0:T(8,128)(2,1)} %get-tuple-element.49.do_ref, f32[2048,128]{1,0:T(8,128)} %get-tuple-element.50.o32_ref, ...), custom_call_target="tpu_custom_call" | custom-call | flops 14000000000 | bytes 8000000 | tf_op jit(solution)/shard_map/attention_bwd/pallas_call | solution.py:639
  128.6 1.6 collective-permute-done.got_ref
  130.9 6.6 %projection_grad.1 = (bf16[2048,256]{1,0:T(8,128)(2,1)}, bf16[1024,256]{1,0:T(8,128)(2,1)}, f32[1,128]{1,0:T(1,128)}) custom-call(s32[3]{0:T(128)} %pad_add_fusion.idx_ref, bf16[2048,1024]{1,0:T(8,128)(2,1)} %bitcast.100, bf16[2048,128]{1,0:T(8,128)(2,1)} %get-tuple-element.56.dq_ref, bf16[2048,128]{1,0:T(8,128)(2,1)} %get-tuple-element.57.keep_ref, ...), custom_call_target="tpu_custom_call" | custom-call | flops 4000000000 | bytes 8000000 | tf_op jit(solution)/shard_map/projection_grad/pallas_call | solution.py:646
  137.5 2.3 copy.29
  140.6 8.9 %all-to-all-start.1 = ((bf16[16,128,256]{1,2,0:T(8,128)(2,1)}), bf16[16,128,256]{1,2,0:T(8,128)(2,1)S(1)}, u32[]{:S(2)}, u32[]{:S(2)}) async-start(bf16[16,128,256]{1,2,0:T(8,128)(2,1)} %copy.29), calls=%async_computation.1 | async-start | bytes 2097152 | tf_op jit(solution)/shard_map/all_to_all | solution.py:673
  149.5 90.9 %gather_weights.1 = (bf16[1024,2048]{1,0:T(8,128)(2,1)}, bf16[1024,1024]{1,0:T(8,128)(2,1)}, bf16[1024,1024]{1,0:T(8,128)(2,1)}, bf16[2048,1024]{1,0:T(8,128)(2,...) custom-call(bf16[128,1024]{1,0:T(8,128)(2,1)} %get-tuple-element.62.dwo_ref, ...), custom_call_target="tpu_custom_call" | custom-call | flops 60000002048 | bytes 60000000 | tf_op jit(solution)/shard_map/gather_weights/pallas_call | solution.py:657
  240.5 3.8 %fusion.8 = bf16[1,128,1024]{2,1,0:T(8,128)(2,1)} fusion(bf16[128,2048]{0,1:T(8,128)(2,1)S(1)} %bitcast.81, bf16[2048,1024]{1,0:T(8,128)(2,1)} %wo_ref.1, bf16[1,128,1024]{2,1,0:T(8,128)(2,1)S(1)} %copy-done, bf16[128,1024]{1,0:T(8,128)(2,1)} %get-tuple-element.47), kind=kOutput, calls=%fused_computation.12 | convolution fusion | flops 537788416 | bytes 5505024 | tf_op jit(solution)/shard_map/dot_general | solution.py:670
  245.3 2.9 %fusion.30 = f32[128,1024]{1,0:T(8,128)S(1)} fusion(bf16[128,1024]{0,1:T(8,128)(2,1)S(1)} %bitcast.83, bf16[1024,1024]{1,0:T(8,128)(2,1)} %wk_ref.1), kind=kOutput, calls=%fused_computation.52 | convolution fusion | flops 268435456 | bytes 2883584 | tf_op jit(solution)/shard_map/dot_general | solution.py:30
  248.3 1.7 fusion.20
  251.0 3.9 %all-to-all-start.2 = ((f32[16,10,128]{2,1,0:T(8,128)}), f32[16,10,128]{2,1,0:T(8,128)S(1)}, u32[]{:S(2)}, u32[]{:S(2)}) async-start(f32[16,10,128]{2,1,0:T(8,128)} %broadcast_in_dim.36), calls=%async_computation.2 | async-start | bytes 262144 | tf_op jit(solution)/shard_map/all_to_all | solution.py:564
  256.0 7.6 %all-to-all-done.2 = f32[16,10,128]{2,1,0:T(8,128)S(1)} async-done(((f32[16,10,128]{2,1,0:T(8,128)}), f32[16,10,128]{2,1,0:T(8,128)S(1)}, u32[]{:S(2)}, u32[]{:S(2)}) %all-to-all-start.2) | async-done | bytes 81952 | tf_op jit(solution)/shard_map/all_to_all | solution.py:564
  265.4 5.1 %copy.37 = bf16[1024,2048]{1,0:T(8,128)(2,1)} copy(bf16[1024,2048]{1,0:T(8,128)(2,1)} %get-tuple-element.100) | data formatting | bytes 8388608
  274.4 2.1 copy.40
  276.5 3.2 %copy.41 = bf16[1024,3072]{1,0:T(8,128)(2,1)} copy(bf16[1024,3072]{1,0:T(8,128)(2,1)S(1)} %bitcast.77) | data formatting | bytes 12582912
  279.7 1.3 slice-done.3
  281.1 2.9 %copy.42 = bf16[1024,3072]{1,0:T(8,128)(2,1)} copy(bf16[1024,3072]{1,0:T(8,128)(2,1)S(1)} %bitcast.75) | data formatting | bytes 12582912
  284.7 2.7 copy.43
  (67 shorter events, 16.2 us)
Async XLA Ops:
  99.6 40.2 %all-to-all-start = ((bf16[16,128,128]{1,2,0:T(8,128)(2,1)}), bf16[16,128,128]{1,2,0:T(8,128)(2,1)S(1)}, u32[]{:S(2)}, u32[]{:S(2)}) async-start(bf16[16,128,128]{1,2,0:T(8,128)(2,1)} %copy.28), calls=%async_computation | async-start | bytes 1048576 | tf_op jit(solution)/shard_map/all_to_all | solution.py:669
  128.2 1.9 collective-permute-start
  130.1 0.8 copy-start.13
  139.8 0.8 copy-start.6
  140.6 103.8 %all-to-all-start.1 = ((bf16[16,128,256]{1,2,0:T(8,128)(2,1)}), bf16[16,128,256]{1,2,0:T(8,128)(2,1)S(1)}, u32[]{:S(2)}, u32[]{:S(2)}) async-start(bf16[16,128,256]{1,2,0:T(8,128)(2,1)} %copy.29), calls=%async_computation.1 | async-start | bytes 2097152 | tf_op jit(solution)/shard_map/all_to_all | solution.py:673
  149.5 91.0 %copy-start = (bf16[1,128,1024]{2,1,0:T(8,128)(2,1)S(1)}, bf16[1,128,1024]{2,1,0:T(8,128)(2,1)}, u32[]{:S(2)}) copy-start(bf16[1,128,1024]{2,1,0:T(8,128)(2,1)} %param.13) | copy-start | bytes 786436
  149.5 91.0 %copy-start.7 = (bf16[16,128,128]{1,2,0:T(8,128)(2,1)S(1)}, bf16[16,128,128]{1,2,0:T(8,128)(2,1)}, u32[]{:S(2)}) copy-start(bf16[16,128,128]{1,2,0:T(8,128)(2,1)} %copy-done.6) | copy-start | bytes 1572868
  240.5 4.0 %copy-start.3 = (bf16[1024,1024]{1,0:T(8,128)(2,1)S(1)}, bf16[1024,1024]{1,0:T(8,128)(2,1)}, u32[]{:S(2)}) copy-start(bf16[1024,1024]{1,0:T(8,128)(2,1)} %wv_ref.1) | copy-start | bytes 6291460
  244.3 3.9 %copy-start.10 = (f32[1024]{0:T(1024)S(1)}, f32[1024]{0:T(1024)}, u32[]{:S(2)}) copy-start(f32[1024]{0:T(1024)} %param.23) | copy-start | bytes 12292
  244.3 3.9 %copy-start.1 = (bf16[1024,2048]{1,0:T(8,128)(2,1)S(1)}, bf16[1024,2048]{1,0:T(8,128)(2,1)}, u32[]{:S(2)}) copy-start(bf16[1024,2048]{1,0:T(8,128)(2,1)} %wq_ref.1) | copy-start | bytes 12582916
  244.3 3.9 %copy-start.8 = (f32[128,1024]{1,0:T(8,128)S(1)}, f32[128,1024]{1,0:T(8,128)}, u32[]{:S(2)}) copy-start(f32[128,1024]{1,0:T(8,128)} %get-tuple-element.61) | copy-start | bytes 1572868
  248.2 2.1 copy-start.11
  248.2 2.1 copy-start.12
  248.2 6.7 %copy-start.9 = (bf16[1,128,1024]{2,1,0:T(8,128)(2,1)S(1)}, bf16[1,128,1024]{2,1,0:T(8,128)(2,1)}, u32[]{:S(2)}) copy-start(bf16[1,128,1024]{2,1,0:T(8,128)(2,1)} %param.14) | copy-start | bytes 786436
  251.0 12.6 %all-to-all-start.2 = ((f32[16,10,128]{2,1,0:T(8,128)}), f32[16,10,128]{2,1,0:T(8,128)S(1)}, u32[]{:S(2)}, u32[]{:S(2)}) async-start(f32[16,10,128]{2,1,0:T(8,128)} %broadcast_in_dim.36), calls=%async_computation.2 | async-start | bytes 262144 | tf_op jit(solution)/shard_map/all_to_all | solution.py:564
  265.4 5.1 %copy-start.5 = (bf16[1024,1024]{1,0:T(8,128)(2,1)S(1)}, bf16[1024,1024]{1,0:T(8,128)(2,1)}, u32[]{:S(2)}) copy-start(bf16[1024,1024]{1,0:T(8,128)(2,1)} %get-tuple-element.101) | copy-start | bytes 6291460
  265.4 6.4 %copy-start.4 = (bf16[1024,1024]{1,0:T(8,128)(2,1)S(1)}, bf16[1024,1024]{1,0:T(8,128)(2,1)}, u32[]{:S(2)}) copy-start(bf16[1024,1024]{1,0:T(8,128)(2,1)} %get-tuple-element.102) | copy-start | bytes 6291460
  265.4 11.1 %slice-start.4 = ((s8[6291456]{0:T(1024)(128)(4,1)}), s8[4194304]{0:T(1024)(128)(4,1)S(1)}, s32[]{:S(2)}) async-start(s8[6291456]{0:T(1024)(128)(4,1)} %bitcast.76), calls=%async_computation.7 | async-start | bytes 8388608
  270.5 3.9 %copy-start.2 = (bf16[2048,1024]{1,0:T(8,128)(2,1)S(1)}, bf16[2048,1024]{1,0:T(8,128)(2,1)}, u32[]{:S(2)}) copy-start(bf16[2048,1024]{1,0:T(8,128)(2,1)} %get-tuple-element.103) | copy-start | bytes 12582916
  271.8 4.7 %slice-start.5 = ((s8[6291456]{0:T(1024)(128)(4,1)}), s8[2097152]{0:T(1024)(128)(4,1)S(1)}, s32[]{:S(2)}) async-start(s8[6291456]{0:T(1024)(128)(4,1)} %bitcast.76), calls=%async_computation.8 | async-start | bytes 4194304
  274.3 5.4 %slice-start.2 = ((s8[6291456]{0:T(1024)(128)(4,1)}), s8[4194304]{0:T(1024)(128)(4,1)S(1)}, s32[]{:S(2)}) async-start(s8[6291456]{0:T(1024)(128)(4,1)} %bitcast.74), calls=%async_computation.5 | async-start | bytes 8388608
  276.5 4.6 %slice-start.3 = ((s8[6291456]{0:T(1024)(128)(4,1)}), s8[2097152]{0:T(1024)(128)(4,1)S(1)}, s32[]{:S(2)}) async-start(s8[6291456]{0:T(1024)(128)(4,1)} %bitcast.74), calls=%async_computation.6 | async-start | bytes 4194304
  276.5 7.5 %slice-start = ((s8[6291456]{0:T(1024)(128)(4,1)}), s8[4194304]{0:T(1024)(128)(4,1)S(1)}, s32[]{:S(2)}) async-start(s8[6291456]{0:T(1024)(128)(4,1)} %bitcast.72), calls=%async_computation.3 | async-start | bytes 8388608
  281.1 3.6 %slice-start.1 = ((s8[6291456]{0:T(1024)(128)(4,1)}), s8[2097152]{0:T(1024)(128)(4,1)S(1)}, s32[]{:S(2)}) async-start(s8[6291456]{0:T(1024)(128)(4,1)} %bitcast.72), calls=%async_computation.4 | async-start | bytes 4194304

commit v4 on v3

--- a/solution.py
+++ b/solution.py
@@ -9,7 +9,7 @@
 
 NORM_EPS = 1e-5
 ROPE_THETA = 75.0e6
-VMEM_LIMIT = 60 * 1024 * 1024
+VMEM_LIMIT = 63 * 1024 * 1024
 F32 = jnp.float32
 BF16 = jnp.bfloat16
 MESH = pl.DeviceIdType.MESH
@@ -136,82 +136,6 @@
     lax.fori_loop(0, steps, query_block, 0)
 
 
-def output_grad_kernel(idx_ref, dy_s, wo_ref, o_ref, do_ref, dwo_ref):
-    dwo_ref[...] = transposed_times(o_ref[...], dy_s[...]).astype(BF16)
-    do_ref[...] = times_transposed(dy_s[...], wo_ref[...]).astype(BF16)
-
-
-def backward_kernel(block, idx_ref, do_ref, o32_ref, lse_ref, q_ref, k_ref, v_ref, qproj_ref, qn_ref, cos_ref, sin_ref,
-                    dq_ref, send_ref, keep_ref, gq_ref, dk_s, dv_s):
-    seq_len, head_dim = do_ref.shape
-    steps = seq_len // block
-    scale = head_dim ** -0.5
-    causal = lax.broadcasted_iota(jnp.int32, (block, block), 0) >= lax.broadcasted_iota(jnp.int32, (block, block), 1)
-    dk_s[...] = jnp.zeros_like(dk_s)
-    dv_s[...] = jnp.zeros_like(dv_s)
-    gq_ref[...] = jnp.zeros_like(gq_ref)
-
-    def query_block(i, carry):
-        rows = pl.ds(pl.multiple_of(i * block, block), block)
-        q_rows, do_rows = q_ref[rows, :], do_ref[rows, :]
-        delta = jnp.sum(o32_ref[rows, :] * do_rows.astype(F32), axis=-1, keepdims=True)
-        lse = lse_ref[rows, :][:, :1]
-
-        def tile_back(keys, masked):
-            k_rows, v_rows = k_ref[keys, :], v_ref[keys, :]
-            probs = jnp.exp(times_transposed(q_rows, k_rows) * scale - lse)
-            if masked:
-                probs = jnp.where(causal, probs, 0.0)
-            d_probs = times_transposed(do_rows, v_rows).astype(BF16).astype(F32)
-            d_score = (probs * (d_probs - delta) * scale).astype(BF16)
-            dv_s[keys, :] += transposed_times(probs.astype(BF16), do_rows)
-            dk_s[keys, :] += transposed_times(d_score, q_rows)
-            return jnp.dot(d_score, k_rows, preferred_element_type=F32)
-
-        def back(j, acc):
-            return acc + tile_back(pl.ds(pl.multiple_of(j * block, block), block), False)
-
-        dq = lax.fori_loop(0, i, back, tile_back(rows, True)).astype(BF16).astype(F32)
-        dq_proj, d_weight = head_backward(dq, qproj_ref[rows, :].astype(F32), qn_ref[0], cos_ref[rows, :], sin_ref[rows, :])
-        dq_ref[rows, :] = dq_proj.astype(BF16)
-        gq_ref[...] += d_weight
-        return carry
-
-    lax.fori_loop(0, steps, query_block, 0)
-    first = idx_ref[2] == 0
-
-    @pl.when(first)
-    def _():
-        keep_ref[...] = dk_s[...].astype(BF16)
-        send_ref[...] = dv_s[...].astype(BF16)
-
-    @pl.when(jnp.logical_not(first))
-    def _():
-        keep_ref[...] = dv_s[...].astype(BF16)
-        send_ref[...] = dk_s[...].astype(BF16)
-
-
-def projection_grad_kernel(idx_ref, n_s, dq_ref, keep_ref, got_ref, kproj_ref, kn_ref, cos_ref, sin_ref,
-                           rows_ref, dw_ref, gk_ref):
-    head_dim = dq_ref.shape[1]
-    total = (keep_ref[...].astype(F32) + got_ref[...].astype(F32)).astype(BF16)
-    rows_ref[:, :head_dim] = dq_ref[...]
-    first = idx_ref[2] == 0
-
-    @pl.when(first)
-    def _():
-        dk_proj, d_weight = head_backward(total.astype(F32), kproj_ref[...].astype(F32), kn_ref[0], cos_ref[...], sin_ref[...])
-        rows_ref[:, head_dim:] = dk_proj.astype(BF16)
-        gk_ref[...] = d_weight
-
-    @pl.when(jnp.logical_not(first))
-    def _():
-        rows_ref[:, head_dim:] = total
-        gk_ref[...] = jnp.zeros_like(gk_ref)
-
-    dw_ref[...] = transposed_times(n_s[...], rows_ref[...]).astype(BF16)
-
-
 class Ring:
     def __init__(self, devices):
         self.chips = devices // 2
@@ -237,6 +161,22 @@
             pl.semaphore_signal(sem, inc=1, device_id={'sp': device}, device_id_type=MESH)
         pl.semaphore_wait(sem, 3)
 
+    def barrier_all(self):
+        sem = pltpu.get_barrier_semaphore()
+
+        def signal(hop, carry):
+            pl.semaphore_signal(sem, inc=1, device_id={'sp': self.peer(hop)}, device_id_type=MESH)
+            return carry
+        lax.fori_loop(1, 2 * self.chips, signal, 0)
+        pl.semaphore_wait(sem, 2 * self.chips - 1)
+
+    def peer(self, hop):
+        return lax.rem(self.me + hop, 2 * self.chips)
+
+    def direct(self, src, dst, send, recv, hop):
+        return pltpu.make_async_remote_copy(src, dst, send.at[hop], recv.at[hop],
+                                            device_id={'sp': self.peer(hop)}, device_id_type=MESH)
+
     def forward(self, buf, sems, lane, step):
         slot = buf.at[self.own_slot(step)]
         return pltpu.make_async_remote_copy(slot, slot, sems[0].at[lane, step], sems[1].at[lane, step + 1],
@@ -277,21 +217,22 @@
         lax.fori_loop(0, self.chips, body, 0)
 
 
-def gather_kernel(devices, n_ref, dy_ref, pos_ref, wg_ref, wu_ref, wd_ref,
+def gather_kernel(devices, x_ref, gain_ref, dy_ref, pos_ref, wg_ref, wu_ref, wd_ref,
                   n_out, dy_out, pos_out, hid_out, dg_out, du_out, mlp_out, dn_out,
                   n_s, dy_s, pos_s, wg_s, wu_s, wd_s, hid_s, dg_s, du_s, gate_s, up_s, part_s, got_s, mine_s,
                   load_sem, weight_sem, ring_send, ring_recv, pair_send, pair_recv, out_sem, act_sem, swap_send, swap_recv):
     ring = Ring(devices)
     sems = (ring_send, ring_recv, pair_send, pair_recv)
     half = wg_s.shape[1]
-    lanes = ((pos_s, pos_ref, pos_out), (n_s, n_ref, n_out), (dy_s, dy_ref, dy_out))
-    loads = [pltpu.make_async_copy(src, buf.at[ring.me], load_sem.at[i]) for i, (buf, src, _) in enumerate(lanes)]
+    lanes = ((pos_s, pos_ref, pos_out), (n_s, None, n_out), (dy_s, dy_ref, dy_out))
+    loads = [pltpu.make_async_copy(src, buf.at[ring.me], load_sem.at[i]) for i, (buf, src, _) in enumerate(lanes) if src is not None]
     columns = pl.ds(pl.multiple_of(ring.core * half, half), half)
     weights = [pltpu.make_async_copy(wg_ref.at[:, columns], wg_s, weight_sem.at[0]),
                pltpu.make_async_copy(wu_ref.at[:, columns], wu_s, weight_sem.at[1]),
                pltpu.make_async_copy(wd_ref.at[columns, :], wd_s, weight_sem.at[2])]
     for copy in loads + weights:
         copy.start()
+    n_s[ring.me] = input_norm(x_ref[...].astype(F32), gain_ref[...])
     ring.barrier()
     for copy in loads:
         copy.wait()
@@ -415,21 +356,132 @@
     dn_out[...] = mine_s[1] + got_s[1]
 
 
-def weight_kernel(devices, dwo_ref, dwqkv_ref, n_ref, dy_ref, hid_ref, dg_ref, du_ref,
-                  q_out, k_out, v_out, o_out, g_out, u_out, d_out,
-                  wo_s, wqkv_s, n_s, dy_s, nt_s, hid_s, dg_s, du_s, st_g, st_u, st_d,
-                  load_sem, tile_sem, ring_send, ring_recv, pair_send, pair_recv, out_sem, kv_sem,
-                  put_sem, swap_send, swap_recv):
+def backward_kernel(devices, block, dy_ref, n_ref, wo_ref, o_ref, o32_ref, lse_ref, q_ref, k_ref, v_ref, qproj_ref, kproj_ref,
+                    qn_ref, kn_ref, cos_ref, sin_ref,
+                    rows_out, dw_out, wo_out, gq_ref, gk_ref,
+                    dy_s, n_s, w_s, wo_s, do_s, dk_s, dv_s, send_s, got_s, rows_s,
+                    load_sem, ring_send, ring_recv, pair_send, pair_recv, out_sem, swap_send, swap_recv):
     ring = Ring(devices)
     sems = (ring_send, ring_recv, pair_send, pair_recv)
-    head_dim, model_dim = dwo_ref.shape
+    seq_len, head_dim = do_s.shape
+    steps = seq_len // block
+    scale = head_dim ** -0.5
+    share = devices // kn_ref.shape[0]
+    w_rows = pl.ds(pl.multiple_of(ring.me * head_dim, head_dim), head_dim)
+    loads = [pltpu.make_async_copy(dy_ref, dy_s, load_sem.at[0]), pltpu.make_async_copy(wo_ref.at[w_rows, :], w_s, load_sem.at[1]),
+             pltpu.make_async_copy(n_ref, n_s, load_sem.at[2])]
+    for copy in loads:
+        copy.start()
+    ring.barrier()
+    dk_s[...] = jnp.zeros_like(dk_s)
+    dv_s[...] = jnp.zeros_like(dv_s)
+    gq_ref[...] = jnp.zeros_like(gq_ref)
+    loads[0].wait()
+    wo_s[ring.me] = transposed_times(o_ref[...], dy_s[...]).astype(BF16)
+    loads[1].wait()
+    do_s[...] = times_transposed(dy_s[...], w_s[...]).astype(BF16)
+    ring.take(wo_s, sems, 0, 0)
+    causal = lax.broadcasted_iota(jnp.int32, (block, block), 0) >= lax.broadcasted_iota(jnp.int32, (block, block), 1)
+    q_weight = qn_ref[ring.me]
+    done = 0
+    passed = 1
+    for i in range(steps):
+        rows = pl.ds(i * block, block)
+        q_rows, do_rows = q_ref[rows, :], do_s[rows, :]
+        delta = jnp.sum(o32_ref[rows, :] * do_rows.astype(F32), axis=-1, keepdims=True)
+        lse = lse_ref[rows, :][:, :1]
+        dq = jnp.zeros((block, head_dim), F32)
+        for j in range(i + 1):
+            keys = pl.ds(j * block, block)
+            k_rows, v_rows = k_ref[keys, :], v_ref[keys, :]
+            probs = jnp.exp(times_transposed(q_rows, k_rows) * scale - lse)
+            if i == j:
+                probs = jnp.where(causal, probs, 0.0)
+            d_probs = times_transposed(do_rows, v_rows).astype(BF16).astype(F32)
+            d_score = (probs * (d_probs - delta) * scale).astype(BF16)
+            dv_s[keys, :] += transposed_times(probs.astype(BF16), do_rows)
+            dk_s[keys, :] += transposed_times(d_score, q_rows)
+            dq = dq + jnp.dot(d_score, k_rows, preferred_element_type=F32)
+            done += 1
+            if done % 2 == 0 and passed < ring.chips - 2:
+                ring.take(wo_s, sems, 0, passed)
+                passed += 1
+        dq_proj, d_weight = head_backward(dq.astype(BF16).astype(F32), qproj_ref[rows, :].astype(F32), q_weight,
+                                          cos_ref[rows, :], sin_ref[rows, :])
+        rows_s[rows, pl.ds(0, head_dim)] = dq_proj.astype(BF16)
+        gq_ref[...] += d_weight
+
+    @pl.when(ring.core == 0)
+    def _():
+        send_s[...] = dv_s[...].astype(BF16)
+
+    @pl.when(ring.core == 1)
+    def _():
+        send_s[...] = dk_s[...].astype(BF16)
+    while passed < ring.chips - 1:
+        ring.take(wo_s, sems, 0, passed)
+        passed += 1
+    swap = pltpu.make_async_remote_copy(send_s, got_s, swap_send, swap_recv, device_id={'sp': ring.partner}, device_id_type=MESH)
+    swap.start()
+    loads[2].wait()
+    swap.wait()
+
+    @pl.when(ring.core == 0)
+    def _():
+        total = (dk_s[...].astype(BF16).astype(F32) + got_s[...].astype(F32)).astype(BF16).astype(F32)
+        dk_proj, d_weight = head_backward(total, kproj_ref[...].astype(F32), kn_ref[ring.me // share], cos_ref[...], sin_ref[...])
+        rows_s[:, head_dim:] = dk_proj.astype(BF16)
+        gk_ref[...] = d_weight
+
+    @pl.when(ring.core == 1)
+    def _():
+        rows_s[:, head_dim:] = (dv_s[...].astype(BF16).astype(F32) + got_s[...].astype(F32)).astype(BF16)
+        gk_ref[...] = jnp.zeros_like(gk_ref)
+    ring.take(wo_s, sems, 0, passed)
+    put_rows = pltpu.make_async_copy(rows_s, rows_out, load_sem.at[3])
+    put_rows.start()
+    dw_out[...] = transposed_times(n_s[...], rows_s[...]).astype(BF16)
+
+    def put_o(slot):
+        rows = pl.ds(pl.multiple_of(slot * head_dim, head_dim), head_dim)
+        return pltpu.make_async_copy(wo_s.at[slot], wo_out.at[rows, :], out_sem.at[slot])
+
+    def collect(step, carry):
+        ring.shared(wo_s, sems, 0, step).wait_recv()
+        put_o(ring.own_slot(step)).start()
+        put_o(ring.other_slot(step)).start()
+        return carry
+    lax.fori_loop(0, ring.chips, collect, 0)
+    ring.finish(wo_s, sems, 0)
+
+    def drain(slot, carry):
+        put_o(slot).wait()
+        return carry
+    lax.fori_loop(0, devices, drain, 0)
+    put_rows.wait()
+
+
+def weight_kernel(devices, dwqkv_ref, rows_ref, o_ref, n_ref, dy_ref, hid_ref, dg_ref, du_ref, wq_ref, wk_ref, wv_ref, wo_ref,
+                  x_ref, gain_ref, mlp_ref, dn_ref, gq_ref, gk_ref,
+                  q_out, k_out, v_out, g_out, u_out, d_out, y_out, dx_out, gain_out, qn_out, kn_out,
+                  wqkv_s, n_s, dy_s, nt_s, hid_s, dg_s, du_s, st_g, st_u, st_d, got_s, of_s, df_s, kf_s, vf_s, wq_s, wk_s, wv_s, wo_s, small_s,
+                  load_sem, tile_sem, ring_send, ring_recv, pair_send, pair_recv, out_sem, kv_sem,
+                  put_sem, swap_send, swap_recv, rows_send, rows_recv, small_send, small_recv):
+    ring = Ring(devices)
+    sems = (ring_send, ring_recv, pair_send, pair_recv)
+    model_dim = n_ref.shape[1]
+    local_len, head_dim = o_ref.shape[1:]
     half = hid_ref.shape[1]
     tile = st_g.shape[2]
     tiles = half // tile
-    loads = [pltpu.make_async_copy(dwo_ref, wo_s.at[ring.me], load_sem.at[0]),
-             pltpu.make_async_copy(dwqkv_ref, wqkv_s.at[ring.me], load_sem.at[1]),
+    num_kv = kn_out.shape[0]
+    share = devices // num_kv
+    loads = [pltpu.make_async_copy(dwqkv_ref, wqkv_s.at[ring.me], load_sem.at[0]),
+             pltpu.make_async_copy(rows_ref.at[ring.me], got_s.at[ring.me], load_sem.at[1]),
              pltpu.make_async_copy(n_ref, n_s, load_sem.at[2]),
              pltpu.make_async_copy(dy_ref, dy_s, load_sem.at[3])]
+    late = [pltpu.make_async_copy(src, dst, load_sem.at[4 + i])
+            for i, (src, dst) in enumerate(((wo_ref, wo_s), (wq_ref, wq_s), (wk_ref, wk_s), (wv_ref, wv_s)))]
     tile_bufs = ((hid_ref, hid_s), (dg_ref, dg_s), (du_ref, du_s))
 
     def fetch(i, t):
@@ -440,20 +492,35 @@
         copy.start()
     for i in range(3):
         fetch(i, 0).start()
-    ring.barrier()
+    ring.barrier_all()
     loads[0].wait()
-    loads[1].wait()
-
-    def put_o(slot):
-        rows = pl.ds(pl.multiple_of(slot * head_dim, head_dim), head_dim)
-        return pltpu.make_async_copy(wo_s.at[slot], o_out.at[rows, :], out_sem.at[0, slot])
+
+    def rows_copy(hop):
+        return ring.direct(rows_ref.at[ring.peer(hop)], got_s.at[ring.me], rows_send, rows_recv, hop)
+
+    def rows_from(hop):
+        source = lax.rem(ring.me + devices - hop, devices)
+        return ring.direct(rows_ref.at[source], got_s.at[source], rows_send, rows_recv, hop)
+
+    def small_copy(hop):
+        return ring.direct(small_s.at[ring.me], small_s.at[ring.me], small_send, small_recv, hop)
+
+    def small_from(hop):
+        source = lax.rem(ring.me + devices - hop, devices)
+        return ring.direct(small_s.at[source], small_s.at[source], small_send, small_recv, hop)
+
+    def each_peer(body):
+        def step(hop, carry):
+            body(hop)
+            return carry
+        lax.fori_loop(1, devices, step, 0)
 
     def put_q(slot):
         cols = pl.ds(pl.multiple_of(slot * head_dim, head_dim), head_dim)
-        return pltpu.make_async_copy(wqkv_s.at[slot, :, pl.ds(0, head_dim)], q_out.at[:, cols], out_sem.at[1, slot])
+        return pltpu.make_async_copy(wqkv_s.at[slot, :, pl.ds(0, head_dim)], q_out.at[:, cols], out_sem.at[slot])
 
     def put_kv(slot, out):
-        cols = pl.ds(pl.multiple_of(slot // 2 * head_dim, head_dim), head_dim)
+        cols = pl.ds(pl.multiple_of(slot // share * head_dim, head_dim), head_dim)
         return pltpu.make_async_copy(wqkv_s.at[slot, :, pl.ds(head_dim, head_dim)], out.at[:, cols], kv_sem.at[slot])
 
     def store(t, i, core):
@@ -470,11 +537,44 @@
         return pltpu.make_async_remote_copy(src, dst, swap_send.at[i, t], swap_recv.at[i, t],
                                             device_id={'sp': ring.partner}, device_id_type=MESH)
 
+    def finish_forward():
+        late[0].wait()
+        for h in range(devices):
+            of_s[:, h * head_dim:(h + 1) * head_dim] = o_ref[h]
+        attn_out = jnp.dot(of_s[...], wo_s[...], preferred_element_type=F32).astype(BF16)
+        y_out[...] = (x_ref[...].astype(F32) + attn_out.astype(F32) + mlp_ref[...].astype(F32)).astype(BF16)
+
+    def finish_backward():
+        each_peer(lambda hop: rows_from(hop).wait_recv())
+        loads[1].wait()
+        for h in range(devices):
+            df_s[:, h * head_dim:(h + 1) * head_dim] = got_s[h, :, :head_dim]
+        for j in range(num_kv):
+            kf_s[:, j * head_dim:(j + 1) * head_dim] = got_s[share * j, :, head_dim:]
+            vf_s[:, j * head_dim:(j + 1) * head_dim] = got_s[share * j + 1, :, head_dim:]
+        for copy in late[1:]:
+            copy.wait()
+        d_norm = (times_transposed(df_s[...], wq_s[...]) + times_transposed(kf_s[...], wk_s[...])
+                  + times_transposed(vf_s[...], wv_s[...]) + dn_ref[...]).astype(BF16).astype(F32)
+        unit, inv_std = head_stats(x_ref[...].astype(F32))
+        grad_gain = jnp.sum(d_norm * unit, axis=0, keepdims=True)
+        d_unit = d_norm * gain_ref[...]
+        mean_d = jnp.mean(d_unit, axis=-1, keepdims=True)
+        mean_du = jnp.mean(d_unit * unit, axis=-1, keepdims=True)
+        dx = inv_std * (d_unit - mean_d - unit * mean_du)
+        own_rows = pl.ds(pl.multiple_of(ring.me * local_len, local_len), local_len)
+        dx_out[...] = (dy_s[own_rows, :].astype(F32) + dx).astype(BF16)
+        gains = model_dim // head_dim
+        parts = [grad_gain[:, c * head_dim:(c + 1) * head_dim] for c in range(gains)] + [gq_ref[...], gk_ref[...]]
+        pad = jnp.zeros((small_s.shape[1] - len(parts), head_dim), F32)
+        small_s[ring.me] = jnp.concatenate(parts + [pad], axis=0)
+
     def step_body(step, carry):
-        ring.take(wo_s, sems, 0, step)
+        ring.take(wqkv_s, sems, 0, step)
 
         @pl.when(step == 0)
         def _():
+            each_peer(lambda hop: rows_copy(hop).start())
             loads[2].wait()
 
             def turn(i, inner):
@@ -502,17 +602,23 @@
                 st_u[step, rows, :] = jnp.dot(nt_s[rows, :], du_s[step % 2], preferred_element_type=F32).astype(BF16)
                 return inner
             lax.fori_loop(0, 4, in_weights, 0)
-
-        ring.take(wqkv_s, sems, 1, step)
-
-        @pl.when(step < tiles)
-        def _():
             st_d[step] = transposed_times(hid_s[step % 2], dy_s[...]).astype(BF16)
 
-        ring.shared(wo_s, sems, 0, step).wait_recv()
-        ring.shared(wqkv_s, sems, 1, step).wait_recv()
+        @pl.when(step == 1)
+        def _():
+            for copy in late:
+                copy.start()
+
+        @pl.when(step == tiles)
+        def _():
+            finish_forward()
+
+        @pl.when(step == tiles + 1)
+        def _():
+            finish_backward()
+
+        ring.shared(wqkv_s, sems, 0, step).wait_recv()
         for slot in (ring.own_slot(step), ring.other_slot(step)):
-            put_o(slot).start()
             put_q(slot).start()
 
             @pl.when(slot % 2 == 0)
@@ -531,11 +637,10 @@
         return carry
 
     lax.fori_loop(0, ring.chips, step_body, 0)
-    ring.finish(wo_s, sems, 0)
-    ring.finish(wqkv_s, sems, 1)
+    each_peer(lambda hop: small_copy(hop).start())
+    ring.finish(wqkv_s, sems, 0)
 
     def drain(slot, carry):
-        put_o(slot).wait()
         put_q(slot).wait()
         put_kv(slot, k_out).wait()
         return carry
@@ -548,6 +653,16 @@
             send_tile(t, i, 1 - ring.core).wait_recv()
         return carry
     lax.fori_loop(0, tiles, drain_tiles, 0)
+    each_peer(lambda hop: rows_copy(hop).wait_send())
+    each_peer(lambda hop: small_from(hop).wait_recv())
+    each_peer(lambda hop: small_copy(hop).wait_send())
+    gains = model_dim // head_dim
+    total = small_s[0, :gains]
+    for h in range(1, devices):
+        total = total + small_s[h, :gains]
+    gain_out[...] = total
+    qn_out[...] = jnp.concatenate([small_s[h, gains:gains + 1] for h in range(devices)], axis=0)
+    kn_out[...] = jnp.concatenate([small_s[share * j, gains + 1:gains + 2] for j in range(num_kv)], axis=0)
 
 
 def whole(shape):
@@ -558,11 +673,6 @@
     group_devices = mesh.shape['sp']
     seq_spec = P('dp', 'sp', None)
     grad_spec = P('dp', None)
-    pair_swap = [(i, i ^ 1) for i in range(group_devices)]
-    def spread(piece):
-        copies = jnp.broadcast_to(piece[None], (group_devices,) + piece.shape)
-        return lax.all_to_all(copies, 'sp', 0, 0, tiled=True)
-
     def layer_step(x_in, grad_y, positions, w_q, w_k, w_v, w_o, w_gate, w_up, w_down, norm_gain, q_norm, k_norm):
         batch_rows, local_len, model_dim = x_in.shape
         num_heads, head_dim = q_norm.shape
@@ -582,8 +692,8 @@
                 grid_spec=pltpu.PrefetchScalarGridSpec(num_scalar_prefetch=1, grid=grid, in_specs=in_specs, out_specs=out_specs,
                                                        scratch_shapes=scratch))
 
-        x_f32 = x_in.reshape(local_len, model_dim).astype(F32)
-        flat_norm, norm_back = jax.vjp(input_norm, x_f32, norm_gain)
+        x_rows = x_in.reshape(local_len, model_dim)
+        gain_row = norm_gain.reshape(1, model_dim)
         grad_flat = grad_y.reshape(local_len, model_dim)
         half = ffn_dim // 2
         dma = pltpu.SemaphoreType.DMA
@@ -599,14 +709,14 @@
             functools.partial(gather_kernel, group_devices), name="gather_tokens",
             out_shape=[struct(blocks, BF16), struct(blocks, BF16), struct((group_devices, 8, local_len), jnp.int32)]
             + [struct(acts, BF16)] * 3 + [struct((local_len, model_dim), BF16), struct((local_len, model_dim), F32)],
-            in_specs=[hbm] * 6, out_specs=[hbm] * 6 + [in_vmem] * 2,
+            in_specs=[in_vmem] * 2 + [hbm] * 5, out_specs=[hbm] * 6 + [in_vmem] * 2,
             scratch_shapes=[vmem(blocks, BF16), vmem(blocks, BF16), vmem((group_devices, 8, local_len), jnp.int32),
                             vmem((model_dim, half), BF16), vmem((model_dim, half), BF16), vmem((half, model_dim), BF16)]
             + [vmem(acts, BF16)] * 3 + [vmem((2 * local_len, half), F32)] * 2 + [vmem((2, local_len, model_dim), F32)] * 3
             + [dma((3,)), dma((3,))] + ring_sems(3) + [dma((3, group_devices)), dma((3, group_devices)), dma(()), dma(())],
             compiler_params=pltpu.CompilerParams(collective_id=0, has_side_effects=True, vmem_limit_bytes=VMEM_LIMIT),
             cost_estimate=pl.CostEstimate(flops=40_000_000_000, bytes_accessed=40_000_000, transcendentals=0),
-        )(flat_norm, grad_flat, pos_rows, w_gate, w_up, w_down)
+        )(x_rows, gain_row, grad_flat, pos_rows, w_gate, w_up, w_down)
         n_all, dy_all = n_all.reshape(seq_len, model_dim), dy_all.reshape(seq_len, model_dim)
         hid, d_gate, d_up = (act.reshape(seq_len, half) for act in (hid, d_gate, d_up))
         cos_t, sin_t = rope_lanes(pos_all[:, 0].reshape(seq_len), head_dim)
@@ -631,61 +741,40 @@
             [rows_bf, rows_f32, rows_f32] + [rows_bf] * 5, [pltpu.VMEM((block, seq_len), F32)],
         )(idx, n_all, w_q, w_k, w_v, qn3, kn3, cos_t, sin_t)
 
-        d_o, dwo_h = call(
-            output_grad_kernel, "output_grad", 3_000_000_000, 6_000_000, (1,), [tokens, head_rows, rows], [rows, whole((head_dim, model_dim))],
-            [rows_bf, jax.ShapeDtypeStruct((head_dim, model_dim), BF16)], [],
-        )(idx, dy_all, w_o, o_h)
-
-        dq_h, send, keep, gq = call(
-            functools.partial(backward_kernel, block), "attention_bwd", 14_000_000_000, 8_000_000, (1,),
-            [rows] * 7 + [head_vec, rows, rows], [rows] * 3 + [whole((1, head_dim))], [rows_bf] * 3 + [vec],
-            [pltpu.VMEM((seq_len, head_dim), F32)] * 2,
-        )(idx, d_o, o32, lse, q_rot, k_rot, v_h, q_proj, qn3, cos_t, sin_t)
-
-        got = lax.ppermute(send, 'sp', pair_swap)
-        d_rows, dwqkv_h, gk = call(
-            projection_grad_kernel, "projection_grad", 4_000_000_000, 8_000_000, (1,),
-            [tokens] + [rows] * 4 + [kv_vec, rows, rows],
-            [whole((seq_len, 2 * head_dim)), whole((model_dim, 2 * head_dim)), whole((1, head_dim))],
-            [jax.ShapeDtypeStruct((seq_len, 2 * head_dim), BF16), jax.ShapeDtypeStruct((model_dim, 2 * head_dim), BF16), vec],
-            [],
-        )(idx, n_all, dq_h, keep, got, k_proj, kn3, cos_t, sin_t)
+        attn_own = lax.all_to_all(o_h.reshape(group_devices, local_len, head_dim), 'sp', 0, 0, tiled=True)
+        d_rows, dwqkv_h, dw_o, gq, gk = pl.pallas_call(
+            functools.partial(backward_kernel, group_devices, block), name="attention_bwd",
+            out_shape=[struct((seq_len, 2 * head_dim), BF16), struct((model_dim, 2 * head_dim), BF16), struct(w_o.shape, BF16), vec, vec],
+            in_specs=[hbm] * 3 + [in_vmem] * 12, out_specs=[hbm, in_vmem, hbm, in_vmem, in_vmem],
+            scratch_shapes=[vmem((seq_len, model_dim), BF16)] * 2 + [vmem((head_dim, model_dim), BF16), vmem((group_devices, head_dim, model_dim), BF16)]
+            + [vmem((seq_len, head_dim), BF16)] + [vmem((seq_len, head_dim), F32)] * 2 + [vmem((seq_len, head_dim), BF16)] * 2
+            + [vmem((seq_len, 2 * head_dim), BF16), dma((4,))] + ring_sems(1) + [dma((group_devices,)), dma(()), dma(())],
+            compiler_params=pltpu.CompilerParams(collective_id=2, has_side_effects=True, vmem_limit_bytes=VMEM_LIMIT),
+            cost_estimate=pl.CostEstimate(flops=30_000_000_000, bytes_accessed=30_000_000, transcendentals=0),
+        )(dy_all, n_all, w_o, o_h, o32, lse, q_rot, k_rot, v_h, q_proj, k_proj, qn3, kn3, cos_t, sin_t)
 
         tile = 256
         tiles = half // tile
         tile_in = (tiles, model_dim, tile)
-        dw_q, dw_k, dw_v, dw_o, dw_gate, dw_up, dw_down = pl.pallas_call(
+        gain_shape = (model_dim // head_dim, head_dim)
+        flat = (local_len, num_heads * head_dim)
+        flat_kv = (local_len, num_kv * head_dim)
+        dw_q, dw_k, dw_v, dw_gate, dw_up, dw_down, y_out, grad_x, grad_gain, grad_q_norm, grad_k_norm = pl.pallas_call(
             functools.partial(weight_kernel, group_devices), name="gather_weights",
-            out_shape=[struct(w.shape, BF16) for w in (w_q, w_k, w_v, w_o, w_gate, w_up, w_down)],
-            in_specs=[hbm] * 7, out_specs=[hbm] * 7,
-            scratch_shapes=[vmem((group_devices, head_dim, model_dim), BF16), vmem((group_devices, model_dim, 2 * head_dim), BF16),
+            out_shape=[struct(w.shape, BF16) for w in (w_q, w_k, w_v, w_gate, w_up, w_down)]
+            + [struct((local_len, model_dim), BF16)] * 2 + [struct(gain_shape, F32), struct(q_norm.shape, F32), struct(k_norm.shape, F32)],
+            in_specs=[hbm, hbm, in_vmem] + [hbm] * 9 + [in_vmem] * 6, out_specs=[hbm] * 6 + [in_vmem] * 5,
+            scratch_shapes=[vmem((group_devices, model_dim, 2 * head_dim), BF16),
                             vmem((seq_len, model_dim), BF16), vmem((seq_len, model_dim), BF16), vmem((model_dim, seq_len), BF16)]
             + [vmem((2, seq_len, tile), BF16)] * 3 + [vmem(tile_in, BF16), vmem(tile_in, BF16), vmem((tiles, tile, model_dim), BF16)]
-            + [dma((4,)), dma((3, 2))] + ring_sems(2) + [dma((2, group_devices)), dma((group_devices,))] + [dma((3, tiles))] * 3,
+            + [vmem((group_devices, local_len, 2 * head_dim), BF16), vmem(flat, BF16), vmem(flat, BF16), vmem(flat_kv, BF16), vmem(flat_kv, BF16)]
+            + [vmem(w.shape, BF16) for w in (w_q, w_k, w_v, w_o)] + [vmem((group_devices, 16, head_dim), F32)]
+            + [dma((8,)), dma((3, 2))] + ring_sems(1) + [dma((group_devices,))] * 2 + [dma((3, tiles))] * 3 + [dma((group_devices,))] * 4,
             compiler_params=pltpu.CompilerParams(collective_id=1, has_side_effects=True, vmem_limit_bytes=VMEM_LIMIT),
             cost_estimate=pl.CostEstimate(flops=60_000_000_000, bytes_accessed=60_000_000, transcendentals=0),
-        )(dwo_h, dwqkv_h, n_all, dy_all, hid, d_gate, d_up)
-
-        attn_flat = lax.all_to_all(o_h, 'sp', 0, 1, tiled=True)
-        attn_out = jnp.dot(attn_flat, w_o, preferred_element_type=F32).astype(BF16)
-        y_out = (x_f32 + attn_out.astype(F32) + mlp_out.astype(F32)).astype(BF16)
-
-        d_rows = lax.all_to_all(d_rows, 'sp', 0, 1, tiled=True)
-        d_rows = d_rows.reshape(local_len, num_kv, share, 2, head_dim)
-        dq_flat = d_rows[:, :, :, 0].reshape(local_len, num_heads * head_dim)
-        dk_flat = d_rows[:, :, 0, 1].reshape(local_len, num_kv * head_dim)
-        dv_flat = d_rows[:, :, 1, 1].reshape(local_len, num_kv * head_dim)
-        d_norm = (times_transposed(dq_flat, w_q) + times_transposed(dk_flat, w_k) + times_transposed(dv_flat, w_v) + d_norm_mlp).astype(BF16)
-        dx_norm, grad_gain = norm_back(d_norm)
-        grad_x = (grad_flat.astype(F32) + dx_norm).astype(BF16)
-
-        gain_rows = model_dim // head_dim
-        small = jnp.concatenate([grad_gain.reshape(gain_rows, head_dim), gq, gk], axis=0)
-        small_all = spread(small)
-        grad_gain = jnp.sum(small_all[:, :gain_rows], axis=0).reshape(model_dim)
-        grad_q_norm = small_all[:, gain_rows]
-        grad_k_norm = small_all[::share, gain_rows + 1]
-
+        )(dwqkv_h, d_rows.reshape(group_devices, local_len, 2 * head_dim), attn_own, n_all, dy_all, hid, d_gate, d_up,
+          w_q, w_k, w_v, w_o, x_rows, gain_row, mlp_out, d_norm_mlp, gq, gk)
+        grad_gain = grad_gain.reshape(model_dim)
         return (y_out.reshape(x_in.shape), grad_x.reshape(x_in.shape), dw_q, dw_k, dw_v, dw_o, dw_gate, dw_up, dw_down,
                 grad_gain, grad_q_norm, grad_k_norm)
 

time: 288 us -> 279 us (0.969)
  Pallas kernels: 205 us -> 236 us
  starting transfers between devices: 19 us -> 5.81 us
  matrix products: 9.23 us -> 0 us
  waiting for transfers between devices: 9.22 us -> 0.01 us
  other arithmetic: 13.1 us -> 6.97 us
    pallas_call x3 -> x1, Pallas kernels: 29.4 us -> 54.1 us  [layer_step(): pl.pallas_call(functools.partial(backward_kernel, group_devices, block),...]
    all_to_all x3 -> x1, starting transfers between devices: 18.7 us -> 5.81 us  [layer_step(): lax.all_to_all(o_h.reshape(group_devices, local_len, head_dim), 'sp', 0,...]
    dot_general x4 -> x0, matrix products: 9.23 us -> none  [the longest x3 5.41 us: times_transposed(): lax.dot_general(lhs_mat, rhs_mat, (((1,), (1,)), ((), ())), preferred_ele...]
    all_to_all x3 -> x1, waiting for transfers between devices: 7.65 us -> 0.01 us  [layer_step(): lax.all_to_all(o_h.reshape(group_devices, local_len, head_dim), 'sp', 0,...]
    pallas_call x1, Pallas kernels: 90.9 us -> 96.6 us  [layer_step(): pl.pallas_call(functools.partial(weight_kernel, group_devices), name='gat...]
    all_to_all x2 -> x0, local copies, waits for them, and re-layouts: 4.3 us -> none  [the longest x1 2.26 us: layer_step(): d_rows = lax.all_to_all(d_rows, 'sp', 0, 1, tiled=True)]
    unnamed x47 -> x38, local copies, waits for them, and re-layouts: 23.6 us -> 27.8 us
    reduce_sum x4 -> x0, other arithmetic: 3.19 us -> none  [the longest x1 1.17 us: input_norm(): row_var = jnp.mean(centered * centered, axis=-1, keepdims=True)]
  transfers between devices with their start and end apart: 4 -> 1, of which waited for: 2 -> 0; matrix products, arithmetic and copies ran while one was open for 2% -> 0% of each run, Pallas kernels for 42% -> 19%
where the time goes in v4:
time: 279 us
  Pallas kernels  236 us (85%)
  local copies, waits for them, and re-layouts  29.1 us (10%)
  other arithmetic  6.97 us (2%)
  starting transfers between devices  5.81 us (2%)
    pallas_call x1, Pallas kernels, layer_step(): pl.pallas_call(functools.partial(weight_kernel, group_devices), name='gat...  96.6 us
    pallas_call x1, Pallas kernels, layer_step(): pl.pallas_call(functools.partial(gather_kernel, group_devices), name='gat...  63 us
    pallas_call x1, Pallas kernels, layer_step(): pl.pallas_call(functools.partial(backward_kernel, group_devices, block),...  54.1 us
    unnamed x38, local copies, waits for them, and re-layouts  27.8 us
    pallas_call x1, Pallas kernels, layer_step(): call(functools.partial(forward_kernel, block), 'attention_fwd', 100000000...  22.5 us
    all_to_all x1, starting transfers between devices, layer_step(): lax.all_to_all(o_h.reshape(group_devices, local_len, head_dim), 'sp', 0,...  5.81 us
  transfers between devices with their start and end apart: 1, of which 0 were waited for; matrix products, arithmetic and copies ran while one was open for 0% of the time, Pallas kernels for 19%

profile of v4, /device:TPU:21, one launch (start us, length us, event | category | flops | bytes accessed | tf_op | source)
XLA Modules:
  0.0 278.8 jit_solution(5952773392272554018)
XLA Ops:
  0.7 1.3 broadcast_in_dim.16.pos_ref
  1.9 63.0 %gather_tokens.1 = (bf16[16,128,1024]{2,1,0:T(8,128)(2,1)}, bf16[16,128,1024]{2,1,0:T(8,128)(2,1)}, s32[16,8,128]{2,1,0:T(8,128)}, bf16[16,128,1536]{2,1,0:T(8,1...) custom-call(bf16[128,1024]{1,0:T(8,128)(2,1)} %bitcast.31, ...), custom_call_target="tpu_custom_call" | custom-call | flops 40000000000 | bytes 40000000 | tf_op jit(solution)/shard_map/gather_tokens/pallas_call | solution.py:708
  65.0 0.8 slice_convert_fusion
  66.4 5.5 %fusion = (f32[2048,128]{1,0:T(8,128)}, f32[2048,128]{1,0:T(8,128)}) fusion(f32[128]{0:T(128)S(1)} %get-tuple-element.78, f32[128]{0:T(128)S(1)} %get-tuple-element.79, f32[2048]{0:T(1024)S(1)} %bitcast.28), kind=kLoop, calls=%fused_computation.2 | loop fusion | flops 524288 | bytes 2106368 | tf_op jit(solution)/shard_map/mul | solution.py:42
  71.9 22.5 %attention_fwd.1 = (bf16[2048,128]{1,0:T(8,128)(2,1)}, f32[2048,128]{1,0:T(8,128)}, f32[2048,128]{1,0:T(8,128)}, bf16[2048,128]{1,0:T(8,128)(2,1)}, bf16[2048,12...) custom-call(s32[3]{0:T(128)} %pad_add_fusion.idx_ref, ...), custom_call_target="tpu_custom_call" | custom-call | flops 10000000000 | bytes 12000000 | tf_op jit(solution)/shard_map/attention_fwd/pallas_call | solution.py:738
  94.4 5.8 %all-to-all-start = ((bf16[16,128,128]{2,1,0:T(8,128)(2,1)}), bf16[16,128,128]{2,1,0:T(8,128)(2,1)S(1)}, u32[]{:S(2)}, u32[]{:S(2)}) async-start(bf16[16,128,128]{2,1,0:T(8,128)(2,1)} %bitcast.25), calls=%async_computation | async-start | bytes 1048576 | tf_op jit(solution)/shard_map/all_to_all | solution.py:744
  100.2 54.1 %attention_bwd.1 = (bf16[2048,256]{1,0:T(8,128)(2,1)}, bf16[1024,256]{1,0:T(8,128)(2,1)}, bf16[2048,1024]{1,0:T(8,128)(2,1)}, f32[1,128]{1,0:T(1,128)}, f32[1,128]{1,0:T(1,128)}) custom-call(bf16[2048,1024]{1,0:T(8,128)(2,1)} %bitcast.45, bf16[2048,1024]{1,0:T(8,128)(2,1)} %bitcast.43, bf16[2048,1024]{1,0:T(8,128)(2,1)} %wo_ref.3, ...), custom_call_target="tpu_custom_call" | custom-call | flops 30000001024 | bytes 30000000 | tf_op jit(solution)/shard_map/attention_bwd/pallas_call | solution.py:745
  154.3 0.8 copy-done.3
  155.1 96.6 %gather_weights.1 = (bf16[1024,2048]{1,0:T(8,128)(2,1)}, bf16[1024,1024]{1,0:T(8,128)(2,1)}, bf16[1024,1024]{1,0:T(8,128)(2,1)}, bf16[1024,3072]{1,0:T(8,128)(2,...) custom-call(bf16[1024,256]{1,0:T(8,128)(2,1)} %get-tuple-element.55., ...), custom_call_target="tpu_custom_call" | custom-call | flops 60000002048 | bytes 60000000 | tf_op jit(solution)/shard_map/gather_weights/pallas_call | solution.py:762
  251.7 1.7 copy.37
  253.4 1.7 copy.38
  255.1 5.1 %copy.39 = bf16[1024,2048]{1,0:T(8,128)(2,1)} copy(bf16[1024,2048]{1,0:T(8,128)(2,1)} %get-tuple-element.94) | data formatting | bytes 8388608
  260.2 1.3 copy.40
  261.5 1.3 copy.41
  262.8 1.2 copy-done
  264.0 2.1 copy.42
  266.2 3.2 %copy.43 = bf16[1024,3072]{1,0:T(8,128)(2,1)} copy(bf16[1024,3072]{1,0:T(8,128)(2,1)S(1)} %bitcast.24) | data formatting | bytes 12582912
  269.4 1.3 slice-done.3
  270.7 2.9 %copy.44 = bf16[1024,3072]{1,0:T(8,128)(2,1)} copy(bf16[1024,3072]{1,0:T(8,128)(2,1)S(1)} %bitcast.22) | data formatting | bytes 12582912
  273.6 0.7 slice-done.1
  274.3 2.7 copy.45
  277.0 0.6 copy.46
  277.6 0.6 copy.47
  278.2 0.6 copy.48
  (28 shorter events, 0.6 us)
Async XLA Ops:
  94.4 59.9 %all-to-all-start = ((bf16[16,128,128]{2,1,0:T(8,128)(2,1)}), bf16[16,128,128]{2,1,0:T(8,128)(2,1)S(1)}, u32[]{:S(2)}, u32[]{:S(2)}) async-start(bf16[16,128,128]{2,1,0:T(8,128)(2,1)} %bitcast.25), calls=%async_computation | async-start | bytes 1048576 | tf_op jit(solution)/shard_map/all_to_all | solution.py:744
  154.3 0.8 copy-start.3
  255.1 5.1 %copy-start.2 = (bf16[1024,1024]{1,0:T(8,128)(2,1)S(1)}, bf16[1024,1024]{1,0:T(8,128)(2,1)}, u32[]{:S(2)}) copy-start(bf16[1024,1024]{1,0:T(8,128)(2,1)} %get-tuple-element.95) | copy-start | bytes 6291460
  255.1 6.4 %copy-start.1 = (bf16[1024,1024]{1,0:T(8,128)(2,1)S(1)}, bf16[1024,1024]{1,0:T(8,128)(2,1)}, u32[]{:S(2)}) copy-start(bf16[1024,1024]{1,0:T(8,128)(2,1)} %get-tuple-element.96) | copy-start | bytes 6291460
  255.1 11.1 %slice-start.4 = ((s8[6291456]{0:T(1024)(128)(4,1)}), s8[4194304]{0:T(1024)(128)(4,1)S(1)}, s32[]{:S(2)}) async-start(s8[6291456]{0:T(1024)(128)(4,1)} %bitcast.23), calls=%async_computation.5 | async-start | bytes 8388608
  260.2 3.9 %copy-start = (bf16[2048,1024]{1,0:T(8,128)(2,1)S(1)}, bf16[2048,1024]{1,0:T(8,128)(2,1)}, u32[]{:S(2)}) copy-start(bf16[2048,1024]{1,0:T(8,128)(2,1)} %get-tuple-element.97) | copy-start | bytes 12582916
  261.5 4.7 %slice-start.5 = ((s8[6291456]{0:T(1024)(128)(4,1)}), s8[2097152]{0:T(1024)(128)(4,1)S(1)}, s32[]{:S(2)}) async-start(s8[6291456]{0:T(1024)(128)(4,1)} %bitcast.23), calls=%async_computation.6 | async-start | bytes 4194304
  264.0 5.4 %slice-start.2 = ((s8[6291456]{0:T(1024)(128)(4,1)}), s8[4194304]{0:T(1024)(128)(4,1)S(1)}, s32[]{:S(2)}) async-start(s8[6291456]{0:T(1024)(128)(4,1)} %bitcast.21), calls=%async_computation.3 | async-start | bytes 8388608
  266.2 4.6 %slice-start.3 = ((s8[6291456]{0:T(1024)(128)(4,1)}), s8[2097152]{0:T(1024)(128)(4,1)S(1)}, s32[]{:S(2)}) async-start(s8[6291456]{0:T(1024)(128)(4,1)} %bitcast.21), calls=%async_computation.4 | async-start | bytes 4194304
  266.2 7.5 %slice-start = ((s8[6291456]{0:T(1024)(128)(4,1)}), s8[4194304]{0:T(1024)(128)(4,1)S(1)}, s32[]{:S(2)}) async-start(s8[6291456]{0:T(1024)(128)(4,1)} %bitcast.19), calls=%async_computation.1 | async-start | bytes 8388608
  270.7 3.6 %slice-start.1 = ((s8[6291456]{0:T(1024)(128)(4,1)}), s8[2097152]{0:T(1024)(128)(4,1)S(1)}, s32[]{:S(2)}) async-start(s8[6291456]{0:T(1024)(128)(4,1)} %bitcast.19), calls=%async_computation.2 | async-start | bytes 4194304
  274.3 2.7 copy-start.6
  274.3 3.3 %copy-start.4 = (f32[16,128]{1,0:T(8,128)S(1)}, f32[16,128]{1,0:T(8,128)}, u32[]{:S(2)}) copy-start(f32[16,128]{1,0:T(8,128)} %get-tuple-element.102) | copy-start | bytes 24580
  274.3 3.9 %copy-start.5 = (f32[8,128]{1,0:T(8,128)S(1)}, f32[8,128]{1,0:T(8,128)}, u32[]{:S(2)}) copy-start(f32[8,128]{1,0:T(8,128)} %get-tuple-element.103) | copy-start | bytes 12292

commit v5 on v4

--- a/solution.py
+++ b/solution.py
@@ -34,12 +34,11 @@
     return lax.dot_general(lhs_mat, rhs_mat, (((0,), (0,)), ((), ())), preferred_element_type=F32)
 
 
-def rope_lanes(positions, head_dim):
+def rope_lanes(head_dim):
     pair_index = jnp.arange(head_dim, dtype=jnp.int32) // 2
     inv_freq = ROPE_THETA ** (-(pair_index.astype(F32) * 2.0) / head_dim)
-    angles = positions.astype(F32)[:, None] * inv_freq[None, :]
     sign = jnp.where(jnp.arange(head_dim) % 2 == 0, -1.0, 1.0).astype(F32)
-    return jnp.cos(angles), jnp.sin(angles) * sign[None, :]
+    return inv_freq[None, :], sign[None, :]
 
 
 def swap_pairs(rows):
@@ -177,54 +176,66 @@
         return pltpu.make_async_remote_copy(src, dst, send.at[hop], recv.at[hop],
                                             device_id={'sp': self.peer(hop)}, device_id_type=MESH)
 
-    def forward(self, buf, sems, lane, step):
-        slot = buf.at[self.own_slot(step)]
-        return pltpu.make_async_remote_copy(slot, slot, sems[0].at[lane, step], sems[1].at[lane, step + 1],
+    def part(self, buf, slot, parts, k):
+        rows = buf.shape[1] // parts
+        return buf.at[slot, pl.ds(k * rows, rows)]
+
+    def forward(self, lane, k, step):
+        buf, sems, parts = lane
+        piece = self.part(buf, self.own_slot(step), parts, k)
+        return pltpu.make_async_remote_copy(piece, piece, sems[0].at[k, step], sems[1].at[k, step + 1],
                                             device_id={'sp': self.after}, device_id_type=MESH)
 
-    def share(self, buf, sems, lane, step):
-        slot = buf.at[self.own_slot(step)]
-        return pltpu.make_async_remote_copy(slot, slot, sems[2].at[lane, step], sems[3].at[lane, step],
+    def share(self, lane, k, step):
+        buf, sems, parts = lane
+        piece = self.part(buf, self.own_slot(step), parts, k)
+        return pltpu.make_async_remote_copy(piece, piece, sems[2].at[k, step], sems[3].at[k, step],
                                             device_id={'sp': self.partner}, device_id_type=MESH)
 
-    def arrived(self, buf, sems, lane, step):
-        slot = buf.at[self.own_slot(step)]
-        return pltpu.make_async_remote_copy(slot, slot, sems[0].at[lane, step], sems[1].at[lane, step],
+    def arrived(self, lane, k, step):
+        buf, sems, parts = lane
+        piece = self.part(buf, self.own_slot(step), parts, k)
+        return pltpu.make_async_remote_copy(piece, piece, sems[0].at[k, step], sems[1].at[k, step],
                                             device_id={'sp': self.before}, device_id_type=MESH)
 
-    def shared(self, buf, sems, lane, step):
-        slot = buf.at[self.other_slot(step)]
-        return pltpu.make_async_remote_copy(slot, slot, sems[2].at[lane, step], sems[3].at[lane, step],
-                                            device_id={'sp': self.partner}, device_id_type=MESH)
-
-    def take(self, buf, sems, lane, step):
-        @pl.when(step > 0)
-        def _():
-            self.arrived(buf, sems, lane, step).wait_recv()
-
-        @pl.when(step < self.chips - 1)
-        def _():
-            self.forward(buf, sems, lane, step).start()
-        self.share(buf, sems, lane, step).start()
-
-    def finish(self, buf, sems, lane):
-        def body(step, carry):
+    def shared(self, lane, step):
+        buf, sems, parts = lane
+        for k in range(parts):
+            piece = self.part(buf, self.other_slot(step), parts, k)
+            pltpu.make_async_remote_copy(piece, piece, sems[2].at[k, step], sems[3].at[k, step],
+                                         device_id={'sp': self.partner}, device_id_type=MESH).wait_recv()
+
+    def take(self, lane, step, ks=None):
+        for k in range(lane[2]) if ks is None else ks:
+            @pl.when(step > 0)
+            def _():
+                self.arrived(lane, k, step).wait_recv()
+
             @pl.when(step < self.chips - 1)
             def _():
-                self.forward(buf, sems, lane, step).wait_send()
-            self.share(buf, sems, lane, step).wait_send()
+                self.forward(lane, k, step).start()
+            self.share(lane, k, step).start()
+
+    def finish(self, lane):
+        def body(step, carry):
+            for k in range(lane[2]):
+                @pl.when(step < self.chips - 1)
+                def _():
+                    self.forward(lane, k, step).wait_send()
+                self.share(lane, k, step).wait_send()
             return carry
         lax.fori_loop(0, self.chips, body, 0)
 
 
-def gather_kernel(devices, x_ref, gain_ref, dy_ref, pos_ref, wg_ref, wu_ref, wd_ref,
-                  n_out, dy_out, pos_out, hid_out, dg_out, du_out, mlp_out, dn_out,
+def gather_kernel(devices, x_ref, gain_ref, freq_ref, sign_ref, dy_ref, pos_ref, wg_ref, wu_ref, wd_ref,
+                  n_out, dy_out, cos_out, sin_out, hid_out, dg_out, du_out, mlp_out, dn_out,
                   n_s, dy_s, pos_s, wg_s, wu_s, wd_s, hid_s, dg_s, du_s, gate_s, up_s, part_s, got_s, mine_s,
-                  load_sem, weight_sem, ring_send, ring_recv, pair_send, pair_recv, out_sem, act_sem, swap_send, swap_recv):
+                  load_sem, weight_sem, *sem_refs):
     ring = Ring(devices)
-    sems = (ring_send, ring_recv, pair_send, pair_recv)
+    out_sem, act_sem, swap_send, swap_recv = sem_refs[12:]
+    p_lane, n_lane, dy_lane = ((buf, sem_refs[4 * i:4 * i + 4], parts) for i, (buf, parts) in enumerate(((pos_s, 1), (n_s, 2), (dy_s, 2))))
     half = wg_s.shape[1]
-    lanes = ((pos_s, pos_ref, pos_out), (n_s, None, n_out), (dy_s, dy_ref, dy_out))
+    lanes = ((pos_s, pos_ref, None), (n_s, None, n_out), (dy_s, dy_ref, dy_out))
     loads = [pltpu.make_async_copy(src, buf.at[ring.me], load_sem.at[i]) for i, (buf, src, _) in enumerate(lanes) if src is not None]
     columns = pl.ds(pl.multiple_of(ring.core * half, half), half)
     weights = [pltpu.make_async_copy(wg_ref.at[:, columns], wg_s, weight_sem.at[0]),
@@ -278,6 +289,12 @@
             return inner
         lax.fori_loop(0, half // tile, body, 0)
 
+    def tables(step):
+        for slot in (ring.own_slot(step), ring.other_slot(step)):
+            angles = pos_s[slot].astype(F32).T[:, :1] * freq_ref[...]
+            cos_out[slot] = jnp.cos(angles)
+            sin_out[slot] = jnp.sin(angles) * sign_ref[...]
+
     def put_acts(step):
         for i in range(3):
             put_act(i, ring.own_slot(step)).start()
@@ -304,8 +321,8 @@
             swap.start()
 
     def step_body(step, carry):
-        ring.take(n_s, sems, 1, step)
-        ring.take(pos_s, sems, 0, step)
+        ring.take(n_lane, step)
+        ring.take(p_lane, step)
 
         @pl.when(step == 1)
         def _():
@@ -315,7 +332,7 @@
         @pl.when(step > 0)
         def _():
             gate_up(step - 1)
-        ring.take(dy_s, sems, 2, step)
+        ring.take(dy_lane, step)
 
         @pl.when(step == 1)
         def _():
@@ -328,9 +345,11 @@
         @pl.when(step > 1)
         def _():
             put_acts(step - 2)
+            tables(step - 2)
         own_tokens(step)
-        for lane in range(3):
-            ring.shared(lanes[lane][0], sems, lane, step).wait_recv()
+        for lane in (p_lane, n_lane, dy_lane):
+            ring.shared(lane, step)
+        for lane in (1, 2):
             put(lane, ring.own_slot(step)).start()
             put(lane, ring.other_slot(step)).start()
         return carry
@@ -339,16 +358,19 @@
     last = ring.chips - 1
     gate_up(last)
     put_acts(last - 1)
+    tables(last - 1)
     hidden(last)
+    tables(last)
     own_tokens(last + 1)
     put_acts(last)
-    for lane in range(3):
-        ring.finish(lanes[lane][0], sems, lane)
+    for lane in (p_lane, n_lane, dy_lane):
+        ring.finish(lane)
 
     def drain(slot, carry):
-        for lane in range(3):
+        for lane in (1, 2):
             put(lane, slot).wait()
-            put_act(lane, slot).wait()
+        for i in range(3):
+            put_act(i, slot).wait()
         return carry
     lax.fori_loop(0, devices, drain, 0)
     swap.wait()
@@ -358,11 +380,11 @@
 
 def backward_kernel(devices, block, dy_ref, n_ref, wo_ref, o_ref, o32_ref, lse_ref, q_ref, k_ref, v_ref, qproj_ref, kproj_ref,
                     qn_ref, kn_ref, cos_ref, sin_ref,
-                    rows_out, dw_out, wo_out, gq_ref, gk_ref,
-                    dy_s, n_s, w_s, wo_s, do_s, dk_s, dv_s, send_s, got_s, rows_s,
-                    load_sem, ring_send, ring_recv, pair_send, pair_recv, out_sem, swap_send, swap_recv):
+                    rows_out, dw_out, wo_out, own_out, gq_ref, gk_ref,
+                    dy_s, n_s, w_s, wo_s, do_s, dk_s, dv_s, send_s, got_s, rows_s, own_s,
+                    load_sem, ring_send, ring_recv, pair_send, pair_recv, out_sem, swap_send, swap_recv, o_send, o_recv):
     ring = Ring(devices)
-    sems = (ring_send, ring_recv, pair_send, pair_recv)
+    lane = (wo_s, (ring_send, ring_recv, pair_send, pair_recv), 2)
     seq_len, head_dim = do_s.shape
     steps = seq_len // block
     scale = head_dim ** -0.5
@@ -372,7 +394,27 @@
              pltpu.make_async_copy(n_ref, n_s, load_sem.at[2])]
     for copy in loads:
         copy.start()
-    ring.barrier()
+    ring.barrier_all()
+    local_len = seq_len // devices
+
+    def tokens_of(device):
+        return pl.ds(pl.multiple_of(device * local_len, local_len), local_len)
+
+    def o_copy(hop):
+        return ring.direct(o_ref.at[tokens_of(ring.peer(hop)), :], own_s.at[ring.me], o_send, o_recv, hop)
+
+    def o_from(hop):
+        source = lax.rem(ring.me + devices - hop, devices)
+        return ring.direct(o_ref.at[tokens_of(source), :], own_s.at[source], o_send, o_recv, hop)
+
+    def each_peer(body):
+        def step(hop, carry):
+            body(hop)
+            return carry
+        lax.fori_loop(1, devices, step, 0)
+
+    each_peer(lambda hop: o_copy(hop).start())
+    own_s[ring.me] = o_ref[tokens_of(ring.me), :]
     dk_s[...] = jnp.zeros_like(dk_s)
     dv_s[...] = jnp.zeros_like(dv_s)
     gq_ref[...] = jnp.zeros_like(gq_ref)
@@ -380,7 +422,7 @@
     wo_s[ring.me] = transposed_times(o_ref[...], dy_s[...]).astype(BF16)
     loads[1].wait()
     do_s[...] = times_transposed(dy_s[...], w_s[...]).astype(BF16)
-    ring.take(wo_s, sems, 0, 0)
+    ring.take(lane, 0)
     causal = lax.broadcasted_iota(jnp.int32, (block, block), 0) >= lax.broadcasted_iota(jnp.int32, (block, block), 1)
     q_weight = qn_ref[ring.me]
     done = 0
@@ -403,8 +445,8 @@
             dk_s[keys, :] += transposed_times(d_score, q_rows)
             dq = dq + jnp.dot(d_score, k_rows, preferred_element_type=F32)
             done += 1
-            if done % 2 == 0 and passed < ring.chips - 2:
-                ring.take(wo_s, sems, 0, passed)
+            if done in (3, 5, 8, 10):
+                ring.take(lane, passed)
                 passed += 1
         dq_proj, d_weight = head_backward(dq.astype(BF16).astype(F32), qproj_ref[rows, :].astype(F32), q_weight,
                                           cos_ref[rows, :], sin_ref[rows, :])
@@ -418,11 +460,10 @@
     @pl.when(ring.core == 1)
     def _():
         send_s[...] = dk_s[...].astype(BF16)
-    while passed < ring.chips - 1:
-        ring.take(wo_s, sems, 0, passed)
-        passed += 1
     swap = pltpu.make_async_remote_copy(send_s, got_s, swap_send, swap_recv, device_id={'sp': ring.partner}, device_id_type=MESH)
     swap.start()
+    ring.take(lane, passed)
+    passed += 1
     loads[2].wait()
     swap.wait()
 
@@ -437,28 +478,37 @@
     def _():
         rows_s[:, head_dim:] = (dv_s[...].astype(BF16).astype(F32) + got_s[...].astype(F32)).astype(BF16)
         gk_ref[...] = jnp.zeros_like(gk_ref)
-    ring.take(wo_s, sems, 0, passed)
+    ring.take(lane, passed)
+    passed += 1
     put_rows = pltpu.make_async_copy(rows_s, rows_out, load_sem.at[3])
     put_rows.start()
     dw_out[...] = transposed_times(n_s[...], rows_s[...]).astype(BF16)
+    while passed < ring.chips:
+        ring.take(lane, passed)
+        passed += 1
+    each_peer(lambda hop: o_from(hop).wait_recv())
+    put_own = pltpu.make_async_copy(own_s, own_out, load_sem.at[4])
+    put_own.start()
 
     def put_o(slot):
         rows = pl.ds(pl.multiple_of(slot * head_dim, head_dim), head_dim)
         return pltpu.make_async_copy(wo_s.at[slot], wo_out.at[rows, :], out_sem.at[slot])
 
     def collect(step, carry):
-        ring.shared(wo_s, sems, 0, step).wait_recv()
+        ring.shared(lane, step)
         put_o(ring.own_slot(step)).start()
         put_o(ring.other_slot(step)).start()
         return carry
     lax.fori_loop(0, ring.chips, collect, 0)
-    ring.finish(wo_s, sems, 0)
+    ring.finish(lane)
+    each_peer(lambda hop: o_copy(hop).wait_send())
 
     def drain(slot, carry):
         put_o(slot).wait()
         return carry
     lax.fori_loop(0, devices, drain, 0)
     put_rows.wait()
+    put_own.wait()
 
 
 def weight_kernel(devices, dwqkv_ref, rows_ref, o_ref, n_ref, dy_ref, hid_ref, dg_ref, du_ref, wq_ref, wk_ref, wv_ref, wo_ref,
@@ -468,7 +518,7 @@
                   load_sem, tile_sem, ring_send, ring_recv, pair_send, pair_recv, out_sem, kv_sem,
                   put_sem, swap_send, swap_recv, rows_send, rows_recv, small_send, small_recv):
     ring = Ring(devices)
-    sems = (ring_send, ring_recv, pair_send, pair_recv)
+    lane = (wqkv_s, (ring_send, ring_recv, pair_send, pair_recv), 4)
     model_dim = n_ref.shape[1]
     local_len, head_dim = o_ref.shape[1:]
     half = hid_ref.shape[1]
@@ -570,7 +620,7 @@
         small_s[ring.me] = jnp.concatenate(parts + [pad], axis=0)
 
     def step_body(step, carry):
-        ring.take(wqkv_s, sems, 0, step)
+        ring.take(lane, step, (0, 1))
 
         @pl.when(step == 0)
         def _():
@@ -602,6 +652,11 @@
                 st_u[step, rows, :] = jnp.dot(nt_s[rows, :], du_s[step % 2], preferred_element_type=F32).astype(BF16)
                 return inner
             lax.fori_loop(0, 4, in_weights, 0)
+
+        ring.take(lane, step, (2, 3))
+
+        @pl.when(step < tiles)
+        def _():
             st_d[step] = transposed_times(hid_s[step % 2], dy_s[...]).astype(BF16)
 
         @pl.when(step == 1)
@@ -617,7 +672,7 @@
         def _():
             finish_backward()
 
-        ring.shared(wqkv_s, sems, 0, step).wait_recv()
+        ring.shared(lane, step)
         for slot in (ring.own_slot(step), ring.other_slot(step)):
             put_q(slot).start()
 
@@ -638,7 +693,7 @@
 
     lax.fori_loop(0, ring.chips, step_body, 0)
     each_peer(lambda hop: small_copy(hop).start())
-    ring.finish(wqkv_s, sems, 0)
+    ring.finish(lane)
 
     def drain(slot, carry):
         put_q(slot).wait()
@@ -705,21 +760,23 @@
         acts = (group_devices, local_len, half)
         blocks = (group_devices, local_len, model_dim)
         pos_rows = jnp.broadcast_to(positions.reshape(1, local_len), (8, local_len))
-        n_all, dy_all, pos_all, hid, d_gate, d_up, mlp_out, d_norm_mlp = pl.pallas_call(
+        freq, sign = rope_lanes(head_dim)
+        rope = struct((group_devices, local_len, head_dim), F32)
+        n_all, dy_all, cos_t, sin_t, hid, d_gate, d_up, mlp_out, d_norm_mlp = pl.pallas_call(
             functools.partial(gather_kernel, group_devices), name="gather_tokens",
-            out_shape=[struct(blocks, BF16), struct(blocks, BF16), struct((group_devices, 8, local_len), jnp.int32)]
+            out_shape=[struct(blocks, BF16), struct(blocks, BF16), rope, rope]
             + [struct(acts, BF16)] * 3 + [struct((local_len, model_dim), BF16), struct((local_len, model_dim), F32)],
-            in_specs=[in_vmem] * 2 + [hbm] * 5, out_specs=[hbm] * 6 + [in_vmem] * 2,
+            in_specs=[in_vmem] * 4 + [hbm] * 5, out_specs=[hbm] * 2 + [in_vmem] * 2 + [hbm] * 3 + [in_vmem] * 2,
             scratch_shapes=[vmem(blocks, BF16), vmem(blocks, BF16), vmem((group_devices, 8, local_len), jnp.int32),
                             vmem((model_dim, half), BF16), vmem((model_dim, half), BF16), vmem((half, model_dim), BF16)]
             + [vmem(acts, BF16)] * 3 + [vmem((2 * local_len, half), F32)] * 2 + [vmem((2, local_len, model_dim), F32)] * 3
-            + [dma((3,)), dma((3,))] + ring_sems(3) + [dma((3, group_devices)), dma((3, group_devices)), dma(()), dma(())],
+            + [dma((3,)), dma((3,))] + ring_sems(1) + ring_sems(2) * 2 + [dma((3, group_devices)), dma((3, group_devices)), dma(()), dma(())],
             compiler_params=pltpu.CompilerParams(collective_id=0, has_side_effects=True, vmem_limit_bytes=VMEM_LIMIT),
             cost_estimate=pl.CostEstimate(flops=40_000_000_000, bytes_accessed=40_000_000, transcendentals=0),
-        )(x_rows, gain_row, grad_flat, pos_rows, w_gate, w_up, w_down)
+        )(x_rows, gain_row, freq, sign, grad_flat, pos_rows, w_gate, w_up, w_down)
         n_all, dy_all = n_all.reshape(seq_len, model_dim), dy_all.reshape(seq_len, model_dim)
         hid, d_gate, d_up = (act.reshape(seq_len, half) for act in (hid, d_gate, d_up))
-        cos_t, sin_t = rope_lanes(pos_all[:, 0].reshape(seq_len), head_dim)
+        cos_t, sin_t = cos_t.reshape(seq_len, head_dim), sin_t.reshape(seq_len, head_dim)
 
         vec = jax.ShapeDtypeStruct((1, head_dim), F32)
         rows_bf = jax.ShapeDtypeStruct((seq_len, head_dim), BF16)
@@ -741,14 +798,14 @@
             [rows_bf, rows_f32, rows_f32] + [rows_bf] * 5, [pltpu.VMEM((block, seq_len), F32)],
         )(idx, n_all, w_q, w_k, w_v, qn3, kn3, cos_t, sin_t)
 
-        attn_own = lax.all_to_all(o_h.reshape(group_devices, local_len, head_dim), 'sp', 0, 0, tiled=True)
-        d_rows, dwqkv_h, dw_o, gq, gk = pl.pallas_call(
+        heads = struct((group_devices, local_len, head_dim), BF16)
+        d_rows, dwqkv_h, dw_o, attn_own, gq, gk = pl.pallas_call(
             functools.partial(backward_kernel, group_devices, block), name="attention_bwd",
-            out_shape=[struct((seq_len, 2 * head_dim), BF16), struct((model_dim, 2 * head_dim), BF16), struct(w_o.shape, BF16), vec, vec],
-            in_specs=[hbm] * 3 + [in_vmem] * 12, out_specs=[hbm, in_vmem, hbm, in_vmem, in_vmem],
+            out_shape=[struct((seq_len, 2 * head_dim), BF16), struct((model_dim, 2 * head_dim), BF16), struct(w_o.shape, BF16), heads, vec, vec],
+            in_specs=[hbm] * 3 + [in_vmem] * 12, out_specs=[hbm, in_vmem, hbm, hbm, in_vmem, in_vmem],
             scratch_shapes=[vmem((seq_len, model_dim), BF16)] * 2 + [vmem((head_dim, model_dim), BF16), vmem((group_devices, head_dim, model_dim), BF16)]
             + [vmem((seq_len, head_dim), BF16)] + [vmem((seq_len, head_dim), F32)] * 2 + [vmem((seq_len, head_dim), BF16)] * 2
-            + [vmem((seq_len, 2 * head_dim), BF16), dma((4,))] + ring_sems(1) + [dma((group_devices,)), dma(()), dma(())],
+            + [vmem((seq_len, 2 * head_dim), BF16), vmem(heads.shape, BF16), dma((5,))] + ring_sems(2) + [dma((group_devices,)), dma(()), dma(())] + [dma((group_devices,))] * 2,
             compiler_params=pltpu.CompilerParams(collective_id=2, has_side_effects=True, vmem_limit_bytes=VMEM_LIMIT),
             cost_estimate=pl.CostEstimate(flops=30_000_000_000, bytes_accessed=30_000_000, transcendentals=0),
         )(dy_all, n_all, w_o, o_h, o32, lse, q_rot, k_rot, v_h, q_proj, k_proj, qn3, kn3, cos_t, sin_t)
@@ -769,7 +826,7 @@
             + [vmem((2, seq_len, tile), BF16)] * 3 + [vmem(tile_in, BF16), vmem(tile_in, BF16), vmem((tiles, tile, model_dim), BF16)]
             + [vmem((group_devices, local_len, 2 * head_dim), BF16), vmem(flat, BF16), vmem(flat, BF16), vmem(flat_kv, BF16), vmem(flat_kv, BF16)]
             + [vmem(w.shape, BF16) for w in (w_q, w_k, w_v, w_o)] + [vmem((group_devices, 16, head_dim), F32)]
-            + [dma((8,)), dma((3, 2))] + ring_sems(1) + [dma((group_devices,))] * 2 + [dma((3, tiles))] * 3 + [dma((group_devices,))] * 4,
+            + [dma((8,)), dma((3, 2))] + ring_sems(4) + [dma((group_devices,))] * 2 + [dma((3, tiles))] * 3 + [dma((group_devices,))] * 4,
             compiler_params=pltpu.CompilerParams(collective_id=1, has_side_effects=True, vmem_limit_bytes=VMEM_LIMIT),
             cost_estimate=pl.CostEstimate(flops=60_000_000_000, bytes_accessed=60_000_000, transcendentals=0),
         )(dwqkv_h, d_rows.reshape(group_devices, local_len, 2 * head_dim), attn_own, n_all, dy_all, hid, d_gate, d_up,

time: 279 us -> 253 us (0.907)
  Pallas kernels: 236 us -> 223 us
  other arithmetic: 6.97 us -> 1.12 us
  starting transfers between devices: 5.81 us -> 0 us
    pallas_call x1, Pallas kernels: 96.6 us -> 82.2 us  [layer_step(): pl.pallas_call(functools.partial(weight_kernel, group_devices), name='gat...]
    all_to_all x1 -> x0, starting transfers between devices: 5.81 us -> none  [layer_step(): lax.all_to_all(o_h.reshape(group_devices, local_len, head_dim), 'sp', 0,...]
    mul x1 -> x0, other arithmetic: 5.53 us -> none  [rope_lanes(): return (jnp.cos(angles), jnp.sin(angles) * sign[None, :])]
    unnamed x38 -> x36, local copies, waits for them, and re-layouts: 27.8 us -> 27.1 us
  transfers between devices with their start and end apart: 1 -> 0, of which waited for: 0 -> 0; matrix products, arithmetic and copies ran while one was open for 0% -> 0% of each run, Pallas kernels for 19% -> 0%
where the time goes in v5:
time: 253 us
  Pallas kernels  223 us (88%)
  local copies, waits for them, and re-layouts  28.3 us (11%)
    pallas_call x1, Pallas kernels, layer_step(): pl.pallas_call(functools.partial(weight_kernel, group_devices), name='gat...  82.2 us
    pallas_call x1, Pallas kernels, layer_step(): pl.pallas_call(functools.partial(gather_kernel, group_devices), name='gat...  65.8 us
    pallas_call x1, Pallas kernels, layer_step(): pl.pallas_call(functools.partial(backward_kernel, group_devices, block),...  52.2 us
    unnamed x36, local copies, waits for them, and re-layouts  27.1 us
    pallas_call x1, Pallas kernels, layer_step(): call(functools.partial(forward_kernel, block), 'attention_fwd', 100000000...  22.5 us

profile of v5, /device:TPU:21, one launch (start us, length us, event | category | flops | bytes accessed | tf_op | source)
XLA Modules:
  0.0 252.8 jit_solution(10972815612929343476)
XLA Ops:
  0.7 0.6 pad_add_fusion.idx_ref
  1.2 0.5 compare_select_fusion
  1.8 1.2 broadcast_in_dim.17.pos_ref
  3.0 65.8 %gather_tokens.1 = (bf16[16,128,1024]{2,1,0:T(8,128)(2,1)}, bf16[16,128,1024]{2,1,0:T(8,128)(2,1)}, f32[16,128,128]{2,1,0:T(8,128)}, f32[16,128,128]{2,1,0:T(8,1...) custom-call(bf16[128,1024]{1,0:T(8,128)(2,1)} %bitcast.29, ...), custom_call_target="tpu_custom_call" | custom-call | flops 40000000000 | bytes 40000000 | tf_op jit(solution)/shard_map/gather_tokens/pallas_call | solution.py:765
  68.8 22.5 %attention_fwd.1 = (bf16[2048,128]{1,0:T(8,128)(2,1)}, f32[2048,128]{1,0:T(8,128)}, f32[2048,128]{1,0:T(8,128)}, bf16[2048,128]{1,0:T(8,128)(2,1)}, bf16[2048,12...) custom-call(s32[3]{0:T(128)} %pad_add_fusion.idx_ref, ...), custom_call_target="tpu_custom_call" | custom-call | flops 10000000000 | bytes 12000000 | tf_op jit(solution)/shard_map/attention_fwd/pallas_call | solution.py:795
  91.3 52.2 %attention_bwd.1 = (bf16[2048,256]{1,0:T(8,128)(2,1)}, bf16[1024,256]{1,0:T(8,128)(2,1)}, bf16[2048,1024]{1,0:T(8,128)(2,1)}, bf16[16,128,128]{2,1,0:T(8,128)(2,1)}, f32[1,128]{1,0:T(1,128)}, /*index=5*/f32[1,128]{1,0:T(1,128)}) custom-call(bf16[2048,1024]{1,0:T(8,128)(2,1)} %bitcast.43, bf16[2048,1024]{1,0:T(8,128)(2,1)} %bitcast.41, ...), custom_call_target="tpu_custom_call" | custom-call | flops 30000001024 | bytes 30000000 | tf_op jit(solution)/shard_map/attention_bwd/pallas_call | solution.py:802
  143.5 82.2 %gather_weights.1 = (bf16[1024,2048]{1,0:T(8,128)(2,1)}, bf16[1024,1024]{1,0:T(8,128)(2,1)}, bf16[1024,1024]{1,0:T(8,128)(2,1)}, bf16[1024,3072]{1,0:T(8,128)(2,...) custom-call(bf16[1024,256]{1,0:T(8,128)(2,1)} %get-tuple-element.58., ...), custom_call_target="tpu_custom_call" | custom-call | flops 60000002048 | bytes 60000000 | tf_op jit(solution)/shard_map/gather_weights/pallas_call | solution.py:819
  225.7 1.7 copy.37
  227.4 1.7 copy.38
  229.1 5.1 %copy.39 = bf16[1024,2048]{1,0:T(8,128)(2,1)} copy(bf16[1024,2048]{1,0:T(8,128)(2,1)} %get-tuple-element.96) | data formatting | bytes 8388608
  234.1 0.0 copy-done.2
  234.1 1.3 copy.40
  235.4 1.3 copy.41
  236.8 1.2 copy-done
  238.0 2.1 copy.42
  240.1 0.0 slice-start
  240.1 3.2 %copy.43 = bf16[1024,3072]{1,0:T(8,128)(2,1)} copy(bf16[1024,3072]{1,0:T(8,128)(2,1)S(1)} %bitcast.24) | data formatting | bytes 12582912
  243.3 1.3 slice-done.3
  244.7 2.9 %copy.44 = bf16[1024,3072]{1,0:T(8,128)(2,1)} copy(bf16[1024,3072]{1,0:T(8,128)(2,1)S(1)} %bitcast.22) | data formatting | bytes 12582912
  247.6 0.7 slice-done.1
  248.3 2.7 %copy.45 = bf16[3072,1024]{1,0:T(8,128)(2,1)} copy(bf16[3072,1024]{1,0:T(8,128)(2,1)S(1)} %bitcast.20) | data formatting | bytes 12582912
  251.0 0.6 copy.46
  251.6 0.6 copy.47
  252.2 0.6 copy.48
  (22 shorter events, 0.0 us)
Async XLA Ops:
  229.1 5.1 %copy-start.2 = (bf16[1024,1024]{1,0:T(8,128)(2,1)S(1)}, bf16[1024,1024]{1,0:T(8,128)(2,1)}, u32[]{:S(2)}) copy-start(bf16[1024,1024]{1,0:T(8,128)(2,1)} %get-tuple-element.97) | copy-start | bytes 6291460
  229.1 6.4 %copy-start.1 = (bf16[1024,1024]{1,0:T(8,128)(2,1)S(1)}, bf16[1024,1024]{1,0:T(8,128)(2,1)}, u32[]{:S(2)}) copy-start(bf16[1024,1024]{1,0:T(8,128)(2,1)} %get-tuple-element.98) | copy-start | bytes 6291460
  229.1 11.1 %slice-start.4 = ((s8[6291456]{0:T(1024)(128)(4,1)}), s8[4194304]{0:T(1024)(128)(4,1)S(1)}, s32[]{:S(2)}) async-start(s8[6291456]{0:T(1024)(128)(4,1)} %bitcast.23), calls=%async_computation.4 | async-start | bytes 8388608
  234.1 3.9 %copy-start = (bf16[2048,1024]{1,0:T(8,128)(2,1)S(1)}, bf16[2048,1024]{1,0:T(8,128)(2,1)}, u32[]{:S(2)}) copy-start(bf16[2048,1024]{1,0:T(8,128)(2,1)} %get-tuple-element.99) | copy-start | bytes 12582916
  235.4 4.7 %slice-start.5 = ((s8[6291456]{0:T(1024)(128)(4,1)}), s8[2097152]{0:T(1024)(128)(4,1)S(1)}, s32[]{:S(2)}) async-start(s8[6291456]{0:T(1024)(128)(4,1)} %bitcast.23), calls=%async_computation.5 | async-start | bytes 4194304
  238.0 5.4 %slice-start.2 = ((s8[6291456]{0:T(1024)(128)(4,1)}), s8[4194304]{0:T(1024)(128)(4,1)S(1)}, s32[]{:S(2)}) async-start(s8[6291456]{0:T(1024)(128)(4,1)} %bitcast.21), calls=%async_computation.2 | async-start | bytes 8388608
  240.1 4.6 %slice-start.3 = ((s8[6291456]{0:T(1024)(128)(4,1)}), s8[2097152]{0:T(1024)(128)(4,1)S(1)}, s32[]{:S(2)}) async-start(s8[6291456]{0:T(1024)(128)(4,1)} %bitcast.21), calls=%async_computation.3 | async-start | bytes 4194304
  240.1 7.5 %slice-start = ((s8[6291456]{0:T(1024)(128)(4,1)}), s8[4194304]{0:T(1024)(128)(4,1)S(1)}, s32[]{:S(2)}) async-start(s8[6291456]{0:T(1024)(128)(4,1)} %bitcast.19), calls=%async_computation | async-start | bytes 8388608
  244.7 3.6 %slice-start.1 = ((s8[6291456]{0:T(1024)(128)(4,1)}), s8[2097152]{0:T(1024)(128)(4,1)S(1)}, s32[]{:S(2)}) async-start(s8[6291456]{0:T(1024)(128)(4,1)} %bitcast.19), calls=%async_computation.1 | async-start | bytes 4194304
  248.3 2.7 %copy-start.5 = (f32[8,128]{1,0:T(8,128)S(1)}, f32[8,128]{1,0:T(8,128)}, u32[]{:S(2)}) copy-start(f32[8,128]{1,0:T(8,128)} %get-tuple-element.77) | copy-start | bytes 12292
  248.3 3.3 %copy-start.3 = (f32[16,128]{1,0:T(8,128)S(1)}, f32[16,128]{1,0:T(8,128)}, u32[]{:S(2)}) copy-start(f32[16,128]{1,0:T(8,128)} %get-tuple-element.104) | copy-start | bytes 24580
  248.3 3.9 %copy-start.4 = (f32[8,128]{1,0:T(8,128)S(1)}, f32[8,128]{1,0:T(8,128)}, u32[]{:S(2)}) copy-start(f32[8,128]{1,0:T(8,128)} %get-tuple-element.105) | copy-start | bytes 12292

commit v6 on v5

--- a/solution.py
+++ b/solution.py
@@ -320,6 +320,11 @@
         def _():
             swap.start()
 
+    def settle(lane, i, step):
+        ring.shared(lane, step)
+        put(i, ring.own_slot(step)).start()
+        put(i, ring.other_slot(step)).start()
+
     def step_body(step, carry):
         ring.take(n_lane, step)
         ring.take(p_lane, step)
@@ -331,7 +336,14 @@
 
         @pl.when(step > 0)
         def _():
+            settle(n_lane, 1, step - 1)
             gate_up(step - 1)
+            ring.shared(p_lane, step - 1)
+            tables(step - 1)
+
+        @pl.when(step > 1)
+        def _():
+            put_acts(step - 2)
         ring.take(dy_lane, step)
 
         @pl.when(step == 1)
@@ -340,26 +352,19 @@
 
         @pl.when(step > 0)
         def _():
+            settle(dy_lane, 2, step - 1)
             hidden(step - 1)
-
-        @pl.when(step > 1)
-        def _():
-            put_acts(step - 2)
-            tables(step - 2)
         own_tokens(step)
-        for lane in (p_lane, n_lane, dy_lane):
-            ring.shared(lane, step)
-        for lane in (1, 2):
-            put(lane, ring.own_slot(step)).start()
-            put(lane, ring.other_slot(step)).start()
         return carry
 
     lax.fori_loop(0, ring.chips, step_body, 0)
     last = ring.chips - 1
+    settle(n_lane, 1, last)
     gate_up(last)
     put_acts(last - 1)
-    tables(last - 1)
+    settle(dy_lane, 2, last)
     hidden(last)
+    ring.shared(p_lane, last)
     tables(last)
     own_tokens(last + 1)
     put_acts(last)
@@ -384,7 +389,7 @@
                     dy_s, n_s, w_s, wo_s, do_s, dk_s, dv_s, send_s, got_s, rows_s, own_s,
                     load_sem, ring_send, ring_recv, pair_send, pair_recv, out_sem, swap_send, swap_recv, o_send, o_recv):
     ring = Ring(devices)
-    lane = (wo_s, (ring_send, ring_recv, pair_send, pair_recv), 2)
+    lane = (wo_s, (ring_send, ring_recv, pair_send, pair_recv), 4)
     seq_len, head_dim = do_s.shape
     steps = seq_len // block
     scale = head_dim ** -0.5
@@ -445,7 +450,7 @@
             dk_s[keys, :] += transposed_times(d_score, q_rows)
             dq = dq + jnp.dot(d_score, k_rows, preferred_element_type=F32)
             done += 1
-            if done in (3, 5, 8, 10):
+            if done % 2 == 0:
                 ring.take(lane, passed)
                 passed += 1
         dq_proj, d_weight = head_backward(dq.astype(BF16).astype(F32), qproj_ref[rows, :].astype(F32), q_weight,
@@ -619,6 +624,19 @@
         pad = jnp.zeros((small_s.shape[1] - len(parts), head_dim), F32)
         small_s[ring.me] = jnp.concatenate(parts + [pad], axis=0)
 
+    def settle(step):
+        ring.shared(lane, step)
+        for slot in (ring.own_slot(step), ring.other_slot(step)):
+            put_q(slot).start()
+
+            @pl.when(slot % 2 == 0)
+            def _():
+                put_kv(slot, k_out).start()
+
+            @pl.when(slot % 2 == 1)
+            def _():
+                put_kv(slot, v_out).start()
+
     def step_body(step, carry):
         ring.take(lane, step, (0, 1))
 
@@ -672,17 +690,9 @@
         def _():
             finish_backward()
 
-        ring.shared(lane, step)
-        for slot in (ring.own_slot(step), ring.other_slot(step)):
-            put_q(slot).start()
-
-            @pl.when(slot % 2 == 0)
-            def _():
-                put_kv(slot, k_out).start()
-
-            @pl.when(slot % 2 == 1)
-            def _():
-                put_kv(slot, v_out).start()
+        @pl.when(step > 0)
+        def _():
+            settle(step - 1)
 
         @pl.when(jnp.logical_and(step > 0, step <= tiles))
         def _():
@@ -693,6 +703,7 @@
 
     lax.fori_loop(0, ring.chips, step_body, 0)
     each_peer(lambda hop: small_copy(hop).start())
+    settle(ring.chips - 1)
     ring.finish(lane)
 
     def drain(slot, carry):
@@ -805,7 +816,7 @@
             in_specs=[hbm] * 3 + [in_vmem] * 12, out_specs=[hbm, in_vmem, hbm, hbm, in_vmem, in_vmem],
             scratch_shapes=[vmem((seq_len, model_dim), BF16)] * 2 + [vmem((head_dim, model_dim), BF16), vmem((group_devices, head_dim, model_dim), BF16)]
             + [vmem((seq_len, head_dim), BF16)] + [vmem((seq_len, head_dim), F32)] * 2 + [vmem((seq_len, head_dim), BF16)] * 2
-            + [vmem((seq_len, 2 * head_dim), BF16), vmem(heads.shape, BF16), dma((5,))] + ring_sems(2) + [dma((group_devices,)), dma(()), dma(())] + [dma((group_devices,))] * 2,
+            + [vmem((seq_len, 2 * head_dim), BF16), vmem(heads.shape, BF16), dma((5,))] + ring_sems(4) + [dma((group_devices,)), dma(()), dma(())] + [dma((group_devices,))] * 2,
             compiler_params=pltpu.CompilerParams(collective_id=2, has_side_effects=True, vmem_limit_bytes=VMEM_LIMIT),
             cost_estimate=pl.CostEstimate(flops=30_000_000_000, bytes_accessed=30_000_000, transcendentals=0),
         )(dy_all, n_all, w_o, o_h, o32, lse, q_rot, k_rot, v_h, q_proj, k_proj, qn3, kn3, cos_t, sin_t)

time: 253 us -> 252 us (level)
  no operation moved by 1% of the time
where the time goes in v6:
time: 252 us
  Pallas kernels  222 us (88%)
  local copies, waits for them, and re-layouts  28.3 us (11%)
    pallas_call x1, Pallas kernels, layer_step(): pl.pallas_call(functools.partial(weight_kernel, group_devices), name='gat...  83.9 us
    pallas_call x1, Pallas kernels, layer_step(): pl.pallas_call(functools.partial(gather_kernel, group_devices), name='gat...  63.6 us
    pallas_call x1, Pallas kernels, layer_step(): pl.pallas_call(functools.partial(backward_kernel, group_devices, block),...  51.9 us
    unnamed x36, local copies, waits for them, and re-layouts  27.1 us
    pallas_call x1, Pallas kernels, layer_step(): call(functools.partial(forward_kernel, block), 'attention_fwd', 100000000...  22.5 us

profile of v6, /device:TPU:21, one launch (start us, length us, event | category | flops | bytes accessed | tf_op | source)
XLA Modules:
  0.0 251.9 jit_solution(866377050671891094)
XLA Ops:
  0.7 0.6 pad_add_fusion.idx_ref
  1.2 0.5 compare_select_fusion
  1.8 1.2 broadcast_in_dim.17.pos_ref
  3.0 63.6 %gather_tokens.1 = (bf16[16,128,1024]{2,1,0:T(8,128)(2,1)}, bf16[16,128,1024]{2,1,0:T(8,128)(2,1)}, f32[16,128,128]{2,1,0:T(8,128)}, f32[16,128,128]{2,1,0:T(8,1...) custom-call(bf16[128,1024]{1,0:T(8,128)(2,1)} %bitcast.29, ...), custom_call_target="tpu_custom_call" | custom-call | flops 40000000000 | bytes 40000000 | tf_op jit(solution)/shard_map/gather_tokens/pallas_call | solution.py:776
  66.6 22.5 %attention_fwd.1 = (bf16[2048,128]{1,0:T(8,128)(2,1)}, f32[2048,128]{1,0:T(8,128)}, f32[2048,128]{1,0:T(8,128)}, bf16[2048,128]{1,0:T(8,128)(2,1)}, bf16[2048,12...) custom-call(s32[3]{0:T(128)} %pad_add_fusion.idx_ref, ...), custom_call_target="tpu_custom_call" | custom-call | flops 10000000000 | bytes 12000000 | tf_op jit(solution)/shard_map/attention_fwd/pallas_call | solution.py:806
  89.1 51.9 %attention_bwd.1 = (bf16[2048,256]{1,0:T(8,128)(2,1)}, bf16[1024,256]{1,0:T(8,128)(2,1)}, bf16[2048,1024]{1,0:T(8,128)(2,1)}, bf16[16,128,128]{2,1,0:T(8,128)(2,1)}, f32[1,128]{1,0:T(1,128)}, /*index=5*/f32[1,128]{1,0:T(1,128)}) custom-call(bf16[2048,1024]{1,0:T(8,128)(2,1)} %bitcast.43, bf16[2048,1024]{1,0:T(8,128)(2,1)} %bitcast.41, ...), custom_call_target="tpu_custom_call" | custom-call | flops 30000001024 | bytes 30000000 | tf_op jit(solution)/shard_map/attention_bwd/pallas_call | solution.py:813
  141.0 83.9 %gather_weights.1 = (bf16[1024,2048]{1,0:T(8,128)(2,1)}, bf16[1024,1024]{1,0:T(8,128)(2,1)}, bf16[1024,1024]{1,0:T(8,128)(2,1)}, bf16[1024,3072]{1,0:T(8,128)(2,...) custom-call(bf16[1024,256]{1,0:T(8,128)(2,1)} %get-tuple-element.58., ...), custom_call_target="tpu_custom_call" | custom-call | flops 60000002048 | bytes 60000000 | tf_op jit(solution)/shard_map/gather_weights/pallas_call | solution.py:830
  224.8 1.7 copy.37
  226.5 1.7 copy.38
  228.2 5.1 %copy.39 = bf16[1024,2048]{1,0:T(8,128)(2,1)} copy(bf16[1024,2048]{1,0:T(8,128)(2,1)} %get-tuple-element.96) | data formatting | bytes 8388608
  233.3 1.3 copy.40
  234.6 0.0 copy-done.1
  234.6 1.3 copy.41
  235.9 1.2 copy-done
  237.1 2.1 copy.42
  239.3 0.0 slice-start
  239.3 3.2 %copy.43 = bf16[1024,3072]{1,0:T(8,128)(2,1)} copy(bf16[1024,3072]{1,0:T(8,128)(2,1)S(1)} %bitcast.24) | data formatting | bytes 12582912
  242.5 1.3 slice-done.3
  243.8 2.9 %copy.44 = bf16[1024,3072]{1,0:T(8,128)(2,1)} copy(bf16[1024,3072]{1,0:T(8,128)(2,1)S(1)} %bitcast.22) | data formatting | bytes 12582912
  246.7 0.7 slice-done.1
  247.4 2.7 %copy.45 = bf16[3072,1024]{1,0:T(8,128)(2,1)} copy(bf16[3072,1024]{1,0:T(8,128)(2,1)S(1)} %bitcast.20) | data formatting | bytes 12582912
  250.1 0.6 copy.46
  250.7 0.6 copy.47
  251.3 0.6 copy.48
  (22 shorter events, 0.0 us)
Async XLA Ops:
  228.2 5.1 %copy-start.2 = (bf16[1024,1024]{1,0:T(8,128)(2,1)S(1)}, bf16[1024,1024]{1,0:T(8,128)(2,1)}, u32[]{:S(2)}) copy-start(bf16[1024,1024]{1,0:T(8,128)(2,1)} %get-tuple-element.97) | copy-start | bytes 6291460
  228.2 6.4 %copy-start.1 = (bf16[1024,1024]{1,0:T(8,128)(2,1)S(1)}, bf16[1024,1024]{1,0:T(8,128)(2,1)}, u32[]{:S(2)}) copy-start(bf16[1024,1024]{1,0:T(8,128)(2,1)} %get-tuple-element.98) | copy-start | bytes 6291460
  228.2 11.1 %slice-start.4 = ((s8[6291456]{0:T(1024)(128)(4,1)}), s8[4194304]{0:T(1024)(128)(4,1)S(1)}, s32[]{:S(2)}) async-start(s8[6291456]{0:T(1024)(128)(4,1)} %bitcast.23), calls=%async_computation.4 | async-start | bytes 8388608
  233.3 3.9 %copy-start = (bf16[2048,1024]{1,0:T(8,128)(2,1)S(1)}, bf16[2048,1024]{1,0:T(8,128)(2,1)}, u32[]{:S(2)}) copy-start(bf16[2048,1024]{1,0:T(8,128)(2,1)} %get-tuple-element.99) | copy-start | bytes 12582916
  234.6 4.7 %slice-start.5 = ((s8[6291456]{0:T(1024)(128)(4,1)}), s8[2097152]{0:T(1024)(128)(4,1)S(1)}, s32[]{:S(2)}) async-start(s8[6291456]{0:T(1024)(128)(4,1)} %bitcast.23), calls=%async_computation.5 | async-start | bytes 4194304
  237.1 5.4 %slice-start.2 = ((s8[6291456]{0:T(1024)(128)(4,1)}), s8[4194304]{0:T(1024)(128)(4,1)S(1)}, s32[]{:S(2)}) async-start(s8[6291456]{0:T(1024)(128)(4,1)} %bitcast.21), calls=%async_computation.2 | async-start | bytes 8388608
  239.3 4.6 %slice-start.3 = ((s8[6291456]{0:T(1024)(128)(4,1)}), s8[2097152]{0:T(1024)(128)(4,1)S(1)}, s32[]{:S(2)}) async-start(s8[6291456]{0:T(1024)(128)(4,1)} %bitcast.21), calls=%async_computation.3 | async-start | bytes 4194304
  239.3 7.5 %slice-start = ((s8[6291456]{0:T(1024)(128)(4,1)}), s8[4194304]{0:T(1024)(128)(4,1)S(1)}, s32[]{:S(2)}) async-start(s8[6291456]{0:T(1024)(128)(4,1)} %bitcast.19), calls=%async_computation | async-start | bytes 8388608
  243.8 3.6 %slice-start.1 = ((s8[6291456]{0:T(1024)(128)(4,1)}), s8[2097152]{0:T(1024)(128)(4,1)S(1)}, s32[]{:S(2)}) async-start(s8[6291456]{0:T(1024)(128)(4,1)} %bitcast.19), calls=%async_computation.1 | async-start | bytes 4194304
  247.4 2.7 %copy-start.5 = (f32[8,128]{1,0:T(8,128)S(1)}, f32[8,128]{1,0:T(8,128)}, u32[]{:S(2)}) copy-start(f32[8,128]{1,0:T(8,128)} %get-tuple-element.77) | copy-start | bytes 12292
  247.4 3.3 %copy-start.3 = (f32[16,128]{1,0:T(8,128)S(1)}, f32[16,128]{1,0:T(8,128)}, u32[]{:S(2)}) copy-start(f32[16,128]{1,0:T(8,128)} %get-tuple-element.104) | copy-start | bytes 24580
  247.4 3.9 %copy-start.4 = (f32[8,128]{1,0:T(8,128)S(1)}, f32[8,128]{1,0:T(8,128)}, u32[]{:S(2)}) copy-start(f32[8,128]{1,0:T(8,128)} %get-tuple-element.105) | copy-start | bytes 12292

commit v7 on v6

--- a/solution.py
+++ b/solution.py
@@ -148,11 +148,17 @@
     def device(self, z, core):
         return 2 * lax.rem(z + 2 * self.chips, self.chips) + core
 
-    def own_slot(self, step):
-        return self.device(self.z - self.turn * step, self.core)
-
-    def other_slot(self, step):
-        return self.device(self.z + self.turn * step, 1 - self.core)
+    def way(self, k):
+        return self.turn if k % 2 == 0 else -self.turn
+
+    def own_slot(self, step, k):
+        return self.device(self.z - self.way(k) * step, self.core)
+
+    def other_slot(self, step, k):
+        return self.device(self.z + self.way(k) * step, 1 - self.core)
+
+    def slots(self, step, k):
+        return self.own_slot(step, k), self.other_slot(step, k)
 
     def barrier(self):
         sem = pltpu.get_barrier_semaphore()
@@ -182,26 +188,26 @@
 
     def forward(self, lane, k, step):
         buf, sems, parts = lane
-        piece = self.part(buf, self.own_slot(step), parts, k)
+        piece = self.part(buf, self.own_slot(step, k), parts, k)
         return pltpu.make_async_remote_copy(piece, piece, sems[0].at[k, step], sems[1].at[k, step + 1],
-                                            device_id={'sp': self.after}, device_id_type=MESH)
+                                            device_id={'sp': self.device(self.z + self.way(k), self.core)}, device_id_type=MESH)
 
     def share(self, lane, k, step):
         buf, sems, parts = lane
-        piece = self.part(buf, self.own_slot(step), parts, k)
+        piece = self.part(buf, self.own_slot(step, k), parts, k)
         return pltpu.make_async_remote_copy(piece, piece, sems[2].at[k, step], sems[3].at[k, step],
                                             device_id={'sp': self.partner}, device_id_type=MESH)
 
     def arrived(self, lane, k, step):
         buf, sems, parts = lane
-        piece = self.part(buf, self.own_slot(step), parts, k)
+        piece = self.part(buf, self.own_slot(step, k), parts, k)
         return pltpu.make_async_remote_copy(piece, piece, sems[0].at[k, step], sems[1].at[k, step],
                                             device_id={'sp': self.before}, device_id_type=MESH)
 
     def shared(self, lane, step):
         buf, sems, parts = lane
         for k in range(parts):
-            piece = self.part(buf, self.other_slot(step), parts, k)
+            piece = self.part(buf, self.other_slot(step, k), parts, k)
             pltpu.make_async_remote_copy(piece, piece, sems[2].at[k, step], sems[3].at[k, step],
                                          device_id={'sp': self.partner}, device_id_type=MESH).wait_recv()
 
@@ -251,30 +257,35 @@
     tile = 512
     acts = ((hid_s, hid_out), (dg_s, dg_out), (du_s, du_out))
 
-    def put(lane, slot):
+    halves = 2
+    piece = n_s.shape[1] // halves
+
+    def span(h):
+        return pl.ds(h * piece, piece)
+
+    def pieces(step):
+        return [(slot, h) for h in range(halves) for slot in ring.slots(step, h)]
+
+    def put(lane, slot, h):
         buf, _, out = lanes[lane]
-        return pltpu.make_async_copy(buf.at[slot], out.at[slot], out_sem.at[lane, slot])
-
-    def put_act(i, slot):
-        return pltpu.make_async_copy(acts[i][0].at[slot], acts[i][1].at[slot], act_sem.at[i, slot])
+        return pltpu.make_async_copy(buf.at[slot, span(h)], out.at[slot, span(h)], out_sem.at[lane, h, slot])
+
+    def put_act(i, slot, h):
+        return pltpu.make_async_copy(acts[i][0].at[slot, span(h)], acts[i][1].at[slot, span(h)], act_sem.at[i, h, slot])
 
     def gate_up(step):
-        mine, other = ring.own_slot(step), ring.other_slot(step)
-
         def body(j, inner):
             cols = pl.ds(pl.multiple_of(j * tile, tile), tile)
-            n_rows = jnp.concatenate([n_s[mine], n_s[other]], axis=0)
+            n_rows = jnp.concatenate([n_s[slot, span(h)] for slot, h in pieces(step)], axis=0)
             gate_s[:, cols] = jnp.dot(n_rows, wg_s[:, cols], preferred_element_type=F32)
             up_s[:, cols] = jnp.dot(n_rows, wu_s[:, cols], preferred_element_type=F32)
             return inner
         lax.fori_loop(0, half // tile, body, 0)
 
     def hidden(step):
-        mine, other = ring.own_slot(step), ring.other_slot(step)
-
         def body(j, inner):
             cols = pl.ds(pl.multiple_of(j * tile, tile), tile)
-            dy_rows = jnp.concatenate([dy_s[mine], dy_s[other]], axis=0)
+            dy_rows = jnp.concatenate([dy_s[slot, span(h)] for slot, h in pieces(step)], axis=0)
             d_hidden = times_transposed(dy_rows, wd_s[cols, :]).astype(BF16).astype(F32)
             gate, up = gate_s[:, cols], up_s[:, cols]
             sig = jax.nn.sigmoid(gate)
@@ -282,23 +293,22 @@
             hid = (silu * up).astype(BF16)
             d_up = (d_hidden * silu).astype(BF16)
             d_gate = (d_hidden * up * (sig * (1.0 + gate * (1.0 - sig)))).astype(BF16)
-            rows = hid.shape[0] // 2
             for buf, value in ((hid_s, hid), (dg_s, d_gate), (du_s, d_up)):
-                buf[mine, :, cols] = value[:rows]
-                buf[other, :, cols] = value[rows:]
+                for i, (slot, h) in enumerate(pieces(step)):
+                    buf[slot, span(h), cols] = value[i * piece:(i + 1) * piece]
             return inner
         lax.fori_loop(0, half // tile, body, 0)
 
     def tables(step):
-        for slot in (ring.own_slot(step), ring.other_slot(step)):
+        for slot in ring.slots(step, 0):
             angles = pos_s[slot].astype(F32).T[:, :1] * freq_ref[...]
             cos_out[slot] = jnp.cos(angles)
             sin_out[slot] = jnp.sin(angles) * sign_ref[...]
 
     def put_acts(step):
         for i in range(3):
-            put_act(i, ring.own_slot(step)).start()
-            put_act(i, ring.other_slot(step)).start()
+            for slot, h in pieces(step):
+                put_act(i, slot, h).start()
 
     swap = pltpu.make_async_remote_copy(part_s, got_s, swap_send, swap_recv, device_id={'sp': ring.partner}, device_id_type=MESH)
 
@@ -322,8 +332,8 @@
 
     def settle(lane, i, step):
         ring.shared(lane, step)
-        put(i, ring.own_slot(step)).start()
-        put(i, ring.other_slot(step)).start()
+        for slot, h in pieces(step):
+            put(i, slot, h).start()
 
     def step_body(step, carry):
         ring.take(n_lane, step)
@@ -372,10 +382,11 @@
         ring.finish(lane)
 
     def drain(slot, carry):
-        for lane in (1, 2):
-            put(lane, slot).wait()
-        for i in range(3):
-            put_act(i, slot).wait()
+        for h in range(halves):
+            for lane in (1, 2):
+                put(lane, slot, h).wait()
+            for i in range(3):
+                put_act(i, slot, h).wait()
         return carry
     lax.fori_loop(0, devices, drain, 0)
     swap.wait()
@@ -495,21 +506,24 @@
     put_own = pltpu.make_async_copy(own_s, own_out, load_sem.at[4])
     put_own.start()
 
-    def put_o(slot):
-        rows = pl.ds(pl.multiple_of(slot * head_dim, head_dim), head_dim)
-        return pltpu.make_async_copy(wo_s.at[slot], wo_out.at[rows, :], out_sem.at[slot])
+    def put_o(slot, k):
+        width = head_dim // lane[2]
+        rows = pl.ds(pl.multiple_of(slot * head_dim + k * width, width), width)
+        return pltpu.make_async_copy(wo_s.at[slot, pl.ds(k * width, width)], wo_out.at[rows, :], out_sem.at[k, slot])
 
     def collect(step, carry):
         ring.shared(lane, step)
-        put_o(ring.own_slot(step)).start()
-        put_o(ring.other_slot(step)).start()
+        for k in range(lane[2]):
+            for slot in ring.slots(step, k):
+                put_o(slot, k).start()
         return carry
     lax.fori_loop(0, ring.chips, collect, 0)
     ring.finish(lane)
     each_peer(lambda hop: o_copy(hop).wait_send())
 
     def drain(slot, carry):
-        put_o(slot).wait()
+        for k in range(lane[2]):
+            put_o(slot, k).wait()
         return carry
     lax.fori_loop(0, devices, drain, 0)
     put_rows.wait()
@@ -570,13 +584,16 @@
             return carry
         lax.fori_loop(1, devices, step, 0)
 
-    def put_q(slot):
+    def part_rows(k):
+        return pl.ds(k * (model_dim // lane[2]), model_dim // lane[2])
+
+    def put_q(slot, k):
         cols = pl.ds(pl.multiple_of(slot * head_dim, head_dim), head_dim)
-        return pltpu.make_async_copy(wqkv_s.at[slot, :, pl.ds(0, head_dim)], q_out.at[:, cols], out_sem.at[slot])
-
-    def put_kv(slot, out):
+        return pltpu.make_async_copy(wqkv_s.at[slot, part_rows(k), pl.ds(0, head_dim)], q_out.at[part_rows(k), cols], out_sem.at[k, slot])
+
+    def put_kv(slot, k, out):
         cols = pl.ds(pl.multiple_of(slot // share * head_dim, head_dim), head_dim)
-        return pltpu.make_async_copy(wqkv_s.at[slot, :, pl.ds(head_dim, head_dim)], out.at[:, cols], kv_sem.at[slot])
+        return pltpu.make_async_copy(wqkv_s.at[slot, part_rows(k), pl.ds(head_dim, head_dim)], out.at[part_rows(k), cols], kv_sem.at[k, slot])
 
     def store(t, i, core):
         st, out = ((st_g, g_out), (st_u, u_out), (st_d, d_out))[i]
@@ -626,16 +643,17 @@
 
     def settle(step):
         ring.shared(lane, step)
-        for slot in (ring.own_slot(step), ring.other_slot(step)):
-            put_q(slot).start()
-
-            @pl.when(slot % 2 == 0)
-            def _():
-                put_kv(slot, k_out).start()
-
-            @pl.when(slot % 2 == 1)
-            def _():
-                put_kv(slot, v_out).start()
+        for k in range(lane[2]):
+            for slot in ring.slots(step, k):
+                put_q(slot, k).start()
+
+                @pl.when(slot % 2 == 0)
+                def _():
+                    put_kv(slot, k, k_out).start()
+
+                @pl.when(slot % 2 == 1)
+                def _():
+                    put_kv(slot, k, v_out).start()
 
     def step_body(step, carry):
         ring.take(lane, step, (0, 1))
@@ -707,8 +725,9 @@
     ring.finish(lane)
 
     def drain(slot, carry):
-        put_q(slot).wait()
-        put_kv(slot, k_out).wait()
+        for k in range(lane[2]):
+            put_q(slot, k).wait()
+            put_kv(slot, k, k_out).wait()
         return carry
     lax.fori_loop(0, devices, drain, 0)
 
@@ -781,7 +800,7 @@
             scratch_shapes=[vmem(blocks, BF16), vmem(blocks, BF16), vmem((group_devices, 8, local_len), jnp.int32),
                             vmem((model_dim, half), BF16), vmem((model_dim, half), BF16), vmem((half, model_dim), BF16)]
             + [vmem(acts, BF16)] * 3 + [vmem((2 * local_len, half), F32)] * 2 + [vmem((2, local_len, model_dim), F32)] * 3
-            + [dma((3,)), dma((3,))] + ring_sems(1) + ring_sems(2) * 2 + [dma((3, group_devices)), dma((3, group_devices)), dma(()), dma(())],
+            + [dma((3,)), dma((3,))] + ring_sems(1) + ring_sems(2) * 2 + [dma((3, 2, group_devices)), dma((3, 2, group_devices)), dma(()), dma(())],
             compiler_params=pltpu.CompilerParams(collective_id=0, has_side_effects=True, vmem_limit_bytes=VMEM_LIMIT),
             cost_estimate=pl.CostEstimate(flops=40_000_000_000, bytes_accessed=40_000_000, transcendentals=0),
         )(x_rows, gain_row, freq, sign, grad_flat, pos_rows, w_gate, w_up, w_down)
@@ -816,7 +835,7 @@
             in_specs=[hbm] * 3 + [in_vmem] * 12, out_specs=[hbm, in_vmem, hbm, hbm, in_vmem, in_vmem],
             scratch_shapes=[vmem((seq_len, model_dim), BF16)] * 2 + [vmem((head_dim, model_dim), BF16), vmem((group_devices, head_dim, model_dim), BF16)]
             + [vmem((seq_len, head_dim), BF16)] + [vmem((seq_len, head_dim), F32)] * 2 + [vmem((seq_len, head_dim), BF16)] * 2
-            + [vmem((seq_len, 2 * head_dim), BF16), vmem(heads.shape, BF16), dma((5,))] + ring_sems(4) + [dma((group_devices,)), dma(()), dma(())] + [dma((group_devices,))] * 2,
+            + [vmem((seq_len, 2 * head_dim), BF16), vmem(heads.shape, BF16), dma((5,))] + ring_sems(4) + [dma((4, group_devices)), dma(()), dma(())] + [dma((group_devices,))] * 2,
             compiler_params=pltpu.CompilerParams(collective_id=2, has_side_effects=True, vmem_limit_bytes=VMEM_LIMIT),
             cost_estimate=pl.CostEstimate(flops=30_000_000_000, bytes_accessed=30_000_000, transcendentals=0),
         )(dy_all, n_all, w_o, o_h, o32, lse, q_rot, k_rot, v_h, q_proj, k_proj, qn3, kn3, cos_t, sin_t)
@@ -837,7 +856,7 @@
             + [vmem((2, seq_len, tile), BF16)] * 3 + [vmem(tile_in, BF16), vmem(tile_in, BF16), vmem((tiles, tile, model_dim), BF16)]
             + [vmem((group_devices, local_len, 2 * head_dim), BF16), vmem(flat, BF16), vmem(flat, BF16), vmem(flat_kv, BF16), vmem(flat_kv, BF16)]
             + [vmem(w.shape, BF16) for w in (w_q, w_k, w_v, w_o)] + [vmem((group_devices, 16, head_dim), F32)]
-            + [dma((8,)), dma((3, 2))] + ring_sems(4) + [dma((group_devices,))] * 2 + [dma((3, tiles))] * 3 + [dma((group_devices,))] * 4,
+            + [dma((8,)), dma((3, 2))] + ring_sems(4) + [dma((4, group_devices))] * 2 + [dma((3, tiles))] * 3 + [dma((group_devices,))] * 4,
             compiler_params=pltpu.CompilerParams(collective_id=1, has_side_effects=True, vmem_limit_bytes=VMEM_LIMIT),
             cost_estimate=pl.CostEstimate(flops=60_000_000_000, bytes_accessed=60_000_000, transcendentals=0),
         )(dwqkv_h, d_rows.reshape(group_devices, local_len, 2 * head_dim), attn_own, n_all, dy_all, hid, d_gate, d_up,

time: 252 us -> 257 us (1.020)
  Pallas kernels: 222 us -> 227 us
    pallas_call x1, Pallas kernels: 63.6 us -> 66.4 us  [layer_step(): pl.pallas_call(functools.partial(gather_kernel, group_devices), name='gat...]
where the time goes in v7:
time: 257 us
  Pallas kernels  227 us (88%)
  local copies, waits for them, and re-layouts  28.3 us (11%)
    pallas_call x1, Pallas kernels, layer_step(): pl.pallas_call(functools.partial(weight_kernel, group_devices), name='gat...  85.4 us
    pallas_call x1, Pallas kernels, layer_step(): pl.pallas_call(functools.partial(gather_kernel, group_devices), name='gat...  66.4 us
    pallas_call x1, Pallas kernels, layer_step(): pl.pallas_call(functools.partial(backward_kernel, group_devices, block),...  52.4 us
    unnamed x36, local copies, waits for them, and re-layouts  27.1 us
    pallas_call x1, Pallas kernels, layer_step(): call(functools.partial(forward_kernel, block), 'attention_fwd', 100000000...  22.5 us

profile of v7, /device:TPU:21, one launch (start us, length us, event | category | flops | bytes accessed | tf_op | source)
XLA Modules:
  0.0 256.8 jit_solution(4721268194551455745)
XLA Ops:
  0.7 0.6 pad_add_fusion.idx_ref
  1.2 0.5 compare_select_fusion
  1.8 1.2 broadcast_in_dim.17.pos_ref
  3.0 66.4 %gather_tokens.1 = (bf16[16,128,1024]{2,1,0:T(8,128)(2,1)}, bf16[16,128,1024]{2,1,0:T(8,128)(2,1)}, f32[16,128,128]{2,1,0:T(8,128)}, f32[16,128,128]{2,1,0:T(8,1...) custom-call(bf16[128,1024]{1,0:T(8,128)(2,1)} %bitcast.29, ...), custom_call_target="tpu_custom_call" | custom-call | flops 40000000000 | bytes 40000000 | tf_op jit(solution)/shard_map/gather_tokens/pallas_call | solution.py:795
  69.4 22.5 %attention_fwd.1 = (bf16[2048,128]{1,0:T(8,128)(2,1)}, f32[2048,128]{1,0:T(8,128)}, f32[2048,128]{1,0:T(8,128)}, bf16[2048,128]{1,0:T(8,128)(2,1)}, bf16[2048,12...) custom-call(s32[3]{0:T(128)} %pad_add_fusion.idx_ref, ...), custom_call_target="tpu_custom_call" | custom-call | flops 10000000000 | bytes 12000000 | tf_op jit(solution)/shard_map/attention_fwd/pallas_call | solution.py:825
  91.9 52.4 %attention_bwd.1 = (bf16[2048,256]{1,0:T(8,128)(2,1)}, bf16[1024,256]{1,0:T(8,128)(2,1)}, bf16[2048,1024]{1,0:T(8,128)(2,1)}, bf16[16,128,128]{2,1,0:T(8,128)(2,1)}, f32[1,128]{1,0:T(1,128)}, /*index=5*/f32[1,128]{1,0:T(1,128)}) custom-call(bf16[2048,1024]{1,0:T(8,128)(2,1)} %bitcast.43, bf16[2048,1024]{1,0:T(8,128)(2,1)} %bitcast.41, ...), custom_call_target="tpu_custom_call" | custom-call | flops 30000001024 | bytes 30000000 | tf_op jit(solution)/shard_map/attention_bwd/pallas_call | solution.py:832
  144.3 85.4 %gather_weights.1 = (bf16[1024,2048]{1,0:T(8,128)(2,1)}, bf16[1024,1024]{1,0:T(8,128)(2,1)}, bf16[1024,1024]{1,0:T(8,128)(2,1)}, bf16[1024,3072]{1,0:T(8,128)(2,...) custom-call(bf16[1024,256]{1,0:T(8,128)(2,1)} %get-tuple-element.58., ...), custom_call_target="tpu_custom_call" | custom-call | flops 60000002048 | bytes 60000000 | tf_op jit(solution)/shard_map/gather_weights/pallas_call | solution.py:849
  229.7 1.7 copy.37
  231.4 1.7 copy.38
  233.0 5.1 %copy.39 = bf16[1024,2048]{1,0:T(8,128)(2,1)} copy(bf16[1024,2048]{1,0:T(8,128)(2,1)} %get-tuple-element.96) | data formatting | bytes 8388608
  238.1 1.3 copy.40
  239.4 1.3 copy.41
  240.7 1.2 copy-done
  242.0 2.1 copy.42
  244.1 0.0 slice-start
  244.1 3.2 %copy.43 = bf16[1024,3072]{1,0:T(8,128)(2,1)} copy(bf16[1024,3072]{1,0:T(8,128)(2,1)S(1)} %bitcast.24) | data formatting | bytes 12582912
  247.3 1.3 slice-done.3
  248.7 2.9 %copy.44 = bf16[1024,3072]{1,0:T(8,128)(2,1)} copy(bf16[1024,3072]{1,0:T(8,128)(2,1)S(1)} %bitcast.22) | data formatting | bytes 12582912
  251.6 0.0 slice-done
  251.6 0.7 slice-done.1
  252.3 2.7 %copy.45 = bf16[3072,1024]{1,0:T(8,128)(2,1)} copy(bf16[3072,1024]{1,0:T(8,128)(2,1)S(1)} %bitcast.20) | data formatting | bytes 12582912
  255.0 0.6 copy.46
  255.6 0.6 copy.47
  256.2 0.6 copy.48
  (22 shorter events, 0.0 us)
Async XLA Ops:
  233.0 5.1 %copy-start.2 = (bf16[1024,1024]{1,0:T(8,128)(2,1)S(1)}, bf16[1024,1024]{1,0:T(8,128)(2,1)}, u32[]{:S(2)}) copy-start(bf16[1024,1024]{1,0:T(8,128)(2,1)} %get-tuple-element.97) | copy-start | bytes 6291460
  233.0 6.4 %copy-start.1 = (bf16[1024,1024]{1,0:T(8,128)(2,1)S(1)}, bf16[1024,1024]{1,0:T(8,128)(2,1)}, u32[]{:S(2)}) copy-start(bf16[1024,1024]{1,0:T(8,128)(2,1)} %get-tuple-element.98) | copy-start | bytes 6291460
  233.0 11.1 %slice-start.4 = ((s8[6291456]{0:T(1024)(128)(4,1)}), s8[4194304]{0:T(1024)(128)(4,1)S(1)}, s32[]{:S(2)}) async-start(s8[6291456]{0:T(1024)(128)(4,1)} %bitcast.23), calls=%async_computation.4 | async-start | bytes 8388608
  238.1 3.9 %copy-start = (bf16[2048,1024]{1,0:T(8,128)(2,1)S(1)}, bf16[2048,1024]{1,0:T(8,128)(2,1)}, u32[]{:S(2)}) copy-start(bf16[2048,1024]{1,0:T(8,128)(2,1)} %get-tuple-element.99) | copy-start | bytes 12582916
  239.4 4.7 %slice-start.5 = ((s8[6291456]{0:T(1024)(128)(4,1)}), s8[2097152]{0:T(1024)(128)(4,1)S(1)}, s32[]{:S(2)}) async-start(s8[6291456]{0:T(1024)(128)(4,1)} %bitcast.23), calls=%async_computation.5 | async-start | bytes 4194304
  242.0 5.4 %slice-start.2 = ((s8[6291456]{0:T(1024)(128)(4,1)}), s8[4194304]{0:T(1024)(128)(4,1)S(1)}, s32[]{:S(2)}) async-start(s8[6291456]{0:T(1024)(128)(4,1)} %bitcast.21), calls=%async_computation.2 | async-start | bytes 8388608
  244.1 4.6 %slice-start.3 = ((s8[6291456]{0:T(1024)(128)(4,1)}), s8[2097152]{0:T(1024)(128)(4,1)S(1)}, s32[]{:S(2)}) async-start(s8[6291456]{0:T(1024)(128)(4,1)} %bitcast.21), calls=%async_computation.3 | async-start | bytes 4194304
  244.1 7.5 %slice-start = ((s8[6291456]{0:T(1024)(128)(4,1)}), s8[4194304]{0:T(1024)(128)(4,1)S(1)}, s32[]{:S(2)}) async-start(s8[6291456]{0:T(1024)(128)(4,1)} %bitcast.19), calls=%async_computation | async-start | bytes 8388608
  248.7 3.6 %slice-start.1 = ((s8[6291456]{0:T(1024)(128)(4,1)}), s8[2097152]{0:T(1024)(128)(4,1)S(1)}, s32[]{:S(2)}) async-start(s8[6291456]{0:T(1024)(128)(4,1)} %bitcast.19), calls=%async_computation.1 | async-start | bytes 4194304
  252.3 2.7 %copy-start.5 = (f32[8,128]{1,0:T(8,128)S(1)}, f32[8,128]{1,0:T(8,128)}, u32[]{:S(2)}) copy-start(f32[8,128]{1,0:T(8,128)} %get-tuple-element.77) | copy-start | bytes 12292
  252.3 3.3 %copy-start.3 = (f32[16,128]{1,0:T(8,128)S(1)}, f32[16,128]{1,0:T(8,128)}, u32[]{:S(2)}) copy-start(f32[16,128]{1,0:T(8,128)} %get-tuple-element.104) | copy-start | bytes 24580
  252.3 3.9 %copy-start.4 = (f32[8,128]{1,0:T(8,128)S(1)}, f32[8,128]{1,0:T(8,128)}, u32[]{:S(2)}) copy-start(f32[8,128]{1,0:T(8,128)} %get-tuple-element.105) | copy-start | bytes 12292
